TPU v7x, 128 devices: a whole 4x4x4 slice. The times are simulated.
128 devices in a mesh: chain: 8 (over x, core), quad: 16 (over z, y).
Axes of the slice: x: 4, y: 4, z: 4, core: 2. Of those that a mesh axis runs over, the one named last changes fastest.
Arguments:
- sections: bfloat16 [8, 4096, 4096], P('chain', 'quad'), may hold values from -8 to 8
- anchor: bfloat16 [4096, 4096], P('quad'), may hold values from -8 to 8
Outputs:
- registered: bfloat16 [8, 4096, 4096], P('chain', 'quad')
- accumulated: float32 [8, 64, 128], P('chain')
All inputs are finite; a program needn't handle non-finite values.
Results may differ from a plain program's by a relative error of at most 0.00135.
The roundings to bfloat16 on the way count: a program that leaves them out, or rounds other values in their place, can miss the bound.
Values may be sent and summed in bfloat16 or wider, within the bound.
No kernel may reach another device: no remote copies, remote signals or barrier semaphores. Data moves between devices by JAX's collectives and lax.ppermute only.
A program may use at most 128 MiB of HBM per device.

v0:
```python
import jax
import jax.numpy as jnp
import numpy as np
from jax import lax
from jax.experimental import pallas as pl
from jax.experimental.pallas import tpu as pltpu
from jax.sharding import PartitionSpec as P

GRID = 64
SPACING = 64
ROWS = 256
COLS = 4096
BLOCK = 1024
STEPS = COLS // BLOCK
CHUNK = 32
EXT = 72
PIXELS = 4096.0 * 4096.0
EPS = 1e-6
RATE = 0.25
SMOOTH = 0.25
BF = jnp.bfloat16
F32 = jnp.float32


def weight(offset, xp):
    d = xp.abs(offset)
    near = 2.0 / 3.0 - d * d + 0.5 * d * d * d
    r = 2.0 - d
    far = r * r * r / 6.0
    return xp.where(d < 1.0, near, xp.where(d < 2.0, far, 0.0 * d))


def local_rows():
    r = np.arange(ROWS, dtype=np.float32)
    j = np.arange(8, dtype=np.float32) - 2.0
    off = (r[:, None] + np.float32(0.5)) / np.float32(SPACING) - j[None, :] - np.float32(0.5)
    return weight(off.astype(np.float32), np).astype(np.float32)


def hi_lo(a):
    hi = a.astype(BF)
    return hi, (a - hi.astype(F32)).astype(BF)


def split3(a):
    hi = a.astype(BF)
    rest = a - hi.astype(F32)
    mid = rest.astype(BF)
    lo = (rest - mid.astype(F32)).astype(BF)
    return jnp.concatenate([hi.astype(F32), mid.astype(F32), lo.astype(F32)], axis=0).astype(BF)


def sum3(a, n):
    return a[0:n] + a[n : 2 * n] + a[2 * n : 3 * n]


def two(a):
    hi = a.astype(np.dtype(BF)).astype(np.float32)
    return np.concatenate([hi, a - hi], 0)


def host_tables():
    r8 = local_rows()
    pairs = np.zeros((32, ROWS), np.float32)
    c8 = r8.astype(np.dtype(BF)).astype(np.float32)
    lanes = np.zeros((BLOCK, 128), np.float32)
    cols = np.zeros((BLOCK, 128), np.float32)
    place = np.zeros((STEPS * 128, 256), np.float32)
    put = np.zeros((STEPS * 128, 128), np.float32)
    for s in range(4):
        cols[256 * s : 256 * s + 256, 8 * s : 8 * s + 8] = c8
    for d in range(4):
        for e in range(8 - d):
            pairs[d * 8 + e] = r8[:, e] * r8[:, e + d]
            for s in range(4):
                lanes[256 * s : 256 * s + 256, 32 * s + 8 * d + e] = c8[:, e] * c8[:, e + d]
                for t in range(STEPS):
                    i = 16 * t + 4 * s - 2 + e
                    if i >= 0 and i + d < GRID:
                        place[128 * t + 32 * s + 8 * d + e, 64 * d + i] = 1.0
    for t in range(STEPS):
        for s in range(4):
            for e in range(8):
                i = 16 * t + 4 * s - 2 + e
                if 0 <= i < GRID:
                    put[128 * t + 8 * s + e, i] = 1.0
    diff = np.zeros((8, ROWS), np.float32)
    diff[:, 1:] += 0.5 * r8.T[:, :-1]
    diff[:, :-1] -= 0.5 * r8.T[:, 1:]
    lanes_hi = lanes.astype(np.dtype(BF)).astype(np.float32)
    table = np.concatenate([lanes_hi, lanes - lanes_hi, cols], 1)
    plain = np.concatenate([two(r8.T), two(diff), np.ones((16, ROWS), np.float32)], 0)
    edge = np.stack([-0.5 * r8[0], 0.5 * r8[ROWS - 1]], 0).reshape(16, 1) * np.ones((1, 128), np.float32)
    bf = [jnp.asarray(a.astype(np.dtype(BF))) for a in (two(pairs), two(r8.T), plain, table, place, put)]
    return r8, bf, edge


def slope_tables():
    down = 0.5 * (np.eye(ROWS, k=1) - np.eye(ROWS, k=-1))
    across = np.zeros((512, 256), np.float32)
    o = np.arange(256)
    across[o + 129, o] = 0.5
    across[o + 127, o] = -0.5
    return jnp.asarray(down.astype(np.dtype(BF))), jnp.asarray(across.astype(np.dtype(BF)))


def col_table():
    x = jnp.arange(COLS, dtype=jnp.int32).astype(F32)
    j = jnp.arange(GRID, dtype=jnp.int32).astype(F32)
    return weight((x[None, :] + 0.5) / SPACING - j[:, None] - 0.5, jnp).astype(BF)


def dot(a, b):
    return jnp.dot(a, b, preferred_element_type=F32)


def rims(pos_ref, left_ref, right_ref, up_ref, dn_ref, step):
    left = jnp.where(step > 0, left_ref[...].astype(F32), 0.0).astype(BF)
    right = jnp.where(step < STEPS - 1, right_ref[...].astype(F32), 0.0).astype(BF)
    up = jnp.where(pos_ref[1] > 0, up_ref[...].astype(F32), 0.0)
    dn = jnp.where(pos_ref[1] < 15, dn_ref[...].astype(F32), 0.0)
    return left, right, up, dn


def slopes(m_ref, rim, down_ref, across_ref, xs, ys, s):
    left, right, up, dn = rim
    at = pl.ds(256 * s, 256)
    if s == 0:
        wide = jnp.concatenate([left, m_ref[:, 0:384]], axis=1)
    elif s == BLOCK // 256 - 1:
        wide = jnp.concatenate([m_ref[:, BLOCK - 384 : BLOCK], right], axis=1)
    else:
        wide = m_ref[:, 256 * s - 128 : 256 * s + 384]
    xs[:, at] = dot(wide, across_ref[...])
    ys[:, at] = dot(down_ref[...], m_ref[:, at])
    ys[0:1, at] = ys[0:1, at] - 0.5 * up[:, 256 * s : 256 * s + 256]
    ys[ROWS - 1 : ROWS, at] = ys[ROWS - 1 : ROWS, at] + 0.5 * dn[:, 256 * s : 256 * s + 256]


def fold8(a):
    return jnp.sum(a.reshape(CHUNK // 8, 8, a.shape[1]), axis=0)


def lanes_to_row(a):
    s = jnp.sum(a, axis=0, keepdims=True)
    out = s[:, 0:128]
    for t in range(1, s.shape[1] // 128):
        out = out + s[:, 128 * t : 128 * t + 128]
    return out


def rows_of(lin, hi, lo):
    a = dot(lin, hi)
    b = dot(lin, lo)
    return a[0:8] + a[8:16] + b[0:8]


def stage0(pos_ref, m_ref, left_ref, right_ref, up_ref, dn_ref, down_ref, across_ref, pairs_ref, lin_ref, plain_ref, tab_ref, place_ref, put_ref, edge_ref, h_ref, p_ref, xs, ys, fxx, fxy, fyy, mxh, mxl, myh, myl, zacc, lacc, sums):
    step = pl.program_id(0)
    rim = rims(pos_ref, left_ref, right_ref, up_ref, dn_ref, step)
    pairs = pairs_ref[...]
    lin = lin_ref[...]
    sumsq = jnp.zeros((8, 256), F32)
    t_parts, lx, ly = [], [], []
    for s in range(BLOCK // 256):
        at = pl.ds(256 * s, 256)
        slopes(m_ref, rim, down_ref, across_ref, xs, ys, s)
        for c in range(ROWS // CHUNK):
            rows = pl.ds(CHUNK * c, CHUNK)
            m, x, y = m_ref[rows, at].astype(F32), xs[rows, at], ys[rows, at]
            fxx[rows, at] = (x * x).astype(BF)
            fxy[rows, at] = (x * y).astype(BF)
            fyy[rows, at] = (y * y).astype(BF)
            mxh[rows, at], mxl[rows, at] = hi_lo(m * x)
            myh[rows, at], myl[rows, at] = hi_lo(m * y)
            sumsq = sumsq + fold8(m * m)
        trio = []
        for f in (fxx, fxy, fyy):
            t = dot(pairs, f[:, at])
            trio.append(t[0:32] + t[32:64])
        t_parts.append(jnp.concatenate(trio, axis=0))
        lx.append(rows_of(lin, mxh[:, at], mxl[:, at]))
        ly.append(rows_of(lin, myh[:, at], myl[:, at]))
    t_hi, t_lo = hi_lo(jnp.concatenate(t_parts, axis=1))
    z = dot(t_hi, tab_ref[:, 0:256]) + dot(t_lo, tab_ref[:, 0:256])
    zacc[pl.ds(96 * step, 96), :] = z[:, 0:128] + z[:, 128:256]
    ext = jnp.concatenate([rim[0], m_ref[...], rim[1]], axis=1)
    ones = dot(plain_ref[...], ext)
    l1 = ones[0:8] + ones[8:16]
    l1x = 0.5 * (pltpu.roll(l1, BLOCK + 255, 1) - pltpu.roll(l1, 1, 1))[:, 128 : 128 + BLOCK]
    l1y = (ones[16:24] + ones[24:32])[:, 128 : 128 + BLOCK]
    l1y = l1y + edge_ref[0:8, 0:1] * rim[2] + edge_ref[8:16, 0:1] * rim[3]
    rows4 = jnp.concatenate([jnp.concatenate(lx, axis=1), jnp.concatenate(ly, axis=1), l1x, l1y], axis=0)
    lacc[pl.ds(32 * step, 32), :] = sum3(dot(split3(rows4), tab_ref[:, 256:384]), 32)
    both = jnp.concatenate([lanes_to_row(ones[32:33, 128 : 128 + BLOCK]), lanes_to_row(sumsq), jnp.zeros((6, 128), F32)], axis=0)

    @pl.when(step == 0)
    def _():
        sums[...] = both

    @pl.when(step > 0)
    def _():
        sums[...] += both

    @pl.when(step == STEPS - 1)
    def _():
        h = jnp.zeros((288, 256), F32)
        p = jnp.zeros((96, 128), F32)
        for t in range(STEPS):
            h = h + dot(split3(zacc[96 * t : 96 * t + 96, :]), place_ref[128 * t : 128 * t + 128, :])
            p = p + dot(split3(lacc[32 * t : 32 * t + 32, :]), put_ref[128 * t : 128 * t + 128, :])
        h = sum3(h, 96)
        hi, lo = hi_lo(h)
        low = [lo[32 * t : 32 * t + 16, 0:128] for t in range(3)]
        for t in range(16):
            h_ref[t, 0:96, :] = hi
            h_ref[t, 96:112, :] = jnp.concatenate(low[0:2], axis=1)
            h_ref[t, 112:128, :] = jnp.concatenate([low[2], jnp.zeros((16, 128), BF)], axis=1)
        p = sum3(p, 32)
        p_ref[0:8, :] = p[0:8] + pltpu.roll(p[8:16], 64, 1)
        p_ref[8:16, :] = p[16:24] + pltpu.roll(p[24:32], 64, 1)
        p_ref[16:24, :] = sums[...]


def stage1(pos_ref, m_ref, left_ref, right_ref, up_ref, dn_ref, down_ref, across_ref, lin_ref, tab_ref, put_ref, anchor_ref, prior_ref, p_ref, out_ref, xs, ys, fxh, fxl, fyh, fyl, lacc, sums):
    step = pl.program_id(0)
    rim = rims(pos_ref, left_ref, right_ref, up_ref, dn_ref, step)
    lin = lin_ref[...]
    cross = jnp.zeros((8, 256), F32)
    whole_sum = jnp.zeros((8, 256), F32)
    first = pos_ref[0] == 0
    lx, ly = [], []
    for s in range(BLOCK // 256):
        at = pl.ds(256 * s, 256)
        slopes(m_ref, rim, down_ref, across_ref, xs, ys, s)
        for c in range(ROWS // CHUNK):
            rows = pl.ds(CHUNK * c, CHUNK)
            m, x, y = m_ref[rows, at].astype(F32), xs[rows, at], ys[rows, at]
            f = jnp.where(first, anchor_ref[rows, at].astype(F32), prior_ref[rows, at].astype(F32))
            fxh[rows, at], fxl[rows, at] = hi_lo(f * x)
            fyh[rows, at], fyl[rows, at] = hi_lo(f * y)
            cross = cross + fold8(f * m)
            whole_sum = whole_sum + fold8(f)
        lx.append(rows_of(lin, fxh[:, at], fxl[:, at]))
        ly.append(rows_of(lin, fyh[:, at], fyl[:, at]))
    rows2 = jnp.concatenate([jnp.concatenate(lx, axis=1), jnp.concatenate(ly, axis=1)], axis=0)
    lacc[pl.ds(16 * step, 16), :] = sum3(dot(split3(rows2), tab_ref[:, 256:384]), 16)
    both = jnp.concatenate([lanes_to_row(cross), lanes_to_row(whole_sum), jnp.zeros((6, 128), F32)], axis=0)

    @pl.when(step == 0)
    def _():
        sums[...] = both

    @pl.when(step > 0)
    def _():
        sums[...] += both

    @pl.when(step == STEPS - 1)
    def _():
        p = jnp.zeros((48, 128), F32)
        for t in range(STEPS):
            p = p + dot(split3(lacc[16 * t : 16 * t + 16, :]), put_ref[128 * t : 128 * t + 128, :])
        p = sum3(p, 16)
        for t in range(16):
            out_ref[t, 0:8, :] = p[0:8] + pltpu.roll(p[8:16], 64, 1)
            out_ref[t, 8:16, :] = sums[...]
            out_ref[t, 16:40, :] = p_ref[...]


def shifted(a, by, axis):
    n = a.shape[axis]
    by = by % n
    return a if by == 0 else pltpu.roll(a, by, axis)


def stacked(pieces):
    pad = jnp.zeros((8, pieces[0].shape[1]), F32)
    even = jnp.concatenate(pieces[0::2] + [pad], axis=0)
    odd = jnp.concatenate(pieces[1::2] + [pad], axis=0)
    return even + pltpu.roll(odd, 4, 0)


def build_operator(h_ref, a1, a2):
    lane = lax.broadcasted_iota(jnp.int32, (EXT, 128), 1)
    low = lane < 64
    for dj in range(4):
        grid = []
        for comp in range(3):
            r = 4 * comp + dj
            base = 16 * (r // 2)
            off = 8 * (r % 2)
            pieces = []
            for q in range(16):
                piece = h_ref[q, base : base + 16, :].astype(F32)[off : off + 8, :]
                if dj < 2:
                    at = 96 + 16 * (comp // 2)
                    side = 128 * (comp % 2)
                    rest = h_ref[q, at : at + 16, side : side + 128].astype(F32)[8 * dj : 8 * dj + 8, :]
                    piece = jnp.concatenate([piece[:, 0:128] + rest, piece[:, 128:256]], axis=1)
                pieces.append(piece)
            grid.append(stacked(pieces))
        for pair in range(2):
            xx, xy, yy = [g[:, 128 * pair : 128 * pair + 128] for g in grid]
            xx_s, xy_s, yy_s = [pltpu.roll(v, 64, 1) for v in (xx, xy, yy)]
            for odd in range(2):
                di = 2 * pair + odd
                if odd == 0:
                    one = jnp.where(low, xx, yy_s)
                    two = jnp.where(low, xy, xy_s)
                else:
                    one = jnp.where(low, xx_s, yy)
                    two = jnp.where(low, xy_s, xy)
                a1[dj * 7 + 3 + di] = one
                a2[dj * 7 + 3 + di] = two
                if di > 0:
                    a1[dj * 7 + 3 - di] = pltpu.roll(one, di, 1)
                    a2[dj * 7 + 3 - di] = pltpu.roll(two, di, 1)


def apply_operator(a1, a2, c):
    cs = pltpu.roll(c, 64, 1)
    plain = [(shifted(c, -di, 1), shifted(cs, -di, 1)) for di in range(-3, 4)]
    y = jnp.zeros((EXT, 128), F32)
    for dj in range(4):
        ahead = jnp.zeros((EXT, 128), F32)
        back = jnp.zeros((EXT, 128), F32)
        for t in range(7):
            p, s = plain[t]
            u, v = a1[dj * 7 + t], a2[dj * 7 + t]
            ahead = ahead + u * shifted(p, -dj, 0) + v * shifted(s, -dj, 0)
            if dj:
                back = back + u * p + v * s
        y = y + ahead
        if dj:
            y = y + pltpu.roll(back, dj, 0)
    return y


def total(a):
    return jnp.sum(jnp.sum(a, axis=0, keepdims=True), axis=1, keepdims=True)


def fields(p_ref):
    row = lax.broadcasted_iota(jnp.int32, (EXT, 128), 0)
    valid = (row >= 2) & (row < 66)
    out = []
    for at in (0, 16, 24):
        out.append(jnp.where(valid, stacked([p_ref[q, at : at + 8, :] for q in range(16)]), 0.0))
    sums = []
    for at in (8, 9, 32, 33):
        acc = p_ref[0, at : at + 1, :]
        for q in range(1, 16):
            acc = acc + p_ref[q, at : at + 1, :]
        sums.append(jnp.sum(acc, axis=1, keepdims=True))
    return valid, out, sums


def direction(valid, grads, sums, c, hc):
    gf, gm, g1 = grads
    s_fm, s_f, s_m, s_mm = sums
    mean_f = s_f / PIXELS
    if c is None:
        s_w, s_ww, s_fw, gw = s_m, s_mm, s_fm, gm
    else:
        s_w = s_m + total(g1 * c)
        s_ww = s_mm + total(c * (2.0 * gm + hc))
        s_fw = s_fm + total(gf * c)
        gw = gm + hc
    mean_w = s_w / PIXELS
    var = s_ww - PIXELS * mean_w * mean_w
    cross = s_fw - PIXELS * mean_f * mean_w
    den = jnp.sqrt(var + EPS)
    ratio = cross / den / (var + EPS)
    g = PIXELS * ((gf - mean_f * g1) / den - ratio * (gw - mean_w * g1))
    g = jnp.where(valid, g, 0.0)
    return g / jnp.sqrt(total(g * g) / 8192.0 + EPS)


def solve_a(h_ref, p_ref, out_ref, lead_ref, a1, a2):
    build_operator(h_ref, a1, a2)
    valid, grads, sums = fields(p_ref)
    c = RATE * direction(valid, grads, sums, None, None)
    hc = apply_operator(a1, a2, c)
    out_ref[0:EXT, :] = c
    lead_ref[...] = c
    out_ref[EXT : 2 * EXT, :] = direction(valid, grads, sums, c, hc)


def solve_b(pos_ref, h_ref, p_ref, own_ref, prev_ref, next_ref, prev2_ref, next2_ref, out_ref, a1, a2):
    k = pos_ref[0]
    build_operator(h_ref, a1, a2)
    valid, grads, sums = fields(p_ref)

    def lap(a, b, c):
        return a - 2.0 * b + c

    c1, d1 = own_ref[0:EXT, :], own_ref[EXT : 2 * EXT, :]
    has_prev, has_next = k > 0, k < 7
    cl, dl = [jnp.where(has_prev, v, 0.0) for v in (prev_ref[0:EXT, :], prev_ref[EXT : 2 * EXT, :])]
    cr, dr = [jnp.where(has_next, v, 0.0) for v in (next_ref[0:EXT, :], next_ref[EXT : 2 * EXT, :])]
    cll = jnp.where(k > 1, prev2_ref[...], 0.0)
    crr = jnp.where(k < 6, next2_ref[...], 0.0)
    c2 = c1 + RATE * d1 + SMOOTH * lap(cl, c1, cr)
    c2l = jnp.where(has_prev, cl + RATE * dl + SMOOTH * lap(cll, cl, c1), 0.0)
    c2r = jnp.where(has_next, cr + RATE * dr + SMOOTH * lap(c1, cr, crr), 0.0)
    d2 = direction(valid, grads, sums, c2, apply_operator(a1, a2, c2))
    c3 = c2 + RATE * d2 + SMOOTH * lap(c2l, c2, c2r)
    d3 = direction(valid, grads, sums, c3, apply_operator(a1, a2, c3))
    u = c3 + RATE * d3
    for t in range(8):
        w = SMOOTH * (jnp.where(k == t + 1, 1.0, 0.0) - jnp.where(k == t, 1.0, 0.0) - jnp.where(k == 0, 1.0, 0.0))
        out_ref[t] = jnp.where(k <= t, 1.0, 0.0) * u + w * c3


def finish(pos_ref, m_ref, left_ref, right_ref, up_ref, dn_ref, down_ref, across_ref, parts_ref, r8_ref, turned_ref, out_ref, acc_ref, xs, ys, sx, sy, total_ref, mixed):
    step = pl.program_id(0)
    rim = rims(pos_ref, left_ref, right_ref, up_ref, dn_ref, step)

    @pl.when(step == 0)
    def _():
        acc = parts_ref[0]
        for t in range(1, 8):
            acc = acc + parts_ref[t]
        total_ref[...] = acc
        acc_ref[...] = total_ref[2:66, :]
        c8 = total_ref[pl.ds(4 * pos_ref[1], 8), :]
        rows = jnp.dot(r8_ref[...], c8, precision=lax.Precision.HIGHEST, preferred_element_type=F32)
        mixed[...] = rows.astype(BF)

    for s in range(BLOCK // 256):
        at = pl.ds(256 * s, 256)
        slopes(m_ref, rim, down_ref, across_ref, xs, ys, s)
        sx[:, at] = dot(mixed[:, 0:64], turned_ref[:, at])
        sy[:, at] = dot(mixed[:, 64:128], turned_ref[:, at])
        for c in range(ROWS // CHUNK):
            rows = pl.ds(CHUNK * c, CHUNK)
            m = m_ref[rows, at].astype(F32)
            out_ref[rows, at] = (m + sx[rows, at] * xs[rows, at] + sy[rows, at] * ys[rows, at]).astype(BF)


def strip_specs():
    return [
        pl.BlockSpec((ROWS, BLOCK), lambda j, pos: (0, j)),
        pl.BlockSpec((ROWS, 128), lambda j, pos: (0, jnp.maximum(8 * j - 1, 0))),
        pl.BlockSpec((ROWS, 128), lambda j, pos: (0, jnp.minimum(8 * j + 8, COLS // 128 - 1))),
        pl.BlockSpec((1, BLOCK), lambda j, pos: (0, j)),
        pl.BlockSpec((1, BLOCK), lambda j, pos: (0, j)),
        whole((ROWS, ROWS)),
        whole((512, 256)),
    ]


def whole(shape):
    return pl.BlockSpec(shape, lambda j, pos: (0,) * len(shape))


def ring(array, axis, by):
    n = lax.axis_size(axis)
    return lax.ppermute(array, axis, [(i, (i + by) % n) for i in range(n)])


FIELD = pltpu.VMEM((ROWS, BLOCK), BF)
WIDE = pltpu.VMEM((ROWS, BLOCK), F32)


def local(sections, anchor):
    strip = sections[0]
    pos = jnp.stack([lax.axis_index("chain"), lax.axis_index("quad")]).astype(jnp.int32)
    r8, (pairs, lin, plain, table, place, put), edge = host_tables()
    down, across = slope_tables()
    prior = ring(strip, "chain", 1)
    up = ring(strip[ROWS - 1 : ROWS], "quad", 1)
    dn = ring(strip[0:1], "quad", -1)
    turned = col_table()
    blocks = (strip, strip, strip, up, dn, down, across)
    h, p = pl.pallas_call(
        stage0,
        grid_spec=pltpu.PrefetchScalarGridSpec(
            num_scalar_prefetch=1,
            grid=(STEPS,),
            in_specs=strip_specs() + [whole(a.shape) for a in (pairs, lin, plain, table, place, put, edge)],
            out_specs=[whole((16, 128, 256)), whole((24, 128))],
            scratch_shapes=[WIDE] * 2 + [FIELD] * 7 + [pltpu.VMEM((96 * STEPS, 128), F32), pltpu.VMEM((32 * STEPS, 128), F32), pltpu.VMEM((8, 128), F32)],
        ),
        out_shape=[jax.ShapeDtypeStruct((16, 128, 256), BF), jax.ShapeDtypeStruct((24, 128), F32)],
        name="stage0",
    )(pos, *blocks, pairs, lin, plain, table, place, put, jnp.asarray(edge))
    h_all = lax.all_to_all(h, "quad", 0, 0, tiled=True)
    packed = pl.pallas_call(
        stage1,
        grid_spec=pltpu.PrefetchScalarGridSpec(
            num_scalar_prefetch=1,
            grid=(STEPS,),
            in_specs=strip_specs()
            + [whole(a.shape) for a in (lin, table, put)]
            + [
                pl.BlockSpec((ROWS, BLOCK), lambda j, pos: (0, jnp.where(pos[0] == 0, j, 0))),
                pl.BlockSpec((ROWS, BLOCK), lambda j, pos: (0, jnp.where(pos[0] == 0, 0, j))),
                whole((24, 128)),
            ],
            out_specs=whole((16, 40, 128)),
            scratch_shapes=[WIDE] * 2 + [FIELD] * 4 + [pltpu.VMEM((16 * STEPS, 128), F32), pltpu.VMEM((8, 128), F32)],
        ),
        out_shape=jax.ShapeDtypeStruct((16, 40, 128), F32),
        name="stage1",
    )(pos, *blocks, lin, table, put, anchor, prior, p)
    p_all = lax.all_to_all(packed, "quad", 0, 0, tiled=True)
    operator = [pltpu.VMEM((28, EXT, 128), F32)] * 2
    first, lead = pl.pallas_call(
        solve_a,
        out_shape=[jax.ShapeDtypeStruct((2 * EXT, 128), F32), jax.ShapeDtypeStruct((EXT, 128), F32)],
        scratch_shapes=operator,
        name="solve_a",
        compiler_params=pltpu.CompilerParams(vmem_limit_bytes=12 << 20),
    )(h_all, p_all)
    around = [ring(first, "chain", 1), ring(first, "chain", -1), ring(lead, "chain", 2), ring(lead, "chain", -2)]
    vm = pl.BlockSpec(memory_space=pltpu.VMEM)
    parts = pl.pallas_call(
        solve_b,
        in_specs=[pl.BlockSpec(memory_space=pltpu.SMEM)] + [vm] * 7,
        out_shape=jax.ShapeDtypeStruct((8, EXT, 128), F32),
        scratch_shapes=operator,
        name="solve_b",
        compiler_params=pltpu.CompilerParams(vmem_limit_bytes=12 << 20),
    )(pos, h_all, p_all, first, *around)
    parts = lax.all_to_all(parts, "chain", 0, 0, tiled=True)
    registered, accumulated = pl.pallas_call(
        finish,
        grid_spec=pltpu.PrefetchScalarGridSpec(
            num_scalar_prefetch=1,
            grid=(STEPS,),
            in_specs=strip_specs() + [whole((8, EXT, 128)), whole((ROWS, 8)), pl.BlockSpec((GRID, BLOCK), lambda j, pos: (0, j))],
            out_specs=[pl.BlockSpec((ROWS, BLOCK), lambda j, pos: (0, j)), whole((GRID, 128))],
            scratch_shapes=[WIDE] * 4 + [pltpu.VMEM((EXT, 128), F32), pltpu.VMEM((ROWS, 128), BF)],
        ),
        out_shape=[jax.ShapeDtypeStruct((ROWS, COLS), BF), jax.ShapeDtypeStruct((GRID, 128), F32)],
        name="finish",
    )(pos, *blocks, parts, jnp.asarray(r8), turned)
    return registered[None], accumulated[None]


def solution(mesh):
    in_specs = (P("chain", "quad", None), P("quad", None))
    out_specs = (P("chain", "quad", None), P("chain", None, None))
    return jax.shard_map(local, mesh=mesh, in_specs=in_specs, out_specs=out_specs, check_vma=False)
```

profile of v0, /device:TPU:1, one launch (start us, length us, event | category | flops | bytes accessed | tf_op | source)
XLA Modules:
  0.0 94.6 jit_solution(15254919829357580865)
XLA Ops:
  0.6 2.6 %collective-permute-start.2 = (bf16[256,4096]{1,0:T(8,128)(2,1)}, bf16[256,4096]{1,0:T(8,128)(2,1)S(1)}, u32[]{:S(2)}, u32[]{:S(2)}) collective-permute-start(bf16[256,4096]{1,0:T(8,128)(2,1)} %bitcast.9), channel_id=1, source_target_pairs={{0,16},{16,32},{32,48},{48,64},{64,80},{80,96},{96,112},{112,0},{1... | collective-permute-start | bytes 6291464 | tf_op jit(solution)/shard_map/ppermute | solution.py:459
  3.2 0.9 slice_bitcast_fusion
  4.1 1.4 %collective-permute-start = (bf16[1,4096]{1,0:T(2,128)(2,1)S(1)}, bf16[1,4096]{1,0:T(2,128)(2,1)S(1)}, u32[]{:S(2)}, u32[]{:S(2)}) collective-permute-start(bf16[1,4096]{1,0:T(2,128)(2,1)S(1)} %get-tuple-element.15), channel_id=1, source_target_pairs={{0,1},{1,2},{2,3},{3,4},{4,5},{5,6},{6,7},{7,8},{8,9},{9,10},{10,1... | collective-permute-start | bytes 24584 | tf_op jit(solution)/shard_map/ppermute | solution.py:459
  5.5 5.0 %collective-permute-start.1 = (bf16[1,4096]{1,0:T(2,128)(2,1)S(1)}, bf16[1,4096]{1,0:T(2,128)(2,1)S(1)}, u32[]{:S(2)}, u32[]{:S(2)}) collective-permute-start(bf16[1,4096]{1,0:T(2,128)(2,1)S(1)} %get-tuple-element.14), channel_id=1, source_target_pairs={{0,15},{1,0},{2,1},{3,2},{4,3},{5,4},{6,5},{7,6},{8,7},{9,8},{10,9... | collective-permute-start | bytes 24584 | tf_op jit(solution)/shard_map/ppermute | solution.py:459
  10.5 0.6 pad_add_fusion.pos_ref
  11.1 0.4 collective-permute-done.up_ref
  11.5 0.0 copy-start.3
  11.5 0.0 collective-permute-done.1.dn_ref
  11.5 0.6 copy-done.3
  12.1 0.0 copy-start.4
  12.1 0.6 copy-done.4
  12.7 12.6 %stage0.1 = (bf16[16,128,256]{2,1,0:T(8,128)(2,1)}, f32[24,128]{1,0:T(8,128)}) custom-call(s32[2]{0:T(128)} %pad_add_fusion.pos_ref, bf16[256,4096]{1,0:T(8,128)(2,1)} %bitcast.10, bf16[256,4096]{1,0:T(8,128)(2,1)} %bitcast.11, bf16[256,4096]{1,0:T(8,128)(2,1)} %bitcast.12, bf16[1,4096]{1,0:T(2,128)(2,1)} %copy-done.3, bf16[1,4096]{1,0:T(2,128)(2,1)} %copy-done.4, ...), custom_call_target="tpu_custom_call" | custom-call | tf_op jit(solution)/shard_map/stage0/pallas_call | solution.py:476
  25.4 5.7 %all-to-all-start = ((bf16[16,128,256]{2,1,0:T(8,128)(2,1)}), bf16[16,128,256]{2,1,0:T(8,128)(2,1)S(1)}, u32[]{:S(2)}, u32[]{:S(2)}) async-start(bf16[16,128,256]{2,1,0:T(8,128)(2,1)} %get-tuple-element.8), calls=%async_computation | async-start | bytes 2097152 | tf_op jit(solution)/shard_map/all_to_all | solution.py:488
  31.0 0.0 collective-permute-done.2.prior_ref
  31.0 0.0 copy-start.1
  31.0 1.3 %copy-done.1 = bf16[256,4096]{1,0:T(8,128)(2,1)} copy-done((bf16[256,4096]{1,0:T(8,128)(2,1)}, bf16[256,4096]{1,0:T(8,128)(2,1)S(1)}, u32[]{:S(2)}) %copy-start.1) | copy-done | bytes 2097176
  32.3 0.0 copy-start
  32.3 9.9 %stage1.1 = f32[16,40,128]{2,1,0:T(8,128)} custom-call(s32[2]{0:T(128)} %pad_add_fusion.pos_ref, bf16[256,4096]{1,0:T(8,128)(2,1)} %bitcast.13, bf16[256,4096]{1,0:T(8,128)(2,1)} %bitcast.14, bf16[256,4096]{1,0:T(8,128)(2,1)} %bitcast.15, bf16[1,4096]{1,0:T(2,128)(2,1)} %copy-done.3, bf16[1,4096]{1,0:T(2,128)(2,1)} %copy-done.4, ...), custom_call_target="tpu_custom_call" | custom-call | tf_op jit(solution)/shard_map/stage1/pallas_call | solution.py:489
  42.2 5.8 %all-to-all-done.h_ref = bf16[16,128,256]{2,1,0:T(8,128)(2,1)S(1)} async-done(((bf16[16,128,256]{2,1,0:T(8,128)(2,1)}), bf16[16,128,256]{2,1,0:T(8,128)(2,1)S(1)}, u32[]{:S(2)}, u32[]{:S(2)}) %all-to-all-start) | async-done | bytes 1048608 | tf_op jit(solution)/shard_map/all_to_all | solution.py:488
  48.0 4.1 %all-to-all-start.1 = ((f32[16,40,128]{2,1,0:T(8,128)}), f32[16,40,128]{2,1,0:T(8,128)S(1)}, u32[]{:S(2)}, u32[]{:S(2)}) async-start(f32[16,40,128]{2,1,0:T(8,128)} %stage1.1), calls=%async_computation.1 | async-start | bytes 655360 | tf_op jit(solution)/shard_map/all_to_all | solution.py:507
  52.2 8.3 %all-to-all-done.1.p_ref = f32[16,40,128]{2,1,0:T(8,128)S(1)} async-done(((f32[16,40,128]{2,1,0:T(8,128)}), f32[16,40,128]{2,1,0:T(8,128)S(1)}, u32[]{:S(2)}, u32[]{:S(2)}) %all-to-all-start.1) | async-done | bytes 327712 | tf_op jit(solution)/shard_map/all_to_all | solution.py:507
  60.5 1.4 %solve_a.1 = (f32[144,128]{1,0:T(8,128)S(1)}, f32[72,128]{1,0:T(8,128)S(1)}) custom-call(bf16[16,128,256]{2,1,0:T(8,128)(2,1)S(1)} %all-to-all-done.h_ref, f32[16,40,128]{2,1,0:T(8,128)S(1)} %all-to-all-done.1.p_ref), custom_call_target="tpu_custom_call" | custom-call | tf_op jit(solution)/shard_map/solve_a/pallas_call | solution.py:509
  61.9 3.1 %collective-permute-start.3 = (f32[144,128]{1,0:T(8,128)S(1)}, f32[144,128]{1,0:T(8,128)S(1)}, u32[]{:S(2)}, u32[]{:S(2)}) collective-permute-start(f32[144,128]{1,0:T(8,128)S(1)} %get-tuple-element.10.own_ref), channel_id=1, source_target_pairs={{0,16},{16,32},{32,48},{48,64},{64,80},{80,96},{96,112},{112,0},{1... | collective-permute-start | bytes 221192 | tf_op jit(solution)/shard_map/ppermute | solution.py:459
  65.0 0.0 collective-permute-start.4
  65.0 0.6 collective-permute-start.5
  65.6 2.0 %collective-permute-start.6 = (f32[72,128]{1,0:T(8,128)S(1)}, f32[72,128]{1,0:T(8,128)S(1)}, u32[]{:S(2)}, u32[]{:S(2)}) collective-permute-start(f32[72,128]{1,0:T(8,128)S(1)} %get-tuple-element.11), channel_id=1, source_target_pairs={{0,96},{16,112},{32,0},{48,16},{64,32},{80,48},{96,64},{112,80},{1... | collective-permute-start | bytes 110600 | tf_op jit(solution)/shard_map/ppermute | solution.py:459
  67.7 1.3 %collective-permute-done.5.prev2_ref = f32[72,128]{1,0:T(8,128)S(1)} collective-permute-done((f32[72,128]{1,0:T(8,128)S(1)}, f32[72,128]{1,0:T(8,128)S(1)}, u32[]{:S(2)}, u32[]{:S(2)}) %collective-permute-start.5) | collective-permute-done | bytes 36896 | tf_op jit(solution)/shard_map/ppermute | solution.py:459
  69.0 0.0 collective-permute-done.6.next2_ref
  69.0 0.0 collective-permute-done.3.prev_ref
  69.0 0.1 collective-permute-done.4.next_ref
  69.1 0.0 copy-done
  69.2 3.3 %solve_b.1 = f32[8,72,128]{2,1,0:T(8,128)} custom-call(s32[2]{0:T(128)S(1)} %copy-done, bf16[16,128,256]{2,1,0:T(8,128)(2,1)S(1)} %all-to-all-done.h_ref, f32[16,40,128]{2,1,0:T(8,128)S(1)} %all-to-all-done.1.p_ref, f32[144,128]{1,0:T(8,128)S(1)} %get-tuple-element.10.own_ref, f32[144,128]{1,0:T(8,128)S(1)} %collective-permute-done.3.prev_ref, ...), custom_call_target="tpu_custom_call" | custom-call | tf_op jit(solution)/shard_map/solve_b/pallas_call | solution.py:518
  72.5 7.4 %all-to-all-start.2 = ((f32[8,72,128]{2,1,0:T(8,128)}), f32[8,72,128]{2,1,0:T(8,128)S(1)}, u32[]{:S(2)}, u32[]{:S(2)}) async-start(f32[8,72,128]{2,1,0:T(8,128)} %solve_b.1), calls=%async_computation.2 | async-start | bytes 589824 | tf_op jit(solution)/shard_map/all_to_all | solution.py:526
  79.9 1.5 %fusion.2.turned_ref = bf16[64,4096]{1,0:T(8,128)(2,1)} fusion(f32[64]{0:T(128)S(1)} %iota_convert_fusion, f32[4096]{0:T(1024)S(1)} %add_multiply_fusion), kind=kLoop, calls=%fused_computation.4 | loop fusion | flops 4980736 | bytes 540928 | tf_op jit(solution)/shard_map/convert_element_type | solution.py:110
  81.4 5.3 %all-to-all-done.2.parts_ref = f32[8,72,128]{2,1,0:T(8,128)S(1)} async-done(((f32[8,72,128]{2,1,0:T(8,128)}), f32[8,72,128]{2,1,0:T(8,128)S(1)}, u32[]{:S(2)}, u32[]{:S(2)}) %all-to-all-start.2) | async-done | bytes 294944 | tf_op jit(solution)/shard_map/all_to_all | solution.py:526
  86.6 0.0 copy-start.2
  86.6 0.7 copy-done.2
  87.3 7.3 %finish.1 = (bf16[256,4096]{1,0:T(8,128)(2,1)}, f32[64,128]{1,0:T(8,128)}) custom-call(s32[2]{0:T(128)} %pad_add_fusion.pos_ref, bf16[256,4096]{1,0:T(8,128)(2,1)} %bitcast.16, bf16[256,4096]{1,0:T(8,128)(2,1)} %bitcast.17, bf16[256,4096]{1,0:T(8,128)(2,1)} %bitcast.18, bf16[1,4096]{1,0:T(2,128)(2,1)} %copy-done.3, bf16[1,4096]{1,0:T(2,128)(2,1)} %copy-done.4, ...), custom_call_target="tpu_custom_call" | custom-call | tf_op jit(solution)/shard_map/finish/pallas_call | solution.py:527
  (2 shorter events, 0.0 us)
Async XLA Ops:
  0.6 30.4 %collective-permute-start.2 = (bf16[256,4096]{1,0:T(8,128)(2,1)}, bf16[256,4096]{1,0:T(8,128)(2,1)S(1)}, u32[]{:S(2)}, u32[]{:S(2)}) collective-permute-start(bf16[256,4096]{1,0:T(8,128)(2,1)} %bitcast.9), channel_id=1, source_target_pairs={{0,16},{16,32},{32,48},{48,64},{64,80},{80,96},{96,112},{112,0},{1... | collective-permute-start | bytes 6291464 | tf_op jit(solution)/shard_map/ppermute | solution.py:459
  4.1 7.4 %collective-permute-start = (bf16[1,4096]{1,0:T(2,128)(2,1)S(1)}, bf16[1,4096]{1,0:T(2,128)(2,1)S(1)}, u32[]{:S(2)}, u32[]{:S(2)}) collective-permute-start(bf16[1,4096]{1,0:T(2,128)(2,1)S(1)} %get-tuple-element.15), channel_id=1, source_target_pairs={{0,1},{1,2},{2,3},{3,4},{4,5},{5,6},{6,7},{7,8},{8,9},{9,10},{10,1... | collective-permute-start | bytes 24584 | tf_op jit(solution)/shard_map/ppermute | solution.py:459
  5.5 6.0 %collective-permute-start.1 = (bf16[1,4096]{1,0:T(2,128)(2,1)S(1)}, bf16[1,4096]{1,0:T(2,128)(2,1)S(1)}, u32[]{:S(2)}, u32[]{:S(2)}) collective-permute-start(bf16[1,4096]{1,0:T(2,128)(2,1)S(1)} %get-tuple-element.14), channel_id=1, source_target_pairs={{0,15},{1,0},{2,1},{3,2},{4,3},{5,4},{6,5},{7,6},{8,7},{9,8},{10,9... | collective-permute-start | bytes 24584 | tf_op jit(solution)/shard_map/ppermute | solution.py:459
  11.5 0.6 copy-start.3
  12.1 0.6 copy-start.4
  25.4 22.7 %all-to-all-start = ((bf16[16,128,256]{2,1,0:T(8,128)(2,1)}), bf16[16,128,256]{2,1,0:T(8,128)(2,1)S(1)}, u32[]{:S(2)}, u32[]{:S(2)}) async-start(bf16[16,128,256]{2,1,0:T(8,128)(2,1)} %get-tuple-element.8), calls=%async_computation | async-start | bytes 2097152 | tf_op jit(solution)/shard_map/all_to_all | solution.py:488
  31.0 1.3 %copy-start.1 = (bf16[256,4096]{1,0:T(8,128)(2,1)}, bf16[256,4096]{1,0:T(8,128)(2,1)S(1)}, u32[]{:S(2)}) copy-start(bf16[256,4096]{1,0:T(8,128)(2,1)S(1)} %collective-permute-done.2.prior_ref) | copy-start | bytes 6291460
  32.3 36.8 %copy-start = (s32[2]{0:T(128)S(1)}, s32[2]{0:T(128)}, u32[]{:S(2)}) copy-start(s32[2]{0:T(128)} %pad_add_fusion.pos_ref) | copy-start | bytes 28
  48.0 12.5 %all-to-all-start.1 = ((f32[16,40,128]{2,1,0:T(8,128)}), f32[16,40,128]{2,1,0:T(8,128)S(1)}, u32[]{:S(2)}, u32[]{:S(2)}) async-start(f32[16,40,128]{2,1,0:T(8,128)} %stage1.1), calls=%async_computation.1 | async-start | bytes 655360 | tf_op jit(solution)/shard_map/all_to_all | solution.py:507
  61.9 7.1 %collective-permute-start.3 = (f32[144,128]{1,0:T(8,128)S(1)}, f32[144,128]{1,0:T(8,128)S(1)}, u32[]{:S(2)}, u32[]{:S(2)}) collective-permute-start(f32[144,128]{1,0:T(8,128)S(1)} %get-tuple-element.10.own_ref), channel_id=1, source_target_pairs={{0,16},{16,32},{32,48},{48,64},{64,80},{80,96},{96,112},{112,0},{1... | collective-permute-start | bytes 221192 | tf_op jit(solution)/shard_map/ppermute | solution.py:459
  65.0 4.2 %collective-permute-start.4 = (f32[144,128]{1,0:T(8,128)S(1)}, f32[144,128]{1,0:T(8,128)S(1)}, u32[]{:S(2)}, u32[]{:S(2)}) collective-permute-start(f32[144,128]{1,0:T(8,128)S(1)} %get-tuple-element.10.own_ref), channel_id=1, source_target_pairs={{0,112},{16,0},{32,16},{48,32},{64,48},{80,64},{96,80},{112,96},{1... | collective-permute-start | bytes 221192 | tf_op jit(solution)/shard_map/ppermute | solution.py:459
  65.0 4.0 %collective-permute-start.5 = (f32[72,128]{1,0:T(8,128)S(1)}, f32[72,128]{1,0:T(8,128)S(1)}, u32[]{:S(2)}, u32[]{:S(2)}) collective-permute-start(f32[72,128]{1,0:T(8,128)S(1)} %get-tuple-element.11), channel_id=1, source_target_pairs={{0,32},{16,48},{32,64},{48,80},{64,96},{80,112},{96,0},{112,16},{1... | collective-permute-start | bytes 110600 | tf_op jit(solution)/shard_map/ppermute | solution.py:459
  65.6 3.4 %collective-permute-start.6 = (f32[72,128]{1,0:T(8,128)S(1)}, f32[72,128]{1,0:T(8,128)S(1)}, u32[]{:S(2)}, u32[]{:S(2)}) collective-permute-start(f32[72,128]{1,0:T(8,128)S(1)} %get-tuple-element.11), channel_id=1, source_target_pairs={{0,96},{16,112},{32,0},{48,16},{64,32},{80,48},{96,64},{112,80},{1... | collective-permute-start | bytes 110600 | tf_op jit(solution)/shard_map/ppermute | solution.py:459
  72.5 14.2 %all-to-all-start.2 = ((f32[8,72,128]{2,1,0:T(8,128)}), f32[8,72,128]{2,1,0:T(8,128)S(1)}, u32[]{:S(2)}, u32[]{:S(2)}) async-start(f32[8,72,128]{2,1,0:T(8,128)} %solve_b.1), calls=%async_computation.2 | async-start | bytes 589824 | tf_op jit(solution)/shard_map/all_to_all | solution.py:526
  86.6 0.7 copy-start.2
where the time goes:
time: 95.2 us; the launch traced here: 94.6 us
  Pallas kernels  34.4 us (36%)
  starting transfers between devices  31.9 us (34%)
  waiting for transfers between devices  21.4 us (22%)
  local copies, waits for them, and re-layouts  4.11 us (4%)
  other arithmetic  2.12 us (2%)
    ppermute x7, starting transfers between devices, ring(): return lax.ppermute(array, axis, [(i, (i + by) % n) for i in range(n)])  14.7 us
    pallas_call x1, Pallas kernels, local(): pl.pallas_call(stage0, grid_spec=pltpu.PrefetchScalarGridSpec(num_scalar_...  12.6 us
    pallas_call x1, Pallas kernels, local(): pl.pallas_call(stage1, grid_spec=pltpu.PrefetchScalarGridSpec(num_scalar_...  9.87 us
    all_to_all x1, waiting for transfers between devices, local(): p_all = lax.all_to_all(packed, 'quad', 0, 0, tiled=True)  8.35 us
    all_to_all x1, starting transfers between devices, local(): parts = lax.all_to_all(parts, 'chain', 0, 0, tiled=True)  7.39 us
    pallas_call x1, Pallas kernels, local(): pl.pallas_call(finish, grid_spec=pltpu.PrefetchScalarGridSpec(num_scalar_...  7.26 us
    all_to_all x1, waiting for transfers between devices, local(): h_all = lax.all_to_all(h, 'quad', 0, 0, tiled=True)  5.81 us
    all_to_all x1, starting transfers between devices, local(): h_all = lax.all_to_all(h, 'quad', 0, 0, tiled=True)  5.65 us
  transfers between devices with their start and end apart: 10, of which 6 were waited for; matrix products, arithmetic and copies ran while one was open for 3% of the time, Pallas kernels for 24%

commit v1 on v0

v1 whole, which is shorter than its diff:
```python
import jax
import jax.numpy as jnp
import numpy as np
from jax import lax
from jax.experimental import pallas as pl
from jax.experimental.pallas import tpu as pltpu
from jax.sharding import PartitionSpec as P

GRID = 64
SPACING = 64
ROWS = 256
COLS = 4096
BLOCK = 1024
STEPS = COLS // BLOCK
CHUNK = 32
EXT = 72
PIXELS = 4096.0 * 4096.0
EPS = 1e-6
RATE = 0.25
SMOOTH = 0.25
BF = jnp.bfloat16
F32 = jnp.float32


def weight(offset, xp):
    d = xp.abs(offset)
    near = 2.0 / 3.0 - d * d + 0.5 * d * d * d
    r = 2.0 - d
    far = r * r * r / 6.0
    return xp.where(d < 1.0, near, xp.where(d < 2.0, far, 0.0 * d))


def local_rows():
    r = np.arange(ROWS, dtype=np.float32)
    j = np.arange(8, dtype=np.float32) - 2.0
    off = (r[:, None] + np.float32(0.5)) / np.float32(SPACING) - j[None, :] - np.float32(0.5)
    return weight(off.astype(np.float32), np).astype(np.float32)


def hi_lo(a):
    hi = a.astype(BF)
    return hi, (a - hi.astype(F32)).astype(BF)


def split3(a):
    hi = a.astype(BF)
    rest = a - hi.astype(F32)
    mid = rest.astype(BF)
    lo = (rest - mid.astype(F32)).astype(BF)
    return jnp.concatenate([hi.astype(F32), mid.astype(F32), lo.astype(F32)], axis=0).astype(BF)


def sum3(a, n):
    return a[0:n] + a[n : 2 * n] + a[2 * n : 3 * n]


def two(a):
    hi = a.astype(np.dtype(BF)).astype(np.float32)
    return np.concatenate([hi, a - hi], 0)


def host_tables():
    r8 = local_rows()
    pairs = np.zeros((32, ROWS), np.float32)
    c8 = r8.astype(np.dtype(BF)).astype(np.float32)
    lanes = np.zeros((BLOCK, 128), np.float32)
    cols = np.zeros((BLOCK, 128), np.float32)
    place = np.zeros((STEPS * 128, 256), np.float32)
    put = np.zeros((STEPS * 128, 128), np.float32)
    for s in range(4):
        cols[256 * s : 256 * s + 256, 8 * s : 8 * s + 8] = c8
    for d in range(4):
        for e in range(8 - d):
            pairs[d * 8 + e] = r8[:, e] * r8[:, e + d]
            for s in range(4):
                lanes[256 * s : 256 * s + 256, 32 * s + 8 * d + e] = c8[:, e] * c8[:, e + d]
                for t in range(STEPS):
                    i = 16 * t + 4 * s - 2 + e
                    if i >= 0 and i + d < GRID:
                        place[128 * t + 32 * s + 8 * d + e, 64 * d + i] = 1.0
    for t in range(STEPS):
        for s in range(4):
            for e in range(8):
                i = 16 * t + 4 * s - 2 + e
                if 0 <= i < GRID:
                    put[128 * t + 8 * s + e, i] = 1.0
    diff = np.zeros((8, ROWS), np.float32)
    diff[:, 1:] += 0.5 * r8.T[:, :-1]
    diff[:, :-1] -= 0.5 * r8.T[:, 1:]
    lanes_hi = lanes.astype(np.dtype(BF)).astype(np.float32)
    down = 0.5 * (np.eye(ROWS, k=1) - np.eye(ROWS, k=-1))
    across = np.zeros((512, 256), np.float32)
    o = np.arange(256)
    across[o + 129, o] = 0.5
    across[o + 127, o] = -0.5
    plain = np.concatenate([two(r8.T), two(diff), np.ones((16, ROWS), np.float32)], 0)
    wide = np.concatenate([lanes_hi, lanes - lanes_hi], 1)
    halves = np.concatenate([np.concatenate([cols[0:512], cols[512:1024]], 1), np.concatenate([put[0:256], put[256:512]], 1)], 0)
    blob = np.concatenate([down, across, two(pairs), two(r8.T), plain, wide, place, halves], 0)
    edge = np.stack([-0.5 * r8[0], 0.5 * r8[ROWS - 1]], 0).reshape(16, 1) * np.ones((1, 128), np.float32)
    return r8, jnp.asarray(blob.astype(np.dtype(BF))), jnp.asarray(edge.astype(np.float32))


DOWN, ACROSS, PAIRS, LIN, PLAIN, TABLE, PLACE, COLT, PUT, BLOB = 0, 256, 768, 832, 848, 896, 1920, 2432, 2944, 3200


def col_part(blob_ref, lhs):
    return dot(lhs[:, 0:512], blob_ref[COLT : COLT + 512, 0:128]) + dot(lhs[:, 512:1024], blob_ref[COLT : COLT + 512, 128:256])


def put_rows(blob_ref, t):
    return blob_ref[PUT + 128 * (t % 2) : PUT + 128 * (t % 2) + 128, 128 * (t // 2) : 128 * (t // 2) + 128]


def col_table():
    x = jnp.arange(COLS, dtype=jnp.int32).astype(F32)
    j = jnp.arange(GRID, dtype=jnp.int32).astype(F32)
    return weight((x[None, :] + 0.5) / SPACING - j[:, None] - 0.5, jnp).astype(BF)


def dot(a, b):
    return jnp.dot(a, b, preferred_element_type=F32)


def tile(step, size=BLOCK):
    return pl.ds(pl.multiple_of(size * step, size), size)


def slopes(pos_ref, m_ref, up_ref, dn_ref, blob_ref, lhs, xs, ys, step):
    start = BLOCK * step
    left = m_ref[:, pl.ds(pl.multiple_of(jnp.maximum(start - 128, 0), 128), 128)]
    right = m_ref[:, pl.ds(pl.multiple_of(jnp.minimum(start + BLOCK, COLS - 128), 128), 128)]
    left = jnp.where(step > 0, left.astype(F32), 0.0).astype(BF)
    right = jnp.where(step < STEPS - 1, right.astype(F32), 0.0).astype(BF)
    block = m_ref[:, tile(step)]
    ext = jnp.concatenate([left, block, right], axis=1)
    stack = jnp.concatenate([ext[:, 256 * s : 256 * s + 512] for s in range(4)], axis=0)
    x = dot(stack, blob_ref[ACROSS : ACROSS + 512, :])
    for s in range(4):
        xs[:, pl.ds(pl.multiple_of(start + 256 * s, 256), 256)] = x[256 * s : 256 * s + 256]
    up = jnp.where(pos_ref[1] > 0, up_ref[:, tile(step)].astype(F32), 0.0)
    dn = jnp.where(pos_ref[1] < 15, dn_ref[:, tile(step)].astype(F32), 0.0)
    both = dot(jnp.concatenate([blob_ref[DOWN : DOWN + 256, :], lhs], axis=0), block)
    at = tile(step)
    ys[:, at] = both[0:256]
    ys[0:1, at] = ys[0:1, at] - 0.5 * up
    ys[ROWS - 1 : ROWS, at] = ys[ROWS - 1 : ROWS, at] + 0.5 * dn
    return up, dn, both[256:]


def fold8(a):
    return jnp.sum(a.reshape(CHUNK // 8, 8, a.shape[1]), axis=0)


def lanes_to_row(a):
    s = jnp.sum(a, axis=0, keepdims=True)
    out = s[:, 0:128]
    for t in range(1, s.shape[1] // 128):
        out = out + s[:, 128 * t : 128 * t + 128]
    return out


def rows_of(lin, hi, lo):
    a = dot(lin, hi)
    b = dot(lin, lo)
    return a[0:8] + a[8:16] + b[0:8]


def stage0(pos_ref, m_ref, up_ref, dn_ref, blob_ref, edge_ref, h_ref, p_ref, xs, ys, fxx, fxy, fyy, mxh, mxl, myh, myl, zacc, lacc, l1_ref, sums):
    sums[...] = jnp.zeros((8, 128), F32)

    def body(step, carry):
        up, dn, ones = slopes(pos_ref, m_ref, up_ref, dn_ref, blob_ref, blob_ref[PLAIN : PLAIN + 48, :], xs, ys, step)
        pairs = blob_ref[PAIRS : PAIRS + 64, :]
        lin = blob_ref[LIN : LIN + 16, :]
        sumsq = jnp.zeros((8, 256), F32)
        t_parts, lx, ly = [], [], []
        for s in range(BLOCK // 256):
            at = pl.ds(256 * s, 256)
            from_m = pl.ds(pl.multiple_of(BLOCK * step + 256 * s, 256), 256)
            for c in range(ROWS // CHUNK):
                rows = pl.ds(CHUNK * c, CHUNK)
                m, x, y = m_ref[rows, from_m].astype(F32), xs[rows, from_m], ys[rows, from_m]
                fxx[rows, at] = (x * x).astype(BF)
                fxy[rows, at] = (x * y).astype(BF)
                fyy[rows, at] = (y * y).astype(BF)
                mxh[rows, at], mxl[rows, at] = hi_lo(m * x)
                myh[rows, at], myl[rows, at] = hi_lo(m * y)
                sumsq = sumsq + fold8(m * m)
            trio = []
            for f in (fxx, fxy, fyy):
                t = dot(pairs, f[:, at])
                trio.append(t[0:32] + t[32:64])
            t_parts.append(jnp.concatenate(trio, axis=0))
            lx.append(rows_of(lin, mxh[:, at], mxl[:, at]))
            ly.append(rows_of(lin, myh[:, at], myl[:, at]))
        t_hi, t_lo = hi_lo(jnp.concatenate(t_parts, axis=1))
        z = dot(jnp.concatenate([t_hi, t_lo], axis=0), blob_ref[TABLE : TABLE + 1024, :])
        z = z[0:96] + z[96:192]
        zacc[tile(step, 96), :] = z[:, 0:128] + z[:, 128:256]
        l1_ref[:, tile(step)] = ones[0:8] + ones[8:16]
        l1y = ones[16:24] + ones[24:32]
        l1y = l1y + edge_ref[0:8, 0:1] * up + edge_ref[8:16, 0:1] * dn
        rows3 = jnp.concatenate([jnp.concatenate(lx, axis=1), jnp.concatenate(ly, axis=1), l1y], axis=0)
        lacc[tile(step, 24), :] = sum3(col_part(blob_ref, split3(rows3)), 24)
        sums[0:1, :] += lanes_to_row(ones[32:33])
        sums[1:2, :] += lanes_to_row(sumsq)
        return carry

    lax.fori_loop(0, STEPS, body, 0)
    l1 = l1_ref[...]
    col = lax.broadcasted_iota(jnp.int32, l1.shape, 1)
    after = jnp.where(col < COLS - 1, pltpu.roll(l1, COLS - 1, 1), 0.0)
    before = jnp.where(col > 0, pltpu.roll(l1, 1, 1), 0.0)
    l1x = split3(0.5 * (after - before))
    h = jnp.zeros((288, 256), F32)
    p = jnp.zeros((96, 128), F32)
    for t in range(STEPS):
        h = h + dot(split3(zacc[96 * t : 96 * t + 96, :]), blob_ref[PLACE + 128 * t : PLACE + 128 * t + 128, :])
        one = sum3(col_part(blob_ref, l1x[:, BLOCK * t : BLOCK * t + BLOCK]), 8)
        p = p + dot(split3(jnp.concatenate([lacc[24 * t : 24 * t + 24, :], one], axis=0)), put_rows(blob_ref, t))
    h_ref[...] = sum3(h, 96)
    p = sum3(p, 32)
    p_ref[0:8, :] = p[0:8] + pltpu.roll(p[8:16], 64, 1)
    p_ref[8:16, :] = p[24:32] + pltpu.roll(p[16:24], 64, 1)
    p_ref[16:24, :] = sums[...]


def cross_part(pos_ref, m_ref, xs, ys, blob_ref, anchor_hbm, prior_hbm, fxh, fxl, fyh, fyl, f_ref, fetched, lacc, sums):
    def fetch(i, from_hbm):
        return pltpu.make_async_copy(from_hbm.at[:, tile(i)], f_ref.at[:, tile(i)], fetched.at[i])

    for i in range(STEPS):

        @pl.when(pos_ref[0] == 0)
        def _():
            fetch(i, anchor_hbm).start()

        @pl.when(pos_ref[0] > 0)
        def _():
            fetch(i, prior_hbm).start()

    sums[...] = jnp.zeros((8, 128), F32)

    def body(step, carry):
        fetch(step, prior_hbm).wait()
        lin = blob_ref[LIN : LIN + 16, :]
        cross = jnp.zeros((8, 256), F32)
        whole_sum = jnp.zeros((8, 256), F32)
        lx, ly = [], []
        for s in range(BLOCK // 256):
            at = pl.ds(256 * s, 256)
            from_m = pl.ds(pl.multiple_of(BLOCK * step + 256 * s, 256), 256)
            for c in range(ROWS // CHUNK):
                rows = pl.ds(CHUNK * c, CHUNK)
                m, x, y = m_ref[rows, from_m].astype(F32), xs[rows, from_m], ys[rows, from_m]
                f = f_ref[rows, from_m].astype(F32)
                fxh[rows, at], fxl[rows, at] = hi_lo(f * x)
                fyh[rows, at], fyl[rows, at] = hi_lo(f * y)
                cross = cross + fold8(f * m)
                whole_sum = whole_sum + fold8(f)
            lx.append(rows_of(lin, fxh[:, at], fxl[:, at]))
            ly.append(rows_of(lin, fyh[:, at], fyl[:, at]))
        rows2 = jnp.concatenate([jnp.concatenate(lx, axis=1), jnp.concatenate(ly, axis=1)], axis=0)
        lacc[tile(step, 16), :] = sum3(col_part(blob_ref, split3(rows2)), 16)
        sums[0:1, :] += lanes_to_row(cross)
        sums[1:2, :] += lanes_to_row(whole_sum)
        return carry

    lax.fori_loop(0, STEPS, body, 0)
    p = jnp.zeros((48, 128), F32)
    for i in range(STEPS):
        p = p + dot(split3(lacc[16 * i : 16 * i + 16, :]), put_rows(blob_ref, i))
    p = sum3(p, 16)
    return p[0:8] + pltpu.roll(p[8:16], 64, 1)


def rows8(shape):
    return lax.broadcasted_iota(jnp.int32, shape, 0) % 8


def stage1(pos_ref, m_ref, xs, ys, blob_ref, anchor_hbm, prior_hbm, h_ref, p_ref, out_ref, *scratch):
    sums = scratch[-1]
    part = cross_part(pos_ref, m_ref, xs, ys, blob_ref, anchor_hbm, prior_hbm, *scratch)
    row = rows8((8, 256))
    lane = lax.broadcasted_iota(jnp.int32, (8, 256), 1)
    last = jnp.zeros((8, 256), F32)
    for t, v in enumerate((sums[0:1, :], sums[1:2, :], p_ref[16:17, :], p_ref[17:18, :])):
        rest = jnp.sum(v, axis=1, keepdims=True)
        for u in range(3):
            piece = rest.astype(BF).astype(F32)
            rest = rest - piece
            last = last + jnp.where((row == 6) & (lane == 4 * u + t), piece, 0.0)
    groups = []
    lows = []
    for c in range(3):
        a, b, d, e = [h_ref[32 * c + 8 * t : 32 * c + 8 * t + 8, :] for t in range(4)]
        groups += [a, b + jnp.where(row == 7, pltpu.roll(e, 3, 0), 0.0), d + jnp.where(row > 5, pltpu.roll(e, 4, 0), 0.0)]
        last = last + jnp.where((row == 2 * c) | (row == 2 * c + 1), shifted(e, 2 * c, 0), 0.0)
        low = [v[:, 0:128] - v[:, 0:128].astype(BF).astype(F32) for v in (a, b)]
        lows.append(jnp.concatenate(low, axis=1))
    groups.append(last)
    groups += lows
    for v in (part, p_ref[0:8, :], p_ref[8:16, :]):
        groups.append(jnp.concatenate([v, v - v.astype(BF).astype(F32)], axis=1))
    packed = jnp.concatenate(groups, axis=0).astype(BF)
    for t in range(16):
        out_ref[t] = packed


def shifted(a, by, axis):
    n = a.shape[axis]
    by = by % n
    return a if by == 0 else pltpu.roll(a, by, axis)


def unpack(h_ref):
    out = [([], []) for _ in range(16)]
    for q in range(16):
        for t in range(8):
            both = h_ref[q, 16 * t : 16 * t + 16, :].astype(F32)
            out[2 * t][q % 2].append(both[0:8])
            out[2 * t + 1][q % 2].append(both[8:16])
    return [[jnp.concatenate(v, axis=0) for v in pair] for pair in out]


def stacked(even, odd):
    pad = jnp.zeros((8, even.shape[1]), F32)
    return jnp.concatenate([even, pad], axis=0) + pltpu.roll(jnp.concatenate([odd, pad], axis=0), 4, 0)


def build_operator(groups, a1, a2):
    lane = lax.broadcasted_iota(jnp.int32, (EXT, 128), 1)
    low = lane < 64
    row = rows8((64, 256))
    pad = jnp.zeros((64, 128), F32)

    def piece(c, dj, side):
        a, b, d, last, rest = [groups[g][side] for g in (3 * c, 3 * c + 1, 3 * c + 2, 9, 10 + c)]
        if dj == 0:
            return a + jnp.concatenate([rest[:, 0:128], pad], axis=1)
        if dj == 1:
            return jnp.where(row < 7, b, 0.0) + jnp.concatenate([rest[:, 128:256], pad], axis=1)
        if dj == 2:
            return jnp.where(row < 6, d, 0.0)
        e = jnp.where(row == 4, pltpu.roll(b, 61, 0), jnp.where(row > 1, pltpu.roll(d, 60, 0), shifted(last, -2 * c, 0)))
        return jnp.where(row < 5, e, 0.0)

    for dj in range(4):
        grid = [stacked(piece(c, dj, 0), piece(c, dj, 1)) for c in range(3)]
        for pair in range(2):
            xx, xy, yy = [g[:, 128 * pair : 128 * pair + 128] for g in grid]
            xx_s, xy_s, yy_s = [pltpu.roll(v, 64, 1) for v in (xx, xy, yy)]
            for odd in range(2):
                di = 2 * pair + odd
                if odd == 0:
                    one = jnp.where(low, xx, yy_s)
                    two = jnp.where(low, xy, xy_s)
                else:
                    one = jnp.where(low, xx_s, yy)
                    two = jnp.where(low, xy_s, xy)
                a1[dj * 7 + 3 + di] = one
                a2[dj * 7 + 3 + di] = two
                if di > 0:
                    a1[dj * 7 + 3 - di] = pltpu.roll(one, di, 1)
                    a2[dj * 7 + 3 - di] = pltpu.roll(two, di, 1)


def apply_operator(a1, a2, c):
    cs = pltpu.roll(c, 64, 1)
    plain = [(shifted(c, -di, 1), shifted(cs, -di, 1)) for di in range(-3, 4)]
    y = jnp.zeros((EXT, 128), F32)
    for dj in range(4):
        ahead = jnp.zeros((EXT, 128), F32)
        back = jnp.zeros((EXT, 128), F32)
        for t in range(7):
            p, s = plain[t]
            u, v = a1[dj * 7 + t], a2[dj * 7 + t]
            ahead = ahead + u * shifted(p, -dj, 0) + v * shifted(s, -dj, 0)
            if dj:
                back = back + u * p + v * s
        y = y + ahead
        if dj:
            y = y + pltpu.roll(back, dj, 0)
    return y


def total(a):
    return jnp.sum(jnp.sum(a, axis=0, keepdims=True), axis=1, keepdims=True)


def fields(groups):
    row = lax.broadcasted_iota(jnp.int32, (EXT, 128), 0)
    valid = (row >= 2) & (row < 66)
    grads = []
    for g in (13, 14, 15):
        even, odd = [v[:, 0:128] + v[:, 128:256] for v in groups[g]]
        grads.append(jnp.where(valid, stacked(even, odd), 0.0))
    last = (groups[9][0] + groups[9][1])[:, 0:128]
    lane = lax.broadcasted_iota(jnp.int32, (64, 128), 1)
    here = (rows8((64, 128)) == 6) & (lane < 12)
    sums = [total(jnp.where(here & (lane % 4 == t), last, 0.0)) for t in range(4)]
    return valid, grads, sums


def narrow(a):
    return pltpu.roll(a, EXT - 2, 0)[0:GRID]


def widen(a):
    return pltpu.roll(jnp.concatenate([a, jnp.zeros((EXT - GRID, 128), F32)], axis=0), 2, 0)


def direction(valid, grads, sums, c, hc):
    gf, gm, g1 = grads
    s_fm, s_f, s_m, s_mm = sums
    mean_f = s_f / PIXELS
    if c is None:
        s_w, s_ww, s_fw, gw = s_m, s_mm, s_fm, gm
    else:
        s_w = s_m + total(g1 * c)
        s_ww = s_mm + total(c * (2.0 * gm + hc))
        s_fw = s_fm + total(gf * c)
        gw = gm + hc
    mean_w = s_w / PIXELS
    var = s_ww - PIXELS * mean_w * mean_w
    cross = s_fw - PIXELS * mean_f * mean_w
    den = jnp.sqrt(var + EPS)
    ratio = cross / den / (var + EPS)
    g = PIXELS * ((gf - mean_f * g1) / den - ratio * (gw - mean_w * g1))
    g = jnp.where(valid, g, 0.0)
    return g / jnp.sqrt(total(g * g) / 8192.0 + EPS)


def solve_a(h_ref, out_ref, lead_ref, a1, a2):
    groups = unpack(h_ref)
    build_operator(groups, a1, a2)
    valid, grads, sums = fields(groups)
    c = RATE * direction(valid, grads, sums, None, None)
    d = direction(valid, grads, sums, c, apply_operator(a1, a2, c))
    lead = narrow(c)
    out_ref[0:GRID, :] = lead
    lead_ref[...] = lead
    out_ref[GRID : 2 * GRID, :] = narrow(d)


def solve_b(pos_ref, h_ref, own_ref, prev_ref, next_ref, prev2_ref, next2_ref, out_ref, a1, a2):
    k = pos_ref[0]
    groups = unpack(h_ref)
    build_operator(groups, a1, a2)
    valid, grads, sums = fields(groups)

    def lap(a, b, c):
        return a - 2.0 * b + c

    def pair(ref, there):
        return [jnp.where(there, widen(ref[GRID * t : GRID * t + GRID, :]), 0.0) for t in range(2)]

    has_prev, has_next = k > 0, k < 7
    c1, d1 = pair(own_ref, k >= 0)
    cl, dl = pair(prev_ref, has_prev)
    cr, dr = pair(next_ref, has_next)
    cll = jnp.where(k > 1, widen(prev2_ref[...]), 0.0)
    crr = jnp.where(k < 6, widen(next2_ref[...]), 0.0)
    c2 = c1 + RATE * d1 + SMOOTH * lap(cl, c1, cr)
    c2l = jnp.where(has_prev, cl + RATE * dl + SMOOTH * lap(cll, cl, c1), 0.0)
    c2r = jnp.where(has_next, cr + RATE * dr + SMOOTH * lap(c1, cr, crr), 0.0)
    d2 = direction(valid, grads, sums, c2, apply_operator(a1, a2, c2))
    c3 = c2 + RATE * d2 + SMOOTH * lap(c2l, c2, c2r)
    d3 = direction(valid, grads, sums, c3, apply_operator(a1, a2, c3))
    u = narrow(c3 + RATE * d3)
    c3 = narrow(c3)
    for t in range(8):
        w = SMOOTH * (jnp.where(k == t + 1, 1.0, 0.0) - jnp.where(k == t, 1.0, 0.0) - jnp.where(k == 0, 1.0, 0.0))
        out_ref[t] = jnp.where(k <= t, 1.0, 0.0) * u + w * c3


def finish(pos_ref, m_ref, xs, ys, parts_ref, r8_hbm, turned_ref, out_ref, acc_ref, sx, sy, total_ref, mixed, buf, r8_ref, sems, fetched):
    bring = pltpu.make_async_copy(r8_hbm, r8_ref, fetched)
    bring.start()
    acc = parts_ref[0]
    for t in range(1, 8):
        acc = acc + parts_ref[t]
    acc_ref[...] = acc
    total_ref[...] = widen(acc)
    c8 = total_ref[pl.ds(4 * pos_ref[1], 8), :]
    bring.wait()
    mixed[...] = jnp.dot(r8_ref[...], c8, precision=lax.Precision.HIGHEST, preferred_element_type=F32).astype(BF)

    def copy(step):
        return pltpu.make_async_copy(buf.at[:, tile(step)], out_ref.at[:, tile(step)], sems.at[step])

    def body(step, carry):
        sx[...] = dot(mixed[:, 0:64], turned_ref[:, tile(step)])
        sy[...] = dot(mixed[:, 64:128], turned_ref[:, tile(step)])
        for s in range(BLOCK // 256):
            at = pl.ds(256 * s, 256)
            from_m = pl.ds(pl.multiple_of(BLOCK * step + 256 * s, 256), 256)
            for c in range(ROWS // CHUNK):
                rows = pl.ds(CHUNK * c, CHUNK)
                m = m_ref[rows, from_m].astype(F32)
                buf[rows, from_m] = (m + sx[rows, at] * xs[rows, from_m] + sy[rows, at] * ys[rows, from_m]).astype(BF)
        copy(step).start()
        return carry

    lax.fori_loop(0, STEPS, body, 0)
    for step in range(STEPS):
        copy(step).wait()


def ring(array, axis, by):
    n = lax.axis_size(axis)
    return lax.ppermute(array, axis, [(i, (i + by) % n) for i in range(n)])


FIELD = pltpu.VMEM((ROWS, BLOCK), BF)
WIDE = pltpu.VMEM((ROWS, BLOCK), F32)
SMALL = pltpu.VMEM((8, 128), F32)


def call(kernel, name, args, outs, scratch, limit, hbm_out=False, hbm_in=()):
    vm = pl.BlockSpec(memory_space=pltpu.VMEM)
    specs = [pl.BlockSpec(memory_space=pltpu.SMEM) if a.dtype == jnp.int32 else vm for a in args]
    for i in hbm_in:
        specs[i] = pl.BlockSpec(memory_space=pltpu.HBM)
    return pl.pallas_call(
        kernel,
        in_specs=specs,
        out_specs=[pl.BlockSpec(memory_space=pl.ANY) if hbm_out and i == 0 else vm for i in range(len(outs))],
        out_shape=outs,
        scratch_shapes=scratch,
        name=name,
        compiler_params=pltpu.CompilerParams(vmem_limit_bytes=limit << 20),
    )(*args)


def local(sections, anchor):
    strip = sections[0]
    pos = jnp.stack([lax.axis_index("chain"), lax.axis_index("quad")]).astype(jnp.int32)
    r8, blob, edge = host_tables()
    prior = ring(strip, "chain", 1)
    up = ring(strip[ROWS - 1 : ROWS], "quad", 1)
    dn = ring(strip[0:1], "quad", -1)
    turned = col_table()
    shape = jax.ShapeDtypeStruct
    slope = shape((ROWS, COLS), F32)
    h, p, xs, ys = call(
        stage0,
        "stage0",
        (pos, strip, up, dn, blob, edge),
        [shape((96, 256), F32), shape((24, 128), F32), slope, slope],
        [FIELD] * 7 + [pltpu.VMEM((96 * STEPS, 128), F32), pltpu.VMEM((24 * STEPS, 128), F32), pltpu.VMEM((8, COLS), F32), SMALL],
        24,
    )
    (packed,) = call(
        stage1,
        "stage1",
        (pos, strip, xs, ys, blob, anchor, prior, h, p),
        [shape((16, 128, 256), BF)],
        [FIELD] * 4 + [pltpu.VMEM((ROWS, COLS), BF), pltpu.SemaphoreType.DMA((STEPS,)), pltpu.VMEM((16 * STEPS, 128), F32), SMALL],
        20,
        hbm_in=(5, 6),
    )
    packed, turned = lax.optimization_barrier((packed, turned))
    h_all = lax.all_to_all(packed, "quad", 0, 0, tiled=True)
    operator = [pltpu.VMEM((28, EXT, 128), F32)] * 2
    first, lead = call(solve_a, "solve_a", (h_all,), [shape((2 * GRID, 128), F32), shape((GRID, 128), F32)], operator, 12)
    around = [ring(first, "chain", 1), ring(first, "chain", -1), ring(lead, "chain", 2), ring(lead, "chain", -2)]
    (parts,) = call(solve_b, "solve_b", (pos, h_all, first, *around), [shape((8, GRID, 128), F32)], operator, 12)
    parts = lax.all_to_all(parts, "chain", 0, 0, tiled=True)
    registered, accumulated = call(
        finish,
        "finish",
        (pos, strip, xs, ys, parts, jnp.asarray(r8), turned),
        [shape((ROWS, COLS), BF), shape((GRID, 128), F32)],
        [WIDE] * 2
        + [pltpu.VMEM((EXT, 128), F32), pltpu.VMEM((ROWS, 128), BF), pltpu.VMEM((ROWS, COLS), BF), pltpu.VMEM((ROWS, 8), F32)]
        + [pltpu.SemaphoreType.DMA((STEPS,)), pltpu.SemaphoreType.DMA],
        24,
        hbm_out=True,
        hbm_in=(5,),
    )
    return registered[None], accumulated[None]


def solution(mesh):
    in_specs = (P("chain", "quad", None), P("quad", None))
    out_specs = (P("chain", "quad", None), P("chain", None, None))
    return jax.shard_map(local, mesh=mesh, in_specs=in_specs, out_specs=out_specs, check_vma=False)
```

time: 95.2 us -> 85.3 us (0.90)
  blocking collectives: 0 us -> 35.7 us
  waiting for transfers between devices: 21.4 us -> 4.18 us
  starting transfers between devices: 31.9 us -> 16.6 us
  Pallas kernels: 34.4 us -> 20.8 us
  local copies, waits for them, and re-layouts: 4.11 us -> 6.22 us
  other arithmetic: 2.12 us -> 0.78 us
    all_to_all x0 -> x2, blocking collectives: none -> 35.7 us  [the longest x1 21.9 us: local(): h_all = lax.all_to_all(packed, 'quad', 0, 0, tiled=True)]
    all_to_all x3 -> x0, waiting for transfers between devices: 19.4 us -> none  [the longest x1 8.35 us: local(): p_all = lax.all_to_all(packed, 'quad', 0, 0, tiled=True)]
    all_to_all x3 -> x0, starting transfers between devices: 17.2 us -> none  [the longest x1 7.39 us: local(): parts = lax.all_to_all(parts, 'chain', 0, 0, tiled=True)]
    pallas_call x5, Pallas kernels: 34.4 us -> 20.8 us  [call(): pl.pallas_call(kernel, in_specs=specs, out_specs=[pl.BlockSpec(memory_spa...]
    ppermute x7, waiting for transfers between devices: 1.93 us -> 4.18 us  [ring(): return lax.ppermute(array, axis, [(i, (i + by) % n) for i in range(n)])]
    unnamed x10 -> x12, local copies, waits for them, and re-layouts: 3.21 us -> 5.32 us
    ppermute x7, starting transfers between devices: 14.7 us -> 16.6 us  [ring(): return lax.ppermute(array, axis, [(i, (i + by) % n) for i in range(n)])]
  transfers between devices with their start and end apart: 10 -> 7, of which waited for: 6 -> 4; matrix products, arithmetic and copies ran while one was open for 3% -> 2% of each run, Pallas kernels for 24% -> 10%
where the time goes in v1:
time: 85.3 us; the launch traced here: 84.9 us
  blocking collectives  35.7 us (42%)
  Pallas kernels  20.8 us (24%)
  starting transfers between devices  16.6 us (19%)
  local copies, waits for them, and re-layouts  6.22 us (7%)
  waiting for transfers between devices  4.18 us (5%)
    all_to_all x1, blocking collectives, local(): h_all = lax.all_to_all(packed, 'quad', 0, 0, tiled=True)  21.9 us
    pallas_call x5, Pallas kernels, call(): pl.pallas_call(kernel, in_specs=specs, out_specs=[pl.BlockSpec(memory_spa...  20.8 us
    ppermute x7, starting transfers between devices, ring(): return lax.ppermute(array, axis, [(i, (i + by) % n) for i in range(n)])  16.6 us
    all_to_all x1, blocking collectives, local(): parts = lax.all_to_all(parts, 'chain', 0, 0, tiled=True)  13.8 us
    unnamed x12, local copies, waits for them, and re-layouts  5.32 us
    ppermute x7, waiting for transfers between devices, ring(): return lax.ppermute(array, axis, [(i, (i + by) % n) for i in range(n)])  4.18 us
  transfers between devices with their start and end apart: 7, of which 4 were waited for; matrix products, arithmetic and copies ran while one was open for 2% of the time, Pallas kernels for 10%

profile of v1, /device:TPU:1, one launch (start us, length us, event | category | flops | bytes accessed | tf_op | source)
XLA Modules:
  0.0 84.9 jit_solution(10905887500211667843)
XLA Ops:
  0.6 2.6 %collective-permute-start.2 = (bf16[256,4096]{1,0:T(8,128)(2,1)}, bf16[256,4096]{1,0:T(8,128)(2,1)S(1)}, u32[]{:S(2)}, u32[]{:S(2)}) collective-permute-start(bf16[256,4096]{1,0:T(8,128)(2,1)} %bitcast.9), channel_id=1, source_target_pairs={{0,16},{16,32},{32,48},{48,64},{64,80},{80,96},{96,112},{112,0},{1... | collective-permute-start | bytes 6291464 | tf_op jit(solution)/shard_map/ppermute | solution.py:513
  3.2 0.9 %slice_bitcast_fusion = (bf16[1,4096]{1,0:T(2,128)(2,1)S(1)}, bf16[1,4096]{1,0:T(2,128)(2,1)S(1)}) fusion(bf16[1,256,4096]{2,1,0:T(8,128)(2,1)} %param.5), kind=kLoop, calls=%fused_computation.12 | loop fusion | bytes 32768 | tf_op jit(solution)/shard_map/slice | solution.py:543
  4.1 1.4 %collective-permute-start = (bf16[1,4096]{1,0:T(2,128)(2,1)S(1)}, bf16[1,4096]{1,0:T(2,128)(2,1)S(1)}, u32[]{:S(2)}, u32[]{:S(2)}) collective-permute-start(bf16[1,4096]{1,0:T(2,128)(2,1)S(1)} %get-tuple-element.23), channel_id=1, source_target_pairs={{0,1},{1,2},{2,3},{3,4},{4,5},{5,6},{6,7},{7,8},{8,9},{9,10},{10,1... | collective-permute-start | bytes 24584 | tf_op jit(solution)/shard_map/ppermute | solution.py:513
  5.5 5.0 %collective-permute-start.1 = (bf16[1,4096]{1,0:T(2,128)(2,1)S(1)}, bf16[1,4096]{1,0:T(2,128)(2,1)S(1)}, u32[]{:S(2)}, u32[]{:S(2)}) collective-permute-start(bf16[1,4096]{1,0:T(2,128)(2,1)S(1)} %get-tuple-element.22), channel_id=1, source_target_pairs={{0,15},{1,0},{2,1},{3,2},{4,3},{5,4},{6,5},{7,6},{8,7},{9,8},{10,9... | collective-permute-start | bytes 24584 | tf_op jit(solution)/shard_map/ppermute | solution.py:513
  10.5 0.7 fusion.2.turned_ref
  11.2 0.1 pad_add_fusion.pos_ref
  11.3 0.3 collective-permute-done.up_ref
  11.5 0.0 collective-permute-done.1.dn_ref
  11.5 0.0 copy-start
  11.5 1.6 %copy-done = bf16[1,256,4096]{2,1,0:T(8,128)(2,1)S(1)} copy-done((bf16[1,256,4096]{2,1,0:T(8,128)(2,1)S(1)}, bf16[1,256,4096]{2,1,0:T(8,128)(2,1)}, u32[]{:S(2)}) %copy-start) | copy-done | bytes 2097176
  13.1 0.0 copy-start.2
  13.1 1.4 %copy-done.2 = bf16[3200,256]{1,0:T(8,128)(2,1)S(1)} copy-done((bf16[3200,256]{1,0:T(8,128)(2,1)S(1)}, bf16[3200,256]{1,0:T(8,128)(2,1)}, u32[]{:S(2)}) %copy-start.2) | copy-done | bytes 1638424
  14.6 0.0 copy-start.5
  14.6 0.7 copy-done.5
  15.3 0.0 copy-start.1
  15.3 8.7 %stage0.1 = (f32[96,256]{1,0:T(8,128)S(1)}, f32[24,128]{1,0:T(8,128)S(1)}, f32[256,4096]{1,0:T(8,128)S(1)}, f32[256,4096]{1,0:T(8,128)S(1)}) custom-call(s32[2]{0:T(128)S(1)} %pad_add_fusion.pos_ref, bf16[256,4096]{1,0:T(8,128)(2,1)S(1)} %bitcast.10, bf16[1,4096]{1,0:T(2,128)(2,1)S(1)} %collective-permute-done.up_ref, ...), custom_call_target="tpu_custom_call" | custom-call | tf_op jit(solution)/shard_map/stage0/pallas_call | solution.py:526
  24.0 2.6 %collective-permute-done.2.prior_hbm = bf16[256,4096]{1,0:T(8,128)(2,1)S(1)} collective-permute-done((bf16[256,4096]{1,0:T(8,128)(2,1)}, bf16[256,4096]{1,0:T(8,128)(2,1)S(1)}, u32[]{:S(2)}, u32[]{:S(2)}) %collective-permute-start.2) | collective-permute-done | bytes 2097184 | tf_op jit(solution)/shard_map/ppermute | solution.py:513
  26.5 0.0 copy-done.1
  26.5 0.0 copy-start.3
  26.5 1.6 %copy-done.3 = bf16[256,4096]{1,0:T(8,128)(2,1)S(1)} copy-done((bf16[256,4096]{1,0:T(8,128)(2,1)S(1)}, bf16[256,4096]{1,0:T(8,128)(2,1)}, u32[]{:S(2)}) %copy-start.3) | copy-done | bytes 2097176
  28.1 3.5 %stage1.1 = bf16[16,128,256]{2,1,0:T(8,128)(2,1)S(1)} custom-call(s32[2]{0:T(128)S(1)} %pad_add_fusion.pos_ref, bf16[256,4096]{1,0:T(8,128)(2,1)S(1)} %bitcast.11, f32[256,4096]{1,0:T(8,128)S(1)} %get-tuple-element.12.xs, f32[256,4096]{1,0:T(8,128)S(1)} %get-tuple-element.13.ys, bf16[3200,256]{1,0:T(8,128)(2,1)S(1)} %copy-done.2, ...), custom_call_target="tpu_custom_call" | custom-call | tf_op jit(solution)/shard_map/stage1/pallas_call | solution.py:526
  31.7 21.9 %all_to_all.10.h_ref = bf16[16,128,256]{2,1,0:T(8,128)(2,1)S(1)} all-to-all(bf16[16,128,256]{2,1,0:T(8,128)(2,1)S(1)} %stage1.1), channel_id=1, replica_groups=mesh['chain'=8,'quad'=16] {'quad'}, dimensions={0} | all-to-all | bytes 2097152 | tf_op jit(solution)/shard_map/all_to_all | solution.py:565
  53.5 0.0 copy-start.4
  53.5 1.5 %solve_a.1 = (f32[128,128]{1,0:T(8,128)S(1)}, f32[64,128]{1,0:T(8,128)S(1)}) custom-call(bf16[16,128,256]{2,1,0:T(8,128)(2,1)S(1)} %all_to_all.10.h_ref), custom_call_target="tpu_custom_call" | custom-call | tf_op jit(solution)/shard_map/solve_a/pallas_call | solution.py:526
  55.0 4.9 %collective-permute-start.3 = (f32[128,128]{1,0:T(8,128)S(1)}, f32[128,128]{1,0:T(8,128)S(1)}, u32[]{:S(2)}, u32[]{:S(2)}) collective-permute-start(f32[128,128]{1,0:T(8,128)S(1)} %get-tuple-element.17.own_ref), channel_id=1, source_target_pairs={{0,16},{16,32},{32,48},{48,64},{64,80},{80,96},{96,112},{112,0},{1... | collective-permute-start | bytes 196616 | tf_op jit(solution)/shard_map/ppermute | solution.py:513
  59.9 0.0 collective-permute-start.4
  59.9 1.0 %collective-permute-start.5 = (f32[64,128]{1,0:T(8,128)S(1)}, f32[64,128]{1,0:T(8,128)S(1)}, u32[]{:S(2)}, u32[]{:S(2)}) collective-permute-start(f32[64,128]{1,0:T(8,128)S(1)} %get-tuple-element.18), channel_id=1, source_target_pairs={{0,32},{16,48},{32,64},{48,80},{64,96},{80,112},{96,0},{112,16},{1... | collective-permute-start | bytes 98312 | tf_op jit(solution)/shard_map/ppermute | solution.py:513
  60.9 1.7 %collective-permute-start.6 = (f32[64,128]{1,0:T(8,128)S(1)}, f32[64,128]{1,0:T(8,128)S(1)}, u32[]{:S(2)}, u32[]{:S(2)}) collective-permute-start(f32[64,128]{1,0:T(8,128)S(1)} %get-tuple-element.18), channel_id=1, source_target_pairs={{0,96},{16,112},{32,0},{48,16},{64,32},{80,48},{96,64},{112,80},{1... | collective-permute-start | bytes 98312 | tf_op jit(solution)/shard_map/ppermute | solution.py:513
  62.6 1.3 %collective-permute-done.5.prev2_ref = f32[64,128]{1,0:T(8,128)S(1)} collective-permute-done((f32[64,128]{1,0:T(8,128)S(1)}, f32[64,128]{1,0:T(8,128)S(1)}, u32[]{:S(2)}, u32[]{:S(2)}) %collective-permute-start.5) | collective-permute-done | bytes 32800 | tf_op jit(solution)/shard_map/ppermute | solution.py:513
  63.9 0.1 collective-permute-done.6.next2_ref
  64.0 0.0 collective-permute-done.3.prev_ref
  64.0 0.0 collective-permute-done.4.next_ref
  64.0 2.7 %solve_b.1 = f32[8,64,128]{2,1,0:T(8,128)S(1)} custom-call(s32[2]{0:T(128)S(1)} %pad_add_fusion.pos_ref, bf16[16,128,256]{2,1,0:T(8,128)(2,1)S(1)} %all_to_all.10.h_ref, f32[128,128]{1,0:T(8,128)S(1)} %get-tuple-element.17.own_ref, f32[128,128]{1,0:T(8,128)S(1)} %collective-permute-done.3.prev_ref, f32[128,128]{1,0:T(8,128)S(1)} %collective-permute-done.4.next_ref, ...), custom_call_target="tpu_custom_call" | custom-call | tf_op jit(solution)/shard_map/solve_b/pallas_call | solution.py:526
  66.7 13.8 %all_to_all.11.parts_ref = f32[8,64,128]{2,1,0:T(8,128)S(1)} all-to-all(f32[8,64,128]{2,1,0:T(8,128)S(1)} %solve_b.1), channel_id=1, replica_groups=mesh['chain'=8,'quad'=16] {'chain'}, dimensions={0} | all-to-all | bytes 524288 | tf_op jit(solution)/shard_map/all_to_all | solution.py:570
  80.5 0.0 copy-done.4
  80.5 4.4 %finish.1 = (bf16[256,4096]{1,0:T(8,128)(2,1)}, f32[64,128]{1,0:T(8,128)}) custom-call(s32[2]{0:T(128)S(1)} %pad_add_fusion.pos_ref, bf16[256,4096]{1,0:T(8,128)(2,1)S(1)} %bitcast.12, f32[256,4096]{1,0:T(8,128)S(1)} %get-tuple-element.12.xs, f32[256,4096]{1,0:T(8,128)S(1)} %get-tuple-element.13.ys, f32[8,64,128]{2,1,0:T(8,128)S(1)} %all_to_all.11.parts_ref, ...), custom_call_target="tpu_custom_call" | custom-call | tf_op jit(solution)/shard_map/finish/pallas_call | solution.py:526
  (2 shorter events, 0.0 us)
Async XLA Ops:
  0.6 25.9 %collective-permute-start.2 = (bf16[256,4096]{1,0:T(8,128)(2,1)}, bf16[256,4096]{1,0:T(8,128)(2,1)S(1)}, u32[]{:S(2)}, u32[]{:S(2)}) collective-permute-start(bf16[256,4096]{1,0:T(8,128)(2,1)} %bitcast.9), channel_id=1, source_target_pairs={{0,16},{16,32},{32,48},{48,64},{64,80},{80,96},{96,112},{112,0},{1... | collective-permute-start | bytes 6291464 | tf_op jit(solution)/shard_map/ppermute | solution.py:513
  4.1 7.4 %collective-permute-start = (bf16[1,4096]{1,0:T(2,128)(2,1)S(1)}, bf16[1,4096]{1,0:T(2,128)(2,1)S(1)}, u32[]{:S(2)}, u32[]{:S(2)}) collective-permute-start(bf16[1,4096]{1,0:T(2,128)(2,1)S(1)} %get-tuple-element.23), channel_id=1, source_target_pairs={{0,1},{1,2},{2,3},{3,4},{4,5},{5,6},{6,7},{7,8},{8,9},{9,10},{10,1... | collective-permute-start | bytes 24584 | tf_op jit(solution)/shard_map/ppermute | solution.py:513
  5.5 6.0 %collective-permute-start.1 = (bf16[1,4096]{1,0:T(2,128)(2,1)S(1)}, bf16[1,4096]{1,0:T(2,128)(2,1)S(1)}, u32[]{:S(2)}, u32[]{:S(2)}) collective-permute-start(bf16[1,4096]{1,0:T(2,128)(2,1)S(1)} %get-tuple-element.22), channel_id=1, source_target_pairs={{0,15},{1,0},{2,1},{3,2},{4,3},{5,4},{6,5},{7,6},{8,7},{9,8},{10,9... | collective-permute-start | bytes 24584 | tf_op jit(solution)/shard_map/ppermute | solution.py:513
  11.5 1.6 %copy-start = (bf16[1,256,4096]{2,1,0:T(8,128)(2,1)S(1)}, bf16[1,256,4096]{2,1,0:T(8,128)(2,1)}, u32[]{:S(2)}) copy-start(bf16[1,256,4096]{2,1,0:T(8,128)(2,1)} %param.5) | copy-start | bytes 6291460
  13.1 1.4 %copy-start.2 = (bf16[3200,256]{1,0:T(8,128)(2,1)S(1)}, bf16[3200,256]{1,0:T(8,128)(2,1)}, u32[]{:S(2)}) copy-start(bf16[3200,256]{1,0:T(8,128)(2,1)} %constant.34.clone.blob_ref) | copy-start | bytes 4915204
  14.6 0.7 copy-start.5
  15.3 11.3 %copy-start.1 = (bf16[1,256,4096]{2,1,0:T(8,128)(2,1)S(1)}, bf16[1,256,4096]{2,1,0:T(8,128)(2,1)}, u32[]{:S(2)}) copy-start(bf16[1,256,4096]{2,1,0:T(8,128)(2,1)} %param.5) | copy-start | bytes 6291460
  26.5 1.6 %copy-start.3 = (bf16[256,4096]{1,0:T(8,128)(2,1)S(1)}, bf16[256,4096]{1,0:T(8,128)(2,1)}, u32[]{:S(2)}) copy-start(bf16[256,4096]{1,0:T(8,128)(2,1)} %anchor_hbm.1) | copy-start | bytes 6291460
  53.5 27.0 %copy-start.4 = (f32[256,8]{1,0:T(8,128)S(1)}, f32[256,8]{1,0:T(8,128)}, u32[]{:S(2)}) copy-start(f32[256,8]{1,0:T(8,128)} %constant.36.clone.r8_hbm) | copy-start | bytes 24580
  55.0 9.0 %collective-permute-start.3 = (f32[128,128]{1,0:T(8,128)S(1)}, f32[128,128]{1,0:T(8,128)S(1)}, u32[]{:S(2)}, u32[]{:S(2)}) collective-permute-start(f32[128,128]{1,0:T(8,128)S(1)} %get-tuple-element.17.own_ref), channel_id=1, source_target_pairs={{0,16},{16,32},{32,48},{48,64},{64,80},{80,96},{96,112},{112,0},{1... | collective-permute-start | bytes 196616 | tf_op jit(solution)/shard_map/ppermute | solution.py:513
  59.9 4.0 %collective-permute-start.4 = (f32[128,128]{1,0:T(8,128)S(1)}, f32[128,128]{1,0:T(8,128)S(1)}, u32[]{:S(2)}, u32[]{:S(2)}) collective-permute-start(f32[128,128]{1,0:T(8,128)S(1)} %get-tuple-element.17.own_ref), channel_id=1, source_target_pairs={{0,112},{16,0},{32,16},{48,32},{64,48},{80,64},{96,80},{112,96},{1... | collective-permute-start | bytes 196616 | tf_op jit(solution)/shard_map/ppermute | solution.py:513
  59.9 4.0 %collective-permute-start.5 = (f32[64,128]{1,0:T(8,128)S(1)}, f32[64,128]{1,0:T(8,128)S(1)}, u32[]{:S(2)}, u32[]{:S(2)}) collective-permute-start(f32[64,128]{1,0:T(8,128)S(1)} %get-tuple-element.18), channel_id=1, source_target_pairs={{0,32},{16,48},{32,64},{48,80},{64,96},{80,112},{96,0},{112,16},{1... | collective-permute-start | bytes 98312 | tf_op jit(solution)/shard_map/ppermute | solution.py:513
  60.9 3.0 %collective-permute-start.6 = (f32[64,128]{1,0:T(8,128)S(1)}, f32[64,128]{1,0:T(8,128)S(1)}, u32[]{:S(2)}, u32[]{:S(2)}) collective-permute-start(f32[64,128]{1,0:T(8,128)S(1)} %get-tuple-element.18), channel_id=1, source_target_pairs={{0,96},{16,112},{32,0},{48,16},{64,32},{80,48},{96,64},{112,80},{1... | collective-permute-start | bytes 98312 | tf_op jit(solution)/shard_map/ppermute | solution.py:513

commit v2 on v1

--- a/solution.py
+++ b/solution.py
@@ -166,7 +166,9 @@
     return a[0:8] + a[8:16] + b[0:8]
 
 
-def stage0(pos_ref, m_ref, up_ref, dn_ref, blob_ref, edge_ref, h_ref, p_ref, xs, ys, fxx, fxy, fyy, mxh, mxl, myh, myl, zacc, lacc, l1_ref, sums):
+def stage0(pos_ref, m_ref, up_ref, dn_ref, blob_ref, edge_ref, anchor_hbm, h_ref, p_ref, xs, ys, anchor_ref, fetched, fxx, fxy, fyy, mxh, mxl, myh, myl, zacc, lacc, l1_ref, sums):
+    bring = pltpu.make_async_copy(anchor_hbm, anchor_ref, fetched)
+    bring.start()
     sums[...] = jnp.zeros((8, 128), F32)
 
     def body(step, carry):
@@ -208,6 +210,7 @@
         return carry
 
     lax.fori_loop(0, STEPS, body, 0)
+    bring.wait()
     l1 = l1_ref[...]
     col = lax.broadcasted_iota(jnp.int32, l1.shape, 1)
     after = jnp.where(col < COLS - 1, pltpu.roll(l1, COLS - 1, 1), 0.0)
@@ -226,24 +229,11 @@
     p_ref[16:24, :] = sums[...]
 
 
-def cross_part(pos_ref, m_ref, xs, ys, blob_ref, anchor_hbm, prior_hbm, fxh, fxl, fyh, fyl, f_ref, fetched, lacc, sums):
-    def fetch(i, from_hbm):
-        return pltpu.make_async_copy(from_hbm.at[:, tile(i)], f_ref.at[:, tile(i)], fetched.at[i])
-
-    for i in range(STEPS):
-
-        @pl.when(pos_ref[0] == 0)
-        def _():
-            fetch(i, anchor_hbm).start()
-
-        @pl.when(pos_ref[0] > 0)
-        def _():
-            fetch(i, prior_hbm).start()
-
+def cross_part(pos_ref, m_ref, xs, ys, blob_ref, anchor_ref, prior_ref, fxh, fxl, fyh, fyl, lacc, sums):
+    first = pos_ref[0] == 0
     sums[...] = jnp.zeros((8, 128), F32)
 
     def body(step, carry):
-        fetch(step, prior_hbm).wait()
         lin = blob_ref[LIN : LIN + 16, :]
         cross = jnp.zeros((8, 256), F32)
         whole_sum = jnp.zeros((8, 256), F32)
@@ -254,7 +244,7 @@
             for c in range(ROWS // CHUNK):
                 rows = pl.ds(CHUNK * c, CHUNK)
                 m, x, y = m_ref[rows, from_m].astype(F32), xs[rows, from_m], ys[rows, from_m]
-                f = f_ref[rows, from_m].astype(F32)
+                f = jnp.where(first, anchor_ref[rows, from_m].astype(F32), prior_ref[rows, from_m].astype(F32))
                 fxh[rows, at], fxl[rows, at] = hi_lo(f * x)
                 fyh[rows, at], fyl[rows, at] = hi_lo(f * y)
                 cross = cross + fold8(f * m)
@@ -279,9 +269,9 @@
     return lax.broadcasted_iota(jnp.int32, shape, 0) % 8
 
 
-def stage1(pos_ref, m_ref, xs, ys, blob_ref, anchor_hbm, prior_hbm, h_ref, p_ref, out_ref, *scratch):
+def stage1(pos_ref, m_ref, xs, ys, blob_ref, anchor_ref, prior_ref, h_ref, p_ref, out_ref, *scratch):
     sums = scratch[-1]
-    part = cross_part(pos_ref, m_ref, xs, ys, blob_ref, anchor_hbm, prior_hbm, *scratch)
+    part = cross_part(pos_ref, m_ref, xs, ys, blob_ref, anchor_ref, prior_ref, *scratch)
     row = rows8((8, 256))
     lane = lax.broadcasted_iota(jnp.int32, (8, 256), 1)
     last = jnp.zeros((8, 256), F32)
@@ -304,8 +294,7 @@
     for v in (part, p_ref[0:8, :], p_ref[8:16, :]):
         groups.append(jnp.concatenate([v, v - v.astype(BF).astype(F32)], axis=1))
     packed = jnp.concatenate(groups, axis=0).astype(BF)
-    for t in range(16):
-        out_ref[t] = packed
+    out_ref[...] = packed
 
 
 def shifted(a, by, axis):
@@ -314,26 +303,24 @@
     return a if by == 0 else pltpu.roll(a, by, axis)
 
 
-def unpack(h_ref):
-    out = [([], []) for _ in range(16)]
-    for q in range(16):
-        for t in range(8):
-            both = h_ref[q, 16 * t : 16 * t + 16, :].astype(F32)
-            out[2 * t][q % 2].append(both[0:8])
-            out[2 * t + 1][q % 2].append(both[8:16])
-    return [[jnp.concatenate(v, axis=0) for v in pair] for pair in out]
-
-
 def stacked(even, odd):
     pad = jnp.zeros((8, even.shape[1]), F32)
     return jnp.concatenate([even, pad], axis=0) + pltpu.roll(jnp.concatenate([odd, pad], axis=0), 4, 0)
 
 
-def build_operator(groups, a1, a2):
-    lane = lax.broadcasted_iota(jnp.int32, (EXT, 128), 1)
-    low = lane < 64
-    row = rows8((64, 256))
-    pad = jnp.zeros((64, 128), F32)
+def merge(pos_ref, near0, near1, near2, near3, out_ref, all_ref):
+    y = pos_ref[1] % 4
+    for e, ref in enumerate((near0, near1, near2, near3)):
+        all_ref[(y + 4 - e) % 4] = ref[...]
+    groups = [([], []) for _ in range(16)]
+    for q in range(4):
+        for t in range(8):
+            both = all_ref[q, 16 * t : 16 * t + 16, :].astype(F32)
+            groups[2 * t][q % 2].append(both[0:8])
+            groups[2 * t + 1][q % 2].append(both[8:16])
+    groups = [[jnp.concatenate(v, axis=0) for v in pair] for pair in groups]
+    row = rows8((16, 256))
+    pad = jnp.zeros((16, 128), F32)
 
     def piece(c, dj, side):
         a, b, d, last, rest = [groups[g][side] for g in (3 * c, 3 * c + 1, 3 * c + 2, 9, 10 + c)]
@@ -343,13 +330,76 @@
             return jnp.where(row < 7, b, 0.0) + jnp.concatenate([rest[:, 128:256], pad], axis=1)
         if dj == 2:
             return jnp.where(row < 6, d, 0.0)
-        e = jnp.where(row == 4, pltpu.roll(b, 61, 0), jnp.where(row > 1, pltpu.roll(d, 60, 0), shifted(last, -2 * c, 0)))
+        e = jnp.where(row == 4, pltpu.roll(b, 13, 0), jnp.where(row > 1, pltpu.roll(d, 12, 0), shifted(last, -2 * c, 0)))
         return jnp.where(row < 5, e, 0.0)
 
+    items, lows = [], []
+    for c in range(3):
+        four = [stacked(piece(c, dj, 0), piece(c, dj, 1)) for dj in range(4)]
+        items += four
+        lows.append(jnp.concatenate([v[:, 0:128] - v[:, 0:128].astype(BF).astype(F32) for v in four[0:2]], axis=1))
+    last = groups[9][0] + groups[9][1]
+    lane = lax.broadcasted_iota(jnp.int32, (16, 256), 1)
+    here = (row == 6) & (lane < 12)
+    row24 = lax.broadcasted_iota(jnp.int32, (24, 256), 0)
+    lane24 = lax.broadcasted_iota(jnp.int32, (24, 256), 1)
+    for t in range(4):
+        rest = total(jnp.where(here & (lane % 4 == t), last, 0.0))
+        for u in range(3):
+            part = rest.astype(BF).astype(F32)
+            rest = rest - part
+            items[3] = items[3] + jnp.where((row24 == 19) & (lane24 == 4 * u + t), part, 0.0)
+    items += lows
+    for g in (13, 14, 15):
+        even, odd = [v[:, 0:128] + v[:, 128:256] for v in groups[g]]
+        v = stacked(even, odd)
+        items.append(jnp.concatenate([v, v - v.astype(BF).astype(F32)], axis=1))
+    room = jnp.zeros((16, 256), F32)
+    pairs = []
+    for p in range(9):
+        a, b = [jnp.concatenate([v, room], axis=0) for v in items[2 * p : 2 * p + 2]]
+        pairs.append(a + pltpu.roll(b, 20, 0))
+    out_ref[...] = jnp.concatenate(pairs, axis=0).astype(BF)
+
+
+def unpack(pos_ref, far, all_ref):
+    z = pos_ref[1] // 4
+    for d in range(4):
+        all_ref[(z + 4 - d) % 4] = far[d][...]
+    blocks = [all_ref[t].astype(F32) for t in range(4)]
+    row = lax.broadcasted_iota(jnp.int32, (8, 256), 0)
+    lane = lax.broadcasted_iota(jnp.int32, (8, 256), 1)
+    eight = jnp.zeros((8, 256), F32)
+    out = []
+    sums = None
+    for i in range(18):
+        body, tails = [], [eight, eight]
+        for t in range(4):
+            full = blocks[t][40 * (i // 2) : 40 * (i // 2) + 40]
+            if i % 2:
+                full = pltpu.roll(full, 20, 0)
+            body.append(full[0:16])
+            tail = full[16:24]
+            if i == 3:
+                sums = tail if sums is None else sums + tail
+            tails += [jnp.where(row < (3 if i == 3 else 4), tail, 0.0), eight]
+        out.append(jnp.concatenate(body + [eight], axis=0) + jnp.concatenate(tails[:-1], axis=0))
+    here = (row == 3) & (lane < 12)
+    return out, [total(jnp.where(here & (lane % 4 == t), sums, 0.0)) for t in range(4)]
+
+
+def build_operator(items, a1, a2):
+    lane = lax.broadcasted_iota(jnp.int32, (EXT, 128), 1)
+    low = lane < 64
     for dj in range(4):
-        grid = [stacked(piece(c, dj, 0), piece(c, dj, 1)) for c in range(3)]
         for pair in range(2):
-            xx, xy, yy = [g[:, 128 * pair : 128 * pair + 128] for g in grid]
+            three = []
+            for c in range(3):
+                v = items[4 * c + dj][:, 128 * pair : 128 * pair + 128]
+                if pair == 0 and dj < 2:
+                    v = v + items[12 + c][:, 128 * dj : 128 * dj + 128]
+                three.append(v)
+            xx, xy, yy = three
             xx_s, xy_s, yy_s = [pltpu.roll(v, 64, 1) for v in (xx, xy, yy)]
             for odd in range(2):
                 di = 2 * pair + odd
@@ -389,18 +439,10 @@
     return jnp.sum(jnp.sum(a, axis=0, keepdims=True), axis=1, keepdims=True)
 
 
-def fields(groups):
+def fields(items):
     row = lax.broadcasted_iota(jnp.int32, (EXT, 128), 0)
     valid = (row >= 2) & (row < 66)
-    grads = []
-    for g in (13, 14, 15):
-        even, odd = [v[:, 0:128] + v[:, 128:256] for v in groups[g]]
-        grads.append(jnp.where(valid, stacked(even, odd), 0.0))
-    last = (groups[9][0] + groups[9][1])[:, 0:128]
-    lane = lax.broadcasted_iota(jnp.int32, (64, 128), 1)
-    here = (rows8((64, 128)) == 6) & (lane < 12)
-    sums = [total(jnp.where(here & (lane % 4 == t), last, 0.0)) for t in range(4)]
-    return valid, grads, sums
+    return valid, [jnp.where(valid, v[:, 0:128] + v[:, 128:256], 0.0) for v in items[15:18]]
 
 
 def narrow(a):
@@ -432,10 +474,10 @@
     return g / jnp.sqrt(total(g * g) / 8192.0 + EPS)
 
 
-def solve_a(h_ref, out_ref, lead_ref, a1, a2):
-    groups = unpack(h_ref)
-    build_operator(groups, a1, a2)
-    valid, grads, sums = fields(groups)
+def solve_a(pos_ref, far0, far1, far2, far3, out_ref, lead_ref, a1, a2, all_ref):
+    items, sums = unpack(pos_ref, (far0, far1, far2, far3), all_ref)
+    build_operator(items, a1, a2)
+    valid, grads = fields(items)
     c = RATE * direction(valid, grads, sums, None, None)
     d = direction(valid, grads, sums, c, apply_operator(a1, a2, c))
     lead = narrow(c)
@@ -444,11 +486,11 @@
     out_ref[GRID : 2 * GRID, :] = narrow(d)
 
 
-def solve_b(pos_ref, h_ref, own_ref, prev_ref, next_ref, prev2_ref, next2_ref, out_ref, a1, a2):
+def solve_b(pos_ref, far0, far1, far2, far3, own_ref, prev_ref, next_ref, prev2_ref, next2_ref, out_ref, a1, a2, all_ref):
     k = pos_ref[0]
-    groups = unpack(h_ref)
-    build_operator(groups, a1, a2)
-    valid, grads, sums = fields(groups)
+    items, sums = unpack(pos_ref, (far0, far1, far2, far3), all_ref)
+    build_operator(items, a1, a2)
+    valid, grads = fields(items)
 
     def lap(a, b, c):
         return a - 2.0 * b + c
@@ -508,6 +550,14 @@
         copy(step).wait()
 
 
+def around_four(array, stride, by):
+    def to(q):
+        here = q // stride % 4
+        return q + stride * ((here + by) % 4 - here)
+
+    return lax.ppermute(array, "quad", [(q, to(q)) for q in range(16)])
+
+
 def ring(array, axis, by):
     n = lax.axis_size(axis)
     return lax.ppermute(array, axis, [(i, (i + by) % n) for i in range(n)])
@@ -544,29 +594,31 @@
     turned = col_table()
     shape = jax.ShapeDtypeStruct
     slope = shape((ROWS, COLS), F32)
-    h, p, xs, ys = call(
+    h, p, xs, ys, before = call(
         stage0,
         "stage0",
-        (pos, strip, up, dn, blob, edge),
-        [shape((96, 256), F32), shape((24, 128), F32), slope, slope],
-        [FIELD] * 7 + [pltpu.VMEM((96 * STEPS, 128), F32), pltpu.VMEM((24 * STEPS, 128), F32), pltpu.VMEM((8, COLS), F32), SMALL],
+        (pos, strip, up, dn, blob, edge, anchor),
+        [shape((96, 256), F32), shape((24, 128), F32), slope, slope, shape((ROWS, COLS), BF)],
+        [pltpu.SemaphoreType.DMA] + [FIELD] * 7 + [pltpu.VMEM((96 * STEPS, 128), F32), pltpu.VMEM((24 * STEPS, 128), F32), pltpu.VMEM((8, COLS), F32), SMALL],
         24,
+        hbm_in=(6,),
     )
     (packed,) = call(
         stage1,
         "stage1",
-        (pos, strip, xs, ys, blob, anchor, prior, h, p),
-        [shape((16, 128, 256), BF)],
-        [FIELD] * 4 + [pltpu.VMEM((ROWS, COLS), BF), pltpu.SemaphoreType.DMA((STEPS,)), pltpu.VMEM((16 * STEPS, 128), F32), SMALL],
+        (pos, strip, xs, ys, blob, before, prior, h, p),
+        [shape((128, 256), BF)],
+        [FIELD] * 4 + [pltpu.VMEM((16 * STEPS, 128), F32), SMALL],
         20,
-        hbm_in=(5, 6),
     )
     packed, turned = lax.optimization_barrier((packed, turned))
-    h_all = lax.all_to_all(packed, "quad", 0, 0, tiled=True)
-    operator = [pltpu.VMEM((28, EXT, 128), F32)] * 2
-    first, lead = call(solve_a, "solve_a", (h_all,), [shape((2 * GRID, 128), F32), shape((GRID, 128), F32)], operator, 12)
+    four = [packed] + [around_four(packed, 1, d) for d in (1, 2, 3)]
+    (near,) = call(merge, "merge", (pos, *four), [shape((360, 256), BF)], [pltpu.VMEM((4, 128, 256), BF)], 12)
+    far = [near] + [around_four(near, 4, d) for d in (1, 2, 3)]
+    operator = [pltpu.VMEM((28, EXT, 128), F32)] * 2 + [pltpu.VMEM((4, 360, 256), BF)]
+    first, lead = call(solve_a, "solve_a", (pos, *far), [shape((2 * GRID, 128), F32), shape((GRID, 128), F32)], operator, 12)
     around = [ring(first, "chain", 1), ring(first, "chain", -1), ring(lead, "chain", 2), ring(lead, "chain", -2)]
-    (parts,) = call(solve_b, "solve_b", (pos, h_all, first, *around), [shape((8, GRID, 128), F32)], operator, 12)
+    (parts,) = call(solve_b, "solve_b", (pos, *far, first, *around), [shape((8, GRID, 128), F32)], operator, 12)
     parts = lax.all_to_all(parts, "chain", 0, 0, tiled=True)
     registered, accumulated = call(
         finish,

time: 85.3 us -> 79.8 us (0.936)
  blocking collectives: 35.7 us -> 11.4 us
  starting transfers between devices: 16.6 us -> 28.6 us
  waiting for transfers between devices: 4.18 us -> 8.94 us
  Pallas kernels: 20.8 us -> 22.7 us
    all_to_all x1 -> x0, blocking collectives: 21.9 us -> none  [local(): h_all = lax.all_to_all(packed, 'quad', 0, 0, tiled=True)]
    ppermute x0 -> x6, starting transfers between devices: none -> 10.7 us  [around_four(): return lax.ppermute(array, 'quad', [(q, to(q)) for q in range(16)])]
    ppermute x0 -> x6, waiting for transfers between devices: none -> 6.61 us  [around_four(): return lax.ppermute(array, 'quad', [(q, to(q)) for q in range(16)])]
    all_to_all x1, blocking collectives: 13.8 us -> 11.4 us  [local(): parts = lax.all_to_all(parts, 'chain', 0, 0, tiled=True)]
    pallas_call x5 -> x6, Pallas kernels: 20.8 us -> 22.7 us  [call(): pl.pallas_call(kernel, in_specs=specs, out_specs=[pl.BlockSpec(memory_spa...]
    ppermute x7, waiting for transfers between devices: 4.18 us -> 2.33 us  [ring(): return lax.ppermute(array, axis, [(i, (i + by) % n) for i in range(n)])]
    ppermute x7, starting transfers between devices: 16.6 us -> 17.9 us  [ring(): return lax.ppermute(array, axis, [(i, (i + by) % n) for i in range(n)])]
  transfers between devices with their start and end apart: 7 -> 13, of which waited for: 4 -> 7; matrix products, arithmetic and copies ran while one was open for 2% -> 2% of each run, Pallas kernels for 10% -> 11%
where the time goes in v2:
time: 79.8 us; the launch traced here: 79.4 us
  starting transfers between devices  28.6 us (36%)
  Pallas kernels  22.7 us (28%)
  blocking collectives  11.4 us (14%)
  waiting for transfers between devices  8.94 us (11%)
  local copies, waits for them, and re-layouts  6.22 us (8%)
    pallas_call x6, Pallas kernels, call(): pl.pallas_call(kernel, in_specs=specs, out_specs=[pl.BlockSpec(memory_spa...  22.7 us
    ppermute x7, starting transfers between devices, ring(): return lax.ppermute(array, axis, [(i, (i + by) % n) for i in range(n)])  17.9 us
    all_to_all x1, blocking collectives, local(): parts = lax.all_to_all(parts, 'chain', 0, 0, tiled=True)  11.4 us
    ppermute x6, starting transfers between devices, around_four(): return lax.ppermute(array, 'quad', [(q, to(q)) for q in range(16)])  10.7 us
    ppermute x6, waiting for transfers between devices, around_four(): return lax.ppermute(array, 'quad', [(q, to(q)) for q in range(16)])  6.61 us
    unnamed x12, local copies, waits for them, and re-layouts  5.32 us
    ppermute x7, waiting for transfers between devices, ring(): return lax.ppermute(array, axis, [(i, (i + by) % n) for i in range(n)])  2.33 us
  transfers between devices with their start and end apart: 13, of which 7 were waited for; matrix products, arithmetic and copies ran while one was open for 2% of the time, Pallas kernels for 11%

profile of v2, /device:TPU:1, one launch (start us, length us, event | category | flops | bytes accessed | tf_op | source)
XLA Modules:
  0.0 79.4 jit_solution(5225393873569252978)
XLA Ops:
  0.6 2.6 %collective-permute-start.2 = (bf16[256,4096]{1,0:T(8,128)(2,1)}, bf16[256,4096]{1,0:T(8,128)(2,1)S(1)}, u32[]{:S(2)}, u32[]{:S(2)}) collective-permute-start(bf16[256,4096]{1,0:T(8,128)(2,1)} %bitcast.9), channel_id=1, source_target_pairs={{0,16},{16,32},{32,48},{48,64},{64,80},{80,96},{96,112},{112,0},{1... | collective-permute-start | bytes 6291464 | tf_op jit(solution)/shard_map/ppermute | solution.py:563
  3.2 0.9 %slice_bitcast_fusion = (bf16[1,4096]{1,0:T(2,128)(2,1)S(1)}, bf16[1,4096]{1,0:T(2,128)(2,1)S(1)}) fusion(bf16[1,256,4096]{2,1,0:T(8,128)(2,1)} %param.5), kind=kLoop, calls=%fused_computation.12 | loop fusion | bytes 32768 | tf_op jit(solution)/shard_map/slice | solution.py:593
  4.1 1.4 %collective-permute-start = (bf16[1,4096]{1,0:T(2,128)(2,1)S(1)}, bf16[1,4096]{1,0:T(2,128)(2,1)S(1)}, u32[]{:S(2)}, u32[]{:S(2)}) collective-permute-start(bf16[1,4096]{1,0:T(2,128)(2,1)S(1)} %get-tuple-element.25), channel_id=1, source_target_pairs={{0,1},{1,2},{2,3},{3,4},{4,5},{5,6},{6,7},{7,8},{8,9},{9,10},{10,1... | collective-permute-start | bytes 24584 | tf_op jit(solution)/shard_map/ppermute | solution.py:563
  5.5 5.0 %collective-permute-start.1 = (bf16[1,4096]{1,0:T(2,128)(2,1)S(1)}, bf16[1,4096]{1,0:T(2,128)(2,1)S(1)}, u32[]{:S(2)}, u32[]{:S(2)}) collective-permute-start(bf16[1,4096]{1,0:T(2,128)(2,1)S(1)} %get-tuple-element.24), channel_id=1, source_target_pairs={{0,15},{1,0},{2,1},{3,2},{4,3},{5,4},{6,5},{7,6},{8,7},{9,8},{10,9... | collective-permute-start | bytes 24584 | tf_op jit(solution)/shard_map/ppermute | solution.py:563
  10.5 0.7 fusion.2.turned_ref
  11.2 0.1 pad_add_fusion.pos_ref
  11.3 0.3 collective-permute-done.up_ref
  11.5 0.0 collective-permute-done.1.dn_ref
  11.5 0.0 copy-start
  11.5 1.6 %copy-done = bf16[1,256,4096]{2,1,0:T(8,128)(2,1)S(1)} copy-done((bf16[1,256,4096]{2,1,0:T(8,128)(2,1)S(1)}, bf16[1,256,4096]{2,1,0:T(8,128)(2,1)}, u32[]{:S(2)}) %copy-start) | copy-done | bytes 2097176
  13.1 0.0 copy-start.2
  13.1 1.4 %copy-done.2 = bf16[3200,256]{1,0:T(8,128)(2,1)S(1)} copy-done((bf16[3200,256]{1,0:T(8,128)(2,1)S(1)}, bf16[3200,256]{1,0:T(8,128)(2,1)}, u32[]{:S(2)}) %copy-start.2) | copy-done | bytes 1638424
  14.6 0.0 copy-start.3
  14.6 1.6 %copy-done.3 = bf16[256,4096]{1,0:T(8,128)(2,1)S(1)} copy-done((bf16[256,4096]{1,0:T(8,128)(2,1)S(1)}, bf16[256,4096]{1,0:T(8,128)(2,1)}, u32[]{:S(2)}) %copy-start.3) | copy-done | bytes 2097176
  16.2 0.0 copy-start.5
  16.2 0.7 copy-done.5
  16.9 0.0 copy-start.1
  16.9 9.0 %stage0.1 = (f32[96,256]{1,0:T(8,128)S(1)}, f32[24,128]{1,0:T(8,128)S(1)}, f32[256,4096]{1,0:T(8,128)S(1)}, f32[256,4096]{1,0:T(8,128)S(1)}, bf16[256,4096]{1,0:T(8,128)(2,1)S(1)}) custom-call(s32[2]{0:T(128)S(1)} %pad_add_fusion.pos_ref, bf16[256,4096]{1,0:T(8,128)(2,1)S(1)} %bitcast.10, bf16[1,4096]{1,0:T(2,128)(2,1)S(1)} %collective-permute-done.up_ref, ...), custom_call_target="tpu_custom_call" | custom-call | tf_op jit(solution)/shard_map/stage0/pallas_call | solution.py:576
  25.8 0.7 collective-permute-done.2.prior_ref
  26.5 0.0 copy-done.1
  26.5 4.0 %stage1.1.near0 = bf16[128,256]{1,0:T(8,128)(2,1)S(1)} custom-call(s32[2]{0:T(128)S(1)} %pad_add_fusion.pos_ref, bf16[256,4096]{1,0:T(8,128)(2,1)S(1)} %bitcast.11, f32[256,4096]{1,0:T(8,128)S(1)} %get-tuple-element.13.xs, f32[256,4096]{1,0:T(8,128)S(1)} %get-tuple-element.14.ys, bf16[3200,256]{1,0:T(8,128)(2,1)S(1)} %copy-done.2, ...), custom_call_target="tpu_custom_call" | custom-call | tf_op jit(solution)/shard_map/stage1/pallas_call | solution.py:576
  30.5 0.0 copy-start.4
  30.5 1.3 %collective-permute-start.3 = (bf16[128,256]{1,0:T(8,128)(2,1)S(1)}, bf16[128,256]{1,0:T(8,128)(2,1)S(1)}, u32[]{:S(2)}, u32[]{:S(2)}) collective-permute-start(bf16[128,256]{1,0:T(8,128)(2,1)S(1)} %stage1.1.near0), channel_id=1, source_target_pairs={{0,1},{1,2},{2,3},{3,0},{4,5},{5,6},{6,7},{7,4},{8,9},{9,10},{10,1... | collective-permute-start | bytes 196616 | tf_op jit(solution)/shard_map/ppermute | solution.py:558
  31.8 2.6 %collective-permute-start.4 = (bf16[128,256]{1,0:T(8,128)(2,1)S(1)}, bf16[128,256]{1,0:T(8,128)(2,1)S(1)}, u32[]{:S(2)}, u32[]{:S(2)}) collective-permute-start(bf16[128,256]{1,0:T(8,128)(2,1)S(1)} %stage1.1.near0), channel_id=1, source_target_pairs={{0,2},{1,3},{2,0},{3,1},{4,6},{5,7},{6,4},{7,5},{8,10},{9,11},{10,... | collective-permute-start | bytes 196616 | tf_op jit(solution)/shard_map/ppermute | solution.py:558
  34.4 1.1 %collective-permute-start.5 = (bf16[128,256]{1,0:T(8,128)(2,1)S(1)}, bf16[128,256]{1,0:T(8,128)(2,1)S(1)}, u32[]{:S(2)}, u32[]{:S(2)}) collective-permute-start(bf16[128,256]{1,0:T(8,128)(2,1)S(1)} %stage1.1.near0), channel_id=1, source_target_pairs={{0,3},{1,0},{2,1},{3,2},{4,7},{5,4},{6,5},{7,6},{8,11},{9,8},{10,9... | collective-permute-start | bytes 196616 | tf_op jit(solution)/shard_map/ppermute | solution.py:558
  35.5 0.0 collective-permute-done.3.near1
  35.5 1.3 %collective-permute-done.4.near2 = bf16[128,256]{1,0:T(8,128)(2,1)S(1)} collective-permute-done((bf16[128,256]{1,0:T(8,128)(2,1)S(1)}, bf16[128,256]{1,0:T(8,128)(2,1)S(1)}, u32[]{:S(2)}, u32[]{:S(2)}) %collective-permute-start.4) | collective-permute-done | bytes 65568 | tf_op jit(solution)/shard_map/ppermute | solution.py:558
  36.8 1.1 %collective-permute-done.5.near3 = bf16[128,256]{1,0:T(8,128)(2,1)S(1)} collective-permute-done((bf16[128,256]{1,0:T(8,128)(2,1)S(1)}, bf16[128,256]{1,0:T(8,128)(2,1)S(1)}, u32[]{:S(2)}, u32[]{:S(2)}) %collective-permute-start.5) | collective-permute-done | bytes 65568 | tf_op jit(solution)/shard_map/ppermute | solution.py:558
  37.9 0.7 merge.1.far0
  38.6 1.7 %collective-permute-start.6 = (bf16[360,256]{1,0:T(8,128)(2,1)S(1)}, bf16[360,256]{1,0:T(8,128)(2,1)S(1)}, u32[]{:S(2)}, u32[]{:S(2)}) collective-permute-start(bf16[360,256]{1,0:T(8,128)(2,1)S(1)} %merge.1.far0), channel_id=1, source_target_pairs={{0,4},{1,5},{2,6},{3,7},{4,8},{5,9},{6,10},{7,11},{8,12},{9,13},{1... | collective-permute-start | bytes 552968 | tf_op jit(solution)/shard_map/ppermute | solution.py:558
  40.3 3.3 %collective-permute-start.7 = (bf16[360,256]{1,0:T(8,128)(2,1)S(1)}, bf16[360,256]{1,0:T(8,128)(2,1)S(1)}, u32[]{:S(2)}, u32[]{:S(2)}) collective-permute-start(bf16[360,256]{1,0:T(8,128)(2,1)S(1)} %merge.1.far0), channel_id=1, source_target_pairs={{0,8},{1,9},{2,10},{3,11},{4,12},{5,13},{6,14},{7,15},{8,0},{9,1},... | collective-permute-start | bytes 552968 | tf_op jit(solution)/shard_map/ppermute | solution.py:558
  43.6 0.7 collective-permute-start.8
  44.3 1.0 %collective-permute-done.6.far1 = bf16[360,256]{1,0:T(8,128)(2,1)S(1)} collective-permute-done((bf16[360,256]{1,0:T(8,128)(2,1)S(1)}, bf16[360,256]{1,0:T(8,128)(2,1)S(1)}, u32[]{:S(2)}, u32[]{:S(2)}) %collective-permute-start.6) | collective-permute-done | bytes 184352 | tf_op jit(solution)/shard_map/ppermute | solution.py:558
  45.3 3.2 %collective-permute-done.7.far2 = bf16[360,256]{1,0:T(8,128)(2,1)S(1)} collective-permute-done((bf16[360,256]{1,0:T(8,128)(2,1)S(1)}, bf16[360,256]{1,0:T(8,128)(2,1)S(1)}, u32[]{:S(2)}, u32[]{:S(2)}) %collective-permute-start.7) | collective-permute-done | bytes 184352 | tf_op jit(solution)/shard_map/ppermute | solution.py:558
  48.6 0.0 collective-permute-done.8.far3
  48.6 2.0 %solve_a.1 = (f32[128,128]{1,0:T(8,128)S(1)}, f32[64,128]{1,0:T(8,128)S(1)}) custom-call(s32[2]{0:T(128)S(1)} %pad_add_fusion.pos_ref, bf16[360,256]{1,0:T(8,128)(2,1)S(1)} %merge.1.far0, bf16[360,256]{1,0:T(8,128)(2,1)S(1)} %collective-permute-done.6.far1, bf16[360,256]{1,0:T(8,128)(2,1)S(1)} %collective-permute-done.7.far2, ...), custom_call_target="tpu_custom_call" | custom-call | tf_op jit(solution)/shard_map/solve_a/pallas_call | solution.py:576
  50.6 5.0 %collective-permute-start.10 = (f32[128,128]{1,0:T(8,128)S(1)}, f32[128,128]{1,0:T(8,128)S(1)}, u32[]{:S(2)}, u32[]{:S(2)}) collective-permute-start(f32[128,128]{1,0:T(8,128)S(1)} %get-tuple-element.19.own_ref), channel_id=1, source_target_pairs={{0,112},{16,0},{32,16},{48,32},{64,48},{80,64},{96,80},{112,96},{1... | collective-permute-start | bytes 196616 | tf_op jit(solution)/shard_map/ppermute | solution.py:563
  55.6 1.3 %collective-permute-start.9 = (f32[128,128]{1,0:T(8,128)S(1)}, f32[128,128]{1,0:T(8,128)S(1)}, u32[]{:S(2)}, u32[]{:S(2)}) collective-permute-start(f32[128,128]{1,0:T(8,128)S(1)} %get-tuple-element.19.own_ref), channel_id=1, source_target_pairs={{0,16},{16,32},{32,48},{48,64},{64,80},{80,96},{96,112},{112,0},{1... | collective-permute-start | bytes 196616 | tf_op jit(solution)/shard_map/ppermute | solution.py:563
  56.9 0.9 %collective-permute-start.11 = (f32[64,128]{1,0:T(8,128)S(1)}, f32[64,128]{1,0:T(8,128)S(1)}, u32[]{:S(2)}, u32[]{:S(2)}) collective-permute-start(f32[64,128]{1,0:T(8,128)S(1)} %get-tuple-element.20), channel_id=1, source_target_pairs={{0,32},{16,48},{32,64},{48,80},{64,96},{80,112},{96,0},{112,16},{1... | collective-permute-start | bytes 98312 | tf_op jit(solution)/shard_map/ppermute | solution.py:563
  57.8 1.8 %collective-permute-start.12 = (f32[64,128]{1,0:T(8,128)S(1)}, f32[64,128]{1,0:T(8,128)S(1)}, u32[]{:S(2)}, u32[]{:S(2)}) collective-permute-start(f32[64,128]{1,0:T(8,128)S(1)} %get-tuple-element.20), channel_id=1, source_target_pairs={{0,96},{16,112},{32,0},{48,16},{64,32},{80,48},{96,64},{112,80},{1... | collective-permute-start | bytes 98312 | tf_op jit(solution)/shard_map/ppermute | solution.py:563
  59.6 1.4 %collective-permute-done.11.prev2_ref = f32[64,128]{1,0:T(8,128)S(1)} collective-permute-done((f32[64,128]{1,0:T(8,128)S(1)}, f32[64,128]{1,0:T(8,128)S(1)}, u32[]{:S(2)}, u32[]{:S(2)}) %collective-permute-start.11) | collective-permute-done | bytes 32800 | tf_op jit(solution)/shard_map/ppermute | solution.py:563
  60.9 0.0 collective-permute-done.12.next2_ref
  60.9 0.0 collective-permute-done.10.next_ref
  61.0 0.0 collective-permute-done.9.prev_ref
  61.0 2.6 %solve_b.1 = f32[8,64,128]{2,1,0:T(8,128)S(1)} custom-call(s32[2]{0:T(128)S(1)} %pad_add_fusion.pos_ref, bf16[360,256]{1,0:T(8,128)(2,1)S(1)} %merge.1.far0, bf16[360,256]{1,0:T(8,128)(2,1)S(1)} %collective-permute-done.6.far1, bf16[360,256]{1,0:T(8,128)(2,1)S(1)} %collective-permute-done.7.far2, bf16[360,256]{1,0:T(8,128)(2,1)S(1)} %collective-permute-done.8.far3, ...), custom_call_target="tpu_custom_call" | custom-call | tf_op jit(solution)/shard_map/solve_b/pallas_call | solution.py:576
  63.5 11.4 %all_to_all.5.parts_ref = f32[8,64,128]{2,1,0:T(8,128)S(1)} all-to-all(f32[8,64,128]{2,1,0:T(8,128)S(1)} %solve_b.1), channel_id=1, replica_groups=mesh['chain'=8,'quad'=16] {'chain'}, dimensions={0} | all-to-all | bytes 524288 | tf_op jit(solution)/shard_map/all_to_all | solution.py:622
  75.0 0.0 copy-done.4
  75.0 4.4 %finish.1 = (bf16[256,4096]{1,0:T(8,128)(2,1)}, f32[64,128]{1,0:T(8,128)}) custom-call(s32[2]{0:T(128)S(1)} %pad_add_fusion.pos_ref, bf16[256,4096]{1,0:T(8,128)(2,1)S(1)} %bitcast.12, f32[256,4096]{1,0:T(8,128)S(1)} %get-tuple-element.13.xs, f32[256,4096]{1,0:T(8,128)S(1)} %get-tuple-element.14.ys, f32[8,64,128]{2,1,0:T(8,128)S(1)} %all_to_all.5.parts_ref, ...), custom_call_target="tpu_custom_call" | custom-call | tf_op jit(solution)/shard_map/finish/pallas_call | solution.py:576
  (2 shorter events, 0.0 us)
Async XLA Ops:
  0.6 25.9 %collective-permute-start.2 = (bf16[256,4096]{1,0:T(8,128)(2,1)}, bf16[256,4096]{1,0:T(8,128)(2,1)S(1)}, u32[]{:S(2)}, u32[]{:S(2)}) collective-permute-start(bf16[256,4096]{1,0:T(8,128)(2,1)} %bitcast.9), channel_id=1, source_target_pairs={{0,16},{16,32},{32,48},{48,64},{64,80},{80,96},{96,112},{112,0},{1... | collective-permute-start | bytes 6291464 | tf_op jit(solution)/shard_map/ppermute | solution.py:563
  4.1 7.4 %collective-permute-start = (bf16[1,4096]{1,0:T(2,128)(2,1)S(1)}, bf16[1,4096]{1,0:T(2,128)(2,1)S(1)}, u32[]{:S(2)}, u32[]{:S(2)}) collective-permute-start(bf16[1,4096]{1,0:T(2,128)(2,1)S(1)} %get-tuple-element.25), channel_id=1, source_target_pairs={{0,1},{1,2},{2,3},{3,4},{4,5},{5,6},{6,7},{7,8},{8,9},{9,10},{10,1... | collective-permute-start | bytes 24584 | tf_op jit(solution)/shard_map/ppermute | solution.py:563
  5.5 6.0 %collective-permute-start.1 = (bf16[1,4096]{1,0:T(2,128)(2,1)S(1)}, bf16[1,4096]{1,0:T(2,128)(2,1)S(1)}, u32[]{:S(2)}, u32[]{:S(2)}) collective-permute-start(bf16[1,4096]{1,0:T(2,128)(2,1)S(1)} %get-tuple-element.24), channel_id=1, source_target_pairs={{0,15},{1,0},{2,1},{3,2},{4,3},{5,4},{6,5},{7,6},{8,7},{9,8},{10,9... | collective-permute-start | bytes 24584 | tf_op jit(solution)/shard_map/ppermute | solution.py:563
  11.5 1.6 %copy-start = (bf16[1,256,4096]{2,1,0:T(8,128)(2,1)S(1)}, bf16[1,256,4096]{2,1,0:T(8,128)(2,1)}, u32[]{:S(2)}) copy-start(bf16[1,256,4096]{2,1,0:T(8,128)(2,1)} %param.5) | copy-start | bytes 6291460
  13.1 1.4 %copy-start.2 = (bf16[3200,256]{1,0:T(8,128)(2,1)S(1)}, bf16[3200,256]{1,0:T(8,128)(2,1)}, u32[]{:S(2)}) copy-start(bf16[3200,256]{1,0:T(8,128)(2,1)} %constant.34.clone.blob_ref) | copy-start | bytes 4915204
  14.6 1.6 %copy-start.3 = (bf16[256,4096]{1,0:T(8,128)(2,1)S(1)}, bf16[256,4096]{1,0:T(8,128)(2,1)}, u32[]{:S(2)}) copy-start(bf16[256,4096]{1,0:T(8,128)(2,1)} %anchor_hbm.1) | copy-start | bytes 6291460
  16.2 0.7 copy-start.5
  16.9 9.7 %copy-start.1 = (bf16[1,256,4096]{2,1,0:T(8,128)(2,1)S(1)}, bf16[1,256,4096]{2,1,0:T(8,128)(2,1)}, u32[]{:S(2)}) copy-start(bf16[1,256,4096]{2,1,0:T(8,128)(2,1)} %param.5) | copy-start | bytes 6291460
  30.5 44.5 %copy-start.4 = (f32[256,8]{1,0:T(8,128)S(1)}, f32[256,8]{1,0:T(8,128)}, u32[]{:S(2)}) copy-start(f32[256,8]{1,0:T(8,128)} %constant.36.clone.r8_hbm) | copy-start | bytes 24580
  30.5 5.0 %collective-permute-start.3 = (bf16[128,256]{1,0:T(8,128)(2,1)S(1)}, bf16[128,256]{1,0:T(8,128)(2,1)S(1)}, u32[]{:S(2)}, u32[]{:S(2)}) collective-permute-start(bf16[128,256]{1,0:T(8,128)(2,1)S(1)} %stage1.1.near0), channel_id=1, source_target_pairs={{0,1},{1,2},{2,3},{3,0},{4,5},{5,6},{6,7},{7,4},{8,9},{9,10},{10,1... | collective-permute-start | bytes 196616 | tf_op jit(solution)/shard_map/ppermute | solution.py:558
  31.8 5.0 %collective-permute-start.4 = (bf16[128,256]{1,0:T(8,128)(2,1)S(1)}, bf16[128,256]{1,0:T(8,128)(2,1)S(1)}, u32[]{:S(2)}, u32[]{:S(2)}) collective-permute-start(bf16[128,256]{1,0:T(8,128)(2,1)S(1)} %stage1.1.near0), channel_id=1, source_target_pairs={{0,2},{1,3},{2,0},{3,1},{4,6},{5,7},{6,4},{7,5},{8,10},{9,11},{10,... | collective-permute-start | bytes 196616 | tf_op jit(solution)/shard_map/ppermute | solution.py:558
  34.4 3.4 %collective-permute-start.5 = (bf16[128,256]{1,0:T(8,128)(2,1)S(1)}, bf16[128,256]{1,0:T(8,128)(2,1)S(1)}, u32[]{:S(2)}, u32[]{:S(2)}) collective-permute-start(bf16[128,256]{1,0:T(8,128)(2,1)S(1)} %stage1.1.near0), channel_id=1, source_target_pairs={{0,3},{1,0},{2,1},{3,2},{4,7},{5,4},{6,5},{7,6},{8,11},{9,8},{10,9... | collective-permute-start | bytes 196616 | tf_op jit(solution)/shard_map/ppermute | solution.py:558
  38.6 6.8 %collective-permute-start.6 = (bf16[360,256]{1,0:T(8,128)(2,1)S(1)}, bf16[360,256]{1,0:T(8,128)(2,1)S(1)}, u32[]{:S(2)}, u32[]{:S(2)}) collective-permute-start(bf16[360,256]{1,0:T(8,128)(2,1)S(1)} %merge.1.far0), channel_id=1, source_target_pairs={{0,4},{1,5},{2,6},{3,7},{4,8},{5,9},{6,10},{7,11},{8,12},{9,13},{1... | collective-permute-start | bytes 552968 | tf_op jit(solution)/shard_map/ppermute | solution.py:558
  40.3 8.3 %collective-permute-start.7 = (bf16[360,256]{1,0:T(8,128)(2,1)S(1)}, bf16[360,256]{1,0:T(8,128)(2,1)S(1)}, u32[]{:S(2)}, u32[]{:S(2)}) collective-permute-start(bf16[360,256]{1,0:T(8,128)(2,1)S(1)} %merge.1.far0), channel_id=1, source_target_pairs={{0,8},{1,9},{2,10},{3,11},{4,12},{5,13},{6,14},{7,15},{8,0},{9,1},... | collective-permute-start | bytes 552968 | tf_op jit(solution)/shard_map/ppermute | solution.py:558
  43.6 5.0 %collective-permute-start.8 = (bf16[360,256]{1,0:T(8,128)(2,1)S(1)}, bf16[360,256]{1,0:T(8,128)(2,1)S(1)}, u32[]{:S(2)}, u32[]{:S(2)}) collective-permute-start(bf16[360,256]{1,0:T(8,128)(2,1)S(1)} %merge.1.far0), channel_id=1, source_target_pairs={{0,12},{1,13},{2,14},{3,15},{4,0},{5,1},{6,2},{7,3},{8,4},{9,5},{1... | collective-permute-start | bytes 552968 | tf_op jit(solution)/shard_map/ppermute | solution.py:558
  50.6 10.3 %collective-permute-start.10 = (f32[128,128]{1,0:T(8,128)S(1)}, f32[128,128]{1,0:T(8,128)S(1)}, u32[]{:S(2)}, u32[]{:S(2)}) collective-permute-start(f32[128,128]{1,0:T(8,128)S(1)} %get-tuple-element.19.own_ref), channel_id=1, source_target_pairs={{0,112},{16,0},{32,16},{48,32},{64,48},{80,64},{96,80},{112,96},{1... | collective-permute-start | bytes 196616 | tf_op jit(solution)/shard_map/ppermute | solution.py:563
  55.6 5.3 %collective-permute-start.9 = (f32[128,128]{1,0:T(8,128)S(1)}, f32[128,128]{1,0:T(8,128)S(1)}, u32[]{:S(2)}, u32[]{:S(2)}) collective-permute-start(f32[128,128]{1,0:T(8,128)S(1)} %get-tuple-element.19.own_ref), channel_id=1, source_target_pairs={{0,16},{16,32},{32,48},{48,64},{64,80},{80,96},{96,112},{112,0},{1... | collective-permute-start | bytes 196616 | tf_op jit(solution)/shard_map/ppermute | solution.py:563
  56.9 4.1 %collective-permute-start.11 = (f32[64,128]{1,0:T(8,128)S(1)}, f32[64,128]{1,0:T(8,128)S(1)}, u32[]{:S(2)}, u32[]{:S(2)}) collective-permute-start(f32[64,128]{1,0:T(8,128)S(1)} %get-tuple-element.20), channel_id=1, source_target_pairs={{0,32},{16,48},{32,64},{48,80},{64,96},{80,112},{96,0},{112,16},{1... | collective-permute-start | bytes 98312 | tf_op jit(solution)/shard_map/ppermute | solution.py:563
  57.8 3.2 %collective-permute-start.12 = (f32[64,128]{1,0:T(8,128)S(1)}, f32[64,128]{1,0:T(8,128)S(1)}, u32[]{:S(2)}, u32[]{:S(2)}) collective-permute-start(f32[64,128]{1,0:T(8,128)S(1)} %get-tuple-element.20), channel_id=1, source_target_pairs={{0,96},{16,112},{32,0},{48,16},{64,32},{80,48},{96,64},{112,80},{1... | collective-permute-start | bytes 98312 | tf_op jit(solution)/shard_map/ppermute | solution.py:563

commit v3 on v2

--- a/solution.py
+++ b/solution.py
@@ -230,10 +230,9 @@
 
 
 def cross_part(pos_ref, m_ref, xs, ys, blob_ref, anchor_ref, prior_ref, fxh, fxl, fyh, fyl, lacc, sums):
-    first = pos_ref[0] == 0
     sums[...] = jnp.zeros((8, 128), F32)
 
-    def body(step, carry):
+    def body(f_ref, step, carry):
         lin = blob_ref[LIN : LIN + 16, :]
         cross = jnp.zeros((8, 256), F32)
         whole_sum = jnp.zeros((8, 256), F32)
@@ -244,7 +243,7 @@
             for c in range(ROWS // CHUNK):
                 rows = pl.ds(CHUNK * c, CHUNK)
                 m, x, y = m_ref[rows, from_m].astype(F32), xs[rows, from_m], ys[rows, from_m]
-                f = jnp.where(first, anchor_ref[rows, from_m].astype(F32), prior_ref[rows, from_m].astype(F32))
+                f = f_ref[rows, from_m].astype(F32)
                 fxh[rows, at], fxl[rows, at] = hi_lo(f * x)
                 fyh[rows, at], fyl[rows, at] = hi_lo(f * y)
                 cross = cross + fold8(f * m)
@@ -257,7 +256,14 @@
         sums[1:2, :] += lanes_to_row(whole_sum)
         return carry
 
-    lax.fori_loop(0, STEPS, body, 0)
+    @pl.when(pos_ref[0] == 0)
+    def _():
+        lax.fori_loop(0, STEPS, lambda i, c: body(anchor_ref, i, c), 0)
+
+    @pl.when(pos_ref[0] > 0)
+    def _():
+        lax.fori_loop(0, STEPS, lambda i, c: body(prior_ref, i, c), 0)
+
     p = jnp.zeros((48, 128), F32)
     for i in range(STEPS):
         p = p + dot(split3(lacc[16 * i : 16 * i + 16, :]), put_rows(blob_ref, i))
@@ -474,10 +480,14 @@
     return g / jnp.sqrt(total(g * g) / 8192.0 + EPS)
 
 
-def solve_a(pos_ref, far0, far1, far2, far3, out_ref, lead_ref, a1, a2, all_ref):
+def solve_a(pos_ref, far0, far1, far2, far3, out_ref, lead_ref, a1, a2, kept_ref, all_ref):
     items, sums = unpack(pos_ref, (far0, far1, far2, far3), all_ref)
     build_operator(items, a1, a2)
     valid, grads = fields(items)
+    for t in range(3):
+        kept_ref[EXT * t : EXT * t + EXT, :] = grads[t]
+    for t in range(4):
+        kept_ref[3 * EXT + t : 3 * EXT + t + 1, :] = jnp.broadcast_to(sums[t], (1, 128))
     c = RATE * direction(valid, grads, sums, None, None)
     d = direction(valid, grads, sums, c, apply_operator(a1, a2, c))
     lead = narrow(c)
@@ -486,11 +496,12 @@
     out_ref[GRID : 2 * GRID, :] = narrow(d)
 
 
-def solve_b(pos_ref, far0, far1, far2, far3, own_ref, prev_ref, next_ref, prev2_ref, next2_ref, out_ref, a1, a2, all_ref):
+def solve_b(pos_ref, a1, a2, kept_ref, own_ref, prev_ref, next_ref, prev2_ref, next2_ref, out_ref):
     k = pos_ref[0]
-    items, sums = unpack(pos_ref, (far0, far1, far2, far3), all_ref)
-    build_operator(items, a1, a2)
-    valid, grads = fields(items)
+    row = lax.broadcasted_iota(jnp.int32, (EXT, 128), 0)
+    valid = (row >= 2) & (row < 66)
+    grads = [kept_ref[EXT * t : EXT * t + EXT, :] for t in range(3)]
+    sums = [kept_ref[3 * EXT + t : 3 * EXT + t + 1, 0:1] for t in range(4)]
 
     def lap(a, b, c):
         return a - 2.0 * b + c
@@ -510,19 +521,30 @@
     d2 = direction(valid, grads, sums, c2, apply_operator(a1, a2, c2))
     c3 = c2 + RATE * d2 + SMOOTH * lap(c2l, c2, c2r)
     d3 = direction(valid, grads, sums, c3, apply_operator(a1, a2, c3))
-    u = narrow(c3 + RATE * d3)
-    c3 = narrow(c3)
-    for t in range(8):
-        w = SMOOTH * (jnp.where(k == t + 1, 1.0, 0.0) - jnp.where(k == t, 1.0, 0.0) - jnp.where(k == 0, 1.0, 0.0))
-        out_ref[t] = jnp.where(k <= t, 1.0, 0.0) * u + w * c3
-
-
-def finish(pos_ref, m_ref, xs, ys, parts_ref, r8_hbm, turned_ref, out_ref, acc_ref, sx, sy, total_ref, mixed, buf, r8_ref, sems, fetched):
+    out_ref[0:GRID, :] = narrow(c3 + RATE * d3)
+    out_ref[GRID : 2 * GRID, :] = narrow(c3)
+
+
+def pair_sum(pos_ref, own_ref, other_ref, out_ref, more_ref):
+    k = pos_ref[0]
+    even = jnp.where(k % 2 == 0, own_ref[GRID : 2 * GRID, :], other_ref[GRID : 2 * GRID, :])
+    both = own_ref[0:GRID, :] + other_ref[0:GRID, :] - jnp.where(k < 2, SMOOTH, 0.0) * even
+    out_ref[...] = both
+    more_ref[0:GRID, :] = both
+    more_ref[GRID : 2 * GRID, :] = even
+
+
+def finish(pos_ref, m_ref, xs, ys, own_ref, other_ref, one_ref, two_ref, more_ref, r8_hbm, turned_ref, out_ref, acc_ref, sx, sy, total_ref, mixed, buf, r8_ref, sems, fetched):
     bring = pltpu.make_async_copy(r8_hbm, r8_ref, fetched)
     bring.start()
-    acc = parts_ref[0]
-    for t in range(1, 8):
-        acc = acc + parts_ref[t]
+    k = pos_ref[0]
+    odd = k % 2 == 1
+    own_c, other_c = own_ref[GRID : 2 * GRID, :], other_ref[GRID : 2 * GRID, :]
+    after = jnp.where(odd, jnp.where(k < 7, more_ref[GRID : 2 * GRID, :], 0.0), other_c)
+    acc = own_ref[0:GRID, :] + jnp.where(odd, other_ref[0:GRID, :], 0.0) + SMOOTH * (after - own_c)
+    acc = acc - jnp.where(k < 2, SMOOTH, 0.0) * jnp.where(odd, other_c, own_c)
+    acc = acc + jnp.where(k > 1, one_ref[...], 0.0) + jnp.where(k > 3, two_ref[...], 0.0)
+    acc = acc + jnp.where(k > 5, more_ref[0:GRID, :], 0.0)
     acc_ref[...] = acc
     total_ref[...] = widen(acc)
     c8 = total_ref[pl.ds(4 * pos_ref[1], 8), :]
@@ -615,22 +637,31 @@
     four = [packed] + [around_four(packed, 1, d) for d in (1, 2, 3)]
     (near,) = call(merge, "merge", (pos, *four), [shape((360, 256), BF)], [pltpu.VMEM((4, 128, 256), BF)], 12)
     far = [near] + [around_four(near, 4, d) for d in (1, 2, 3)]
-    operator = [pltpu.VMEM((28, EXT, 128), F32)] * 2 + [pltpu.VMEM((4, 360, 256), BF)]
-    first, lead = call(solve_a, "solve_a", (pos, *far), [shape((2 * GRID, 128), F32), shape((GRID, 128), F32)], operator, 12)
+    operator = [shape((28, EXT, 128), F32)] * 2
+    first, lead, a1, a2, kept = call(
+        solve_a,
+        "solve_a",
+        (pos, *far),
+        [shape((2 * GRID, 128), F32), shape((GRID, 128), F32), *operator, shape((3 * EXT + 8, 128), F32)],
+        [pltpu.VMEM((4, 360, 256), BF)],
+        12,
+    )
     around = [ring(first, "chain", 1), ring(first, "chain", -1), ring(lead, "chain", 2), ring(lead, "chain", -2)]
-    (parts,) = call(solve_b, "solve_b", (pos, *far, first, *around), [shape((8, GRID, 128), F32)], operator, 12)
-    parts = lax.all_to_all(parts, "chain", 0, 0, tiled=True)
+    (own,) = call(solve_b, "solve_b", (pos, a1, a2, kept, first, *around), [shape((2 * GRID, 128), F32)], [], 12)
+    other = lax.ppermute(own, "chain", [(i, i ^ 1) for i in range(8)])
+    both, more = call(pair_sum, "pair_sum", (pos, own, other), [shape((GRID, 128), F32), shape((2 * GRID, 128), F32)], [], 12)
+    earlier = [ring(both, "chain", 2), ring(both, "chain", 4), ring(more, "chain", -2)]
     registered, accumulated = call(
         finish,
         "finish",
-        (pos, strip, xs, ys, parts, jnp.asarray(r8), turned),
+        (pos, strip, xs, ys, own, other, *earlier, jnp.asarray(r8), turned),
         [shape((ROWS, COLS), BF), shape((GRID, 128), F32)],
         [WIDE] * 2
         + [pltpu.VMEM((EXT, 128), F32), pltpu.VMEM((ROWS, 128), BF), pltpu.VMEM((ROWS, COLS), BF), pltpu.VMEM((ROWS, 8), F32)]
         + [pltpu.SemaphoreType.DMA((STEPS,)), pltpu.SemaphoreType.DMA],
         24,
         hbm_out=True,
-        hbm_in=(5,),
+        hbm_in=(9,),
     )
     return registered[None], accumulated[None]
 

time: 79.8 us -> 77.6 us (0.972)
  blocking collectives: 11.4 us -> 0 us
  starting transfers between devices: 28.6 us -> 33.7 us
  waiting for transfers between devices: 8.94 us -> 12.9 us
    all_to_all x1 -> x0, blocking collectives: 11.4 us -> none  [local(): parts = lax.all_to_all(parts, 'chain', 0, 0, tiled=True)]
    ppermute x7 -> x10, starting transfers between devices: 17.9 us -> 22.1 us  [ring(): return lax.ppermute(array, axis, [(i, (i + by) % n) for i in range(n)])]
    ppermute x7 -> x10, waiting for transfers between devices: 2.33 us -> 5.38 us  [ring(): return lax.ppermute(array, axis, [(i, (i + by) % n) for i in range(n)])]
    ppermute x0 -> x1, waiting for transfers between devices: none -> 0.9 us  [local(): other = lax.ppermute(own, 'chain', [(i, i ^ 1) for i in range(8)])]
    ppermute x0 -> x1, starting transfers between devices: none -> 0.83 us  [local(): other = lax.ppermute(own, 'chain', [(i, i ^ 1) for i in range(8)])]
    pallas_call x6 -> x7, Pallas kernels: 22.7 us -> 22.4 us  [call(): pl.pallas_call(kernel, in_specs=specs, out_specs=[pl.BlockSpec(memory_spa...]
  transfers between devices with their start and end apart: 13 -> 17, of which waited for: 7 -> 10; matrix products, arithmetic and copies ran while one was open for 2% -> 2% of each run, Pallas kernels for 11% -> 12%
where the time goes in v3:
time: 77.6 us; the launch traced here: 76.6 us
  starting transfers between devices  33.7 us (43%)
  Pallas kernels  22.4 us (29%)
  waiting for transfers between devices  12.9 us (17%)
  local copies, waits for them, and re-layouts  6.22 us (8%)
  other arithmetic  0.78 us (1%)
    pallas_call x7, Pallas kernels, call(): pl.pallas_call(kernel, in_specs=specs, out_specs=[pl.BlockSpec(memory_spa...  22.4 us
    ppermute x10, starting transfers between devices, ring(): return lax.ppermute(array, axis, [(i, (i + by) % n) for i in range(n)])  22.1 us
    ppermute x6, starting transfers between devices, around_four(): return lax.ppermute(array, 'quad', [(q, to(q)) for q in range(16)])  10.7 us
    ppermute x6, waiting for transfers between devices, around_four(): return lax.ppermute(array, 'quad', [(q, to(q)) for q in range(16)])  6.61 us
    ppermute x10, waiting for transfers between devices, ring(): return lax.ppermute(array, axis, [(i, (i + by) % n) for i in range(n)])  5.38 us
    unnamed x12, local copies, waits for them, and re-layouts  5.32 us
  transfers between devices with their start and end apart: 17, of which 10 were waited for; matrix products, arithmetic and copies ran while one was open for 2% of the time, Pallas kernels for 12%

profile of v3, /device:TPU:1, one launch (start us, length us, event | category | flops | bytes accessed | tf_op | source)
XLA Modules:
  0.0 76.6 jit_solution(6619469319030502596)
XLA Ops:
  0.6 2.6 %collective-permute-start.2 = (bf16[256,4096]{1,0:T(8,128)(2,1)}, bf16[256,4096]{1,0:T(8,128)(2,1)S(1)}, u32[]{:S(2)}, u32[]{:S(2)}) collective-permute-start(bf16[256,4096]{1,0:T(8,128)(2,1)} %bitcast.9), channel_id=1, source_target_pairs={{0,16},{16,32},{32,48},{48,64},{64,80},{80,96},{96,112},{112,0},{1... | collective-permute-start | bytes 6291464 | tf_op jit(solution)/shard_map/ppermute | solution.py:585
  3.2 0.9 %slice_bitcast_fusion = (bf16[1,4096]{1,0:T(2,128)(2,1)S(1)}, bf16[1,4096]{1,0:T(2,128)(2,1)S(1)}) fusion(bf16[1,256,4096]{2,1,0:T(8,128)(2,1)} %param.5), kind=kLoop, calls=%fused_computation.12 | loop fusion | bytes 32768 | tf_op jit(solution)/shard_map/slice | solution.py:615
  4.1 1.4 %collective-permute-start = (bf16[1,4096]{1,0:T(2,128)(2,1)S(1)}, bf16[1,4096]{1,0:T(2,128)(2,1)S(1)}, u32[]{:S(2)}, u32[]{:S(2)}) collective-permute-start(bf16[1,4096]{1,0:T(2,128)(2,1)S(1)} %get-tuple-element.35), channel_id=1, source_target_pairs={{0,1},{1,2},{2,3},{3,4},{4,5},{5,6},{6,7},{7,8},{8,9},{9,10},{10,1... | collective-permute-start | bytes 24584 | tf_op jit(solution)/shard_map/ppermute | solution.py:585
  5.5 5.0 %collective-permute-start.1 = (bf16[1,4096]{1,0:T(2,128)(2,1)S(1)}, bf16[1,4096]{1,0:T(2,128)(2,1)S(1)}, u32[]{:S(2)}, u32[]{:S(2)}) collective-permute-start(bf16[1,4096]{1,0:T(2,128)(2,1)S(1)} %get-tuple-element.34), channel_id=1, source_target_pairs={{0,15},{1,0},{2,1},{3,2},{4,3},{5,4},{6,5},{7,6},{8,7},{9,8},{10,9... | collective-permute-start | bytes 24584 | tf_op jit(solution)/shard_map/ppermute | solution.py:585
  10.5 0.7 fusion.2.turned_ref
  11.2 0.1 pad_add_fusion.pos_ref
  11.3 0.3 collective-permute-done.up_ref
  11.5 0.0 collective-permute-done.1.dn_ref
  11.5 0.0 copy-start
  11.5 1.6 %copy-done = bf16[1,256,4096]{2,1,0:T(8,128)(2,1)S(1)} copy-done((bf16[1,256,4096]{2,1,0:T(8,128)(2,1)S(1)}, bf16[1,256,4096]{2,1,0:T(8,128)(2,1)}, u32[]{:S(2)}) %copy-start) | copy-done | bytes 2097176
  13.1 0.0 copy-start.2
  13.1 1.4 %copy-done.2 = bf16[3200,256]{1,0:T(8,128)(2,1)S(1)} copy-done((bf16[3200,256]{1,0:T(8,128)(2,1)S(1)}, bf16[3200,256]{1,0:T(8,128)(2,1)}, u32[]{:S(2)}) %copy-start.2) | copy-done | bytes 1638424
  14.6 0.0 copy-start.3
  14.6 1.6 %copy-done.3 = bf16[256,4096]{1,0:T(8,128)(2,1)S(1)} copy-done((bf16[256,4096]{1,0:T(8,128)(2,1)S(1)}, bf16[256,4096]{1,0:T(8,128)(2,1)}, u32[]{:S(2)}) %copy-start.3) | copy-done | bytes 2097176
  16.2 0.0 copy-start.5
  16.2 0.7 copy-done.5
  16.9 0.0 copy-start.1
  16.9 9.0 %stage0.1 = (f32[96,256]{1,0:T(8,128)S(1)}, f32[24,128]{1,0:T(8,128)S(1)}, f32[256,4096]{1,0:T(8,128)S(1)}, f32[256,4096]{1,0:T(8,128)S(1)}, bf16[256,4096]{1,0:T(8,128)(2,1)S(1)}) custom-call(s32[2]{0:T(128)S(1)} %pad_add_fusion.pos_ref, bf16[256,4096]{1,0:T(8,128)(2,1)S(1)} %bitcast.10, bf16[1,4096]{1,0:T(2,128)(2,1)S(1)} %collective-permute-done.up_ref, ...), custom_call_target="tpu_custom_call" | custom-call | tf_op jit(solution)/shard_map/stage0/pallas_call | solution.py:598
  25.8 0.7 collective-permute-done.2.prior_ref
  26.5 0.0 copy-done.1
  26.5 3.5 %stage1.1.near0 = bf16[128,256]{1,0:T(8,128)(2,1)S(1)} custom-call(s32[2]{0:T(128)S(1)} %pad_add_fusion.pos_ref, bf16[256,4096]{1,0:T(8,128)(2,1)S(1)} %bitcast.11, f32[256,4096]{1,0:T(8,128)S(1)} %get-tuple-element.18.xs, f32[256,4096]{1,0:T(8,128)S(1)} %get-tuple-element.19.ys, bf16[3200,256]{1,0:T(8,128)(2,1)S(1)} %copy-done.2, ...), custom_call_target="tpu_custom_call" | custom-call | tf_op jit(solution)/shard_map/stage1/pallas_call | solution.py:598
  30.0 0.0 copy-start.4
  30.0 1.3 %collective-permute-start.3 = (bf16[128,256]{1,0:T(8,128)(2,1)S(1)}, bf16[128,256]{1,0:T(8,128)(2,1)S(1)}, u32[]{:S(2)}, u32[]{:S(2)}) collective-permute-start(bf16[128,256]{1,0:T(8,128)(2,1)S(1)} %stage1.1.near0), channel_id=1, source_target_pairs={{0,1},{1,2},{2,3},{3,0},{4,5},{5,6},{6,7},{7,4},{8,9},{9,10},{10,1... | collective-permute-start | bytes 196616 | tf_op jit(solution)/shard_map/ppermute | solution.py:580
  31.3 2.6 %collective-permute-start.4 = (bf16[128,256]{1,0:T(8,128)(2,1)S(1)}, bf16[128,256]{1,0:T(8,128)(2,1)S(1)}, u32[]{:S(2)}, u32[]{:S(2)}) collective-permute-start(bf16[128,256]{1,0:T(8,128)(2,1)S(1)} %stage1.1.near0), channel_id=1, source_target_pairs={{0,2},{1,3},{2,0},{3,1},{4,6},{5,7},{6,4},{7,5},{8,10},{9,11},{10,... | collective-permute-start | bytes 196616 | tf_op jit(solution)/shard_map/ppermute | solution.py:580
  33.9 1.1 %collective-permute-start.5 = (bf16[128,256]{1,0:T(8,128)(2,1)S(1)}, bf16[128,256]{1,0:T(8,128)(2,1)S(1)}, u32[]{:S(2)}, u32[]{:S(2)}) collective-permute-start(bf16[128,256]{1,0:T(8,128)(2,1)S(1)} %stage1.1.near0), channel_id=1, source_target_pairs={{0,3},{1,0},{2,1},{3,2},{4,7},{5,4},{6,5},{7,6},{8,11},{9,8},{10,9... | collective-permute-start | bytes 196616 | tf_op jit(solution)/shard_map/ppermute | solution.py:580
  35.0 0.0 collective-permute-done.3.near1
  35.0 1.3 %collective-permute-done.4.near2 = bf16[128,256]{1,0:T(8,128)(2,1)S(1)} collective-permute-done((bf16[128,256]{1,0:T(8,128)(2,1)S(1)}, bf16[128,256]{1,0:T(8,128)(2,1)S(1)}, u32[]{:S(2)}, u32[]{:S(2)}) %collective-permute-start.4) | collective-permute-done | bytes 65568 | tf_op jit(solution)/shard_map/ppermute | solution.py:580
  36.3 1.1 %collective-permute-done.5.near3 = bf16[128,256]{1,0:T(8,128)(2,1)S(1)} collective-permute-done((bf16[128,256]{1,0:T(8,128)(2,1)S(1)}, bf16[128,256]{1,0:T(8,128)(2,1)S(1)}, u32[]{:S(2)}, u32[]{:S(2)}) %collective-permute-start.5) | collective-permute-done | bytes 65568 | tf_op jit(solution)/shard_map/ppermute | solution.py:580
  37.3 0.7 merge.1.far0
  38.1 1.7 %collective-permute-start.6 = (bf16[360,256]{1,0:T(8,128)(2,1)S(1)}, bf16[360,256]{1,0:T(8,128)(2,1)S(1)}, u32[]{:S(2)}, u32[]{:S(2)}) collective-permute-start(bf16[360,256]{1,0:T(8,128)(2,1)S(1)} %merge.1.far0), channel_id=1, source_target_pairs={{0,4},{1,5},{2,6},{3,7},{4,8},{5,9},{6,10},{7,11},{8,12},{9,13},{1... | collective-permute-start | bytes 552968 | tf_op jit(solution)/shard_map/ppermute | solution.py:580
  39.8 3.3 %collective-permute-start.7 = (bf16[360,256]{1,0:T(8,128)(2,1)S(1)}, bf16[360,256]{1,0:T(8,128)(2,1)S(1)}, u32[]{:S(2)}, u32[]{:S(2)}) collective-permute-start(bf16[360,256]{1,0:T(8,128)(2,1)S(1)} %merge.1.far0), channel_id=1, source_target_pairs={{0,8},{1,9},{2,10},{3,11},{4,12},{5,13},{6,14},{7,15},{8,0},{9,1},... | collective-permute-start | bytes 552968 | tf_op jit(solution)/shard_map/ppermute | solution.py:580
  43.1 0.7 collective-permute-start.8
  43.8 1.0 %collective-permute-done.6.far1 = bf16[360,256]{1,0:T(8,128)(2,1)S(1)} collective-permute-done((bf16[360,256]{1,0:T(8,128)(2,1)S(1)}, bf16[360,256]{1,0:T(8,128)(2,1)S(1)}, u32[]{:S(2)}, u32[]{:S(2)}) %collective-permute-start.6) | collective-permute-done | bytes 184352 | tf_op jit(solution)/shard_map/ppermute | solution.py:580
  44.8 3.2 %collective-permute-done.7.far2 = bf16[360,256]{1,0:T(8,128)(2,1)S(1)} collective-permute-done((bf16[360,256]{1,0:T(8,128)(2,1)S(1)}, bf16[360,256]{1,0:T(8,128)(2,1)S(1)}, u32[]{:S(2)}, u32[]{:S(2)}) %collective-permute-start.7) | collective-permute-done | bytes 184352 | tf_op jit(solution)/shard_map/ppermute | solution.py:580
  48.1 0.0 collective-permute-done.8.far3
  48.1 2.1 %solve_a.1 = (f32[128,128]{1,0:T(8,128)S(1)}, f32[64,128]{1,0:T(8,128)S(1)}, f32[28,72,128]{2,1,0:T(8,128)S(1)}, f32[28,72,128]{2,1,0:T(8,128)S(1)}, f32[224,128]{1,0:T(8,128)S(1)}) custom-call(s32[2]{0:T(128)S(1)} %pad_add_fusion.pos_ref, bf16[360,256]{1,0:T(8,128)(2,1)S(1)} %merge.1.far0, bf16[360,256]{1,0:T(8,128)(2,1)S(1)} %collective-permute-done.6.far1, ...), custom_call_target="tpu_custom_call" | custom-call | tf_op jit(solution)/shard_map/solve_a/pallas_call | solution.py:598
  50.2 5.0 %collective-permute-start.10 = (f32[128,128]{1,0:T(8,128)S(1)}, f32[128,128]{1,0:T(8,128)S(1)}, u32[]{:S(2)}, u32[]{:S(2)}) collective-permute-start(f32[128,128]{1,0:T(8,128)S(1)} %get-tuple-element.27.own_ref), channel_id=1, source_target_pairs={{0,112},{16,0},{32,16},{48,32},{64,48},{80,64},{96,80},{112,96},{1... | collective-permute-start | bytes 196616 | tf_op jit(solution)/shard_map/ppermute | solution.py:585
  55.2 1.3 %collective-permute-start.9 = (f32[128,128]{1,0:T(8,128)S(1)}, f32[128,128]{1,0:T(8,128)S(1)}, u32[]{:S(2)}, u32[]{:S(2)}) collective-permute-start(f32[128,128]{1,0:T(8,128)S(1)} %get-tuple-element.27.own_ref), channel_id=1, source_target_pairs={{0,16},{16,32},{32,48},{48,64},{64,80},{80,96},{96,112},{112,0},{1... | collective-permute-start | bytes 196616 | tf_op jit(solution)/shard_map/ppermute | solution.py:585
  56.4 0.9 %collective-permute-start.11 = (f32[64,128]{1,0:T(8,128)S(1)}, f32[64,128]{1,0:T(8,128)S(1)}, u32[]{:S(2)}, u32[]{:S(2)}) collective-permute-start(f32[64,128]{1,0:T(8,128)S(1)} %get-tuple-element.28), channel_id=1, source_target_pairs={{0,32},{16,48},{32,64},{48,80},{64,96},{80,112},{96,0},{112,16},{1... | collective-permute-start | bytes 98312 | tf_op jit(solution)/shard_map/ppermute | solution.py:585
  57.3 1.8 %collective-permute-start.12 = (f32[64,128]{1,0:T(8,128)S(1)}, f32[64,128]{1,0:T(8,128)S(1)}, u32[]{:S(2)}, u32[]{:S(2)}) collective-permute-start(f32[64,128]{1,0:T(8,128)S(1)} %get-tuple-element.28), channel_id=1, source_target_pairs={{0,96},{16,112},{32,0},{48,16},{64,32},{80,48},{96,64},{112,80},{1... | collective-permute-start | bytes 98312 | tf_op jit(solution)/shard_map/ppermute | solution.py:585
  59.1 1.4 %collective-permute-done.11.prev2_ref = f32[64,128]{1,0:T(8,128)S(1)} collective-permute-done((f32[64,128]{1,0:T(8,128)S(1)}, f32[64,128]{1,0:T(8,128)S(1)}, u32[]{:S(2)}, u32[]{:S(2)}) %collective-permute-start.11) | collective-permute-done | bytes 32800 | tf_op jit(solution)/shard_map/ppermute | solution.py:585
  60.5 0.0 collective-permute-done.12.next2_ref
  60.5 0.0 collective-permute-done.10.next_ref
  60.5 0.0 collective-permute-done.9.prev_ref
  60.5 2.1 %solve_b.1.own_ref = f32[128,128]{1,0:T(8,128)S(1)} custom-call(s32[2]{0:T(128)S(1)} %pad_add_fusion.pos_ref, f32[28,72,128]{2,1,0:T(8,128)S(1)} %get-tuple-element.24.a1, f32[28,72,128]{2,1,0:T(8,128)S(1)} %get-tuple-element.25.a2, f32[224,128]{1,0:T(8,128)S(1)} %get-tuple-element.26.kept_ref, f32[128,128]{1,0:T(8,128)S(1)} %get-tuple-element.27.own_ref, ...), custom_call_target="tpu_custom_call" | custom-call | tf_op jit(solution)/shard_map/solve_b/pallas_call | solution.py:598
  62.6 0.8 %collective-permute-start.13 = (f32[128,128]{1,0:T(8,128)S(1)}, f32[128,128]{1,0:T(8,128)S(1)}, u32[]{:S(2)}, u32[]{:S(2)}) collective-permute-start(f32[128,128]{1,0:T(8,128)S(1)} %solve_b.1.own_ref), channel_id=1, source_target_pairs={{0,16},{16,0},{32,48},{48,32},{64,80},{80,64},{96,112},{112,96},{1... | collective-permute-start | bytes 196616 | tf_op jit(solution)/shard_map/ppermute | solution.py:651
  63.4 0.9 %collective-permute-done.13.other_ref = f32[128,128]{1,0:T(8,128)S(1)} collective-permute-done((f32[128,128]{1,0:T(8,128)S(1)}, f32[128,128]{1,0:T(8,128)S(1)}, u32[]{:S(2)}, u32[]{:S(2)}) %collective-permute-start.13) | collective-permute-done | bytes 65568 | tf_op jit(solution)/shard_map/ppermute | solution.py:651
  64.3 0.6 pair_sum.1
  64.9 2.9 %collective-permute-start.16 = (f32[128,128]{1,0:T(8,128)S(1)}, f32[128,128]{1,0:T(8,128)S(1)}, u32[]{:S(2)}, u32[]{:S(2)}) collective-permute-start(f32[128,128]{1,0:T(8,128)S(1)} %get-tuple-element.30), channel_id=1, source_target_pairs={{0,96},{16,112},{32,0},{48,16},{64,32},{80,48},{96,64},{112,80},{1... | collective-permute-start | bytes 196616 | tf_op jit(solution)/shard_map/ppermute | solution.py:585
  67.8 0.0 collective-permute-start.14
  67.8 1.3 %collective-permute-start.15 = (f32[64,128]{1,0:T(8,128)S(1)}, f32[64,128]{1,0:T(8,128)S(1)}, u32[]{:S(2)}, u32[]{:S(2)}) collective-permute-start(f32[64,128]{1,0:T(8,128)S(1)} %get-tuple-element.29), channel_id=1, source_target_pairs={{0,64},{16,80},{32,96},{48,112},{64,0},{80,16},{96,32},{112,48},{1... | collective-permute-start | bytes 98312 | tf_op jit(solution)/shard_map/ppermute | solution.py:585
  69.1 2.7 %collective-permute-done.14.one_ref = f32[64,128]{1,0:T(8,128)S(1)} collective-permute-done((f32[64,128]{1,0:T(8,128)S(1)}, f32[64,128]{1,0:T(8,128)S(1)}, u32[]{:S(2)}, u32[]{:S(2)}) %collective-permute-start.14) | collective-permute-done | bytes 32800 | tf_op jit(solution)/shard_map/ppermute | solution.py:585
  71.8 0.3 collective-permute-done.15.two_ref
  72.2 0.0 collective-permute-done.16.more_ref
  72.2 0.0 copy-done.4
  72.2 4.5 %finish.1 = (bf16[256,4096]{1,0:T(8,128)(2,1)}, f32[64,128]{1,0:T(8,128)}) custom-call(s32[2]{0:T(128)S(1)} %pad_add_fusion.pos_ref, bf16[256,4096]{1,0:T(8,128)(2,1)S(1)} %bitcast.12, f32[256,4096]{1,0:T(8,128)S(1)} %get-tuple-element.18.xs, f32[256,4096]{1,0:T(8,128)S(1)} %get-tuple-element.19.ys, f32[128,128]{1,0:T(8,128)S(1)} %solve_b.1.own_ref, ...), custom_call_target="tpu_custom_call" | custom-call | tf_op jit(solution)/shard_map/finish/pallas_call | solution.py:598
  (2 shorter events, 0.0 us)
Async XLA Ops:
  0.6 25.9 %collective-permute-start.2 = (bf16[256,4096]{1,0:T(8,128)(2,1)}, bf16[256,4096]{1,0:T(8,128)(2,1)S(1)}, u32[]{:S(2)}, u32[]{:S(2)}) collective-permute-start(bf16[256,4096]{1,0:T(8,128)(2,1)} %bitcast.9), channel_id=1, source_target_pairs={{0,16},{16,32},{32,48},{48,64},{64,80},{80,96},{96,112},{112,0},{1... | collective-permute-start | bytes 6291464 | tf_op jit(solution)/shard_map/ppermute | solution.py:585
  4.1 7.4 %collective-permute-start = (bf16[1,4096]{1,0:T(2,128)(2,1)S(1)}, bf16[1,4096]{1,0:T(2,128)(2,1)S(1)}, u32[]{:S(2)}, u32[]{:S(2)}) collective-permute-start(bf16[1,4096]{1,0:T(2,128)(2,1)S(1)} %get-tuple-element.35), channel_id=1, source_target_pairs={{0,1},{1,2},{2,3},{3,4},{4,5},{5,6},{6,7},{7,8},{8,9},{9,10},{10,1... | collective-permute-start | bytes 24584 | tf_op jit(solution)/shard_map/ppermute | solution.py:585
  5.5 6.0 %collective-permute-start.1 = (bf16[1,4096]{1,0:T(2,128)(2,1)S(1)}, bf16[1,4096]{1,0:T(2,128)(2,1)S(1)}, u32[]{:S(2)}, u32[]{:S(2)}) collective-permute-start(bf16[1,4096]{1,0:T(2,128)(2,1)S(1)} %get-tuple-element.34), channel_id=1, source_target_pairs={{0,15},{1,0},{2,1},{3,2},{4,3},{5,4},{6,5},{7,6},{8,7},{9,8},{10,9... | collective-permute-start | bytes 24584 | tf_op jit(solution)/shard_map/ppermute | solution.py:585
  11.5 1.6 %copy-start = (bf16[1,256,4096]{2,1,0:T(8,128)(2,1)S(1)}, bf16[1,256,4096]{2,1,0:T(8,128)(2,1)}, u32[]{:S(2)}) copy-start(bf16[1,256,4096]{2,1,0:T(8,128)(2,1)} %param.5) | copy-start | bytes 6291460
  13.1 1.4 %copy-start.2 = (bf16[3200,256]{1,0:T(8,128)(2,1)S(1)}, bf16[3200,256]{1,0:T(8,128)(2,1)}, u32[]{:S(2)}) copy-start(bf16[3200,256]{1,0:T(8,128)(2,1)} %constant.34.clone.blob_ref) | copy-start | bytes 4915204
  14.6 1.6 %copy-start.3 = (bf16[256,4096]{1,0:T(8,128)(2,1)S(1)}, bf16[256,4096]{1,0:T(8,128)(2,1)}, u32[]{:S(2)}) copy-start(bf16[256,4096]{1,0:T(8,128)(2,1)} %anchor_hbm.1) | copy-start | bytes 6291460
  16.2 0.7 copy-start.5
  16.9 9.7 %copy-start.1 = (bf16[1,256,4096]{2,1,0:T(8,128)(2,1)S(1)}, bf16[1,256,4096]{2,1,0:T(8,128)(2,1)}, u32[]{:S(2)}) copy-start(bf16[1,256,4096]{2,1,0:T(8,128)(2,1)} %param.5) | copy-start | bytes 6291460
  30.0 42.2 %copy-start.4 = (f32[256,8]{1,0:T(8,128)S(1)}, f32[256,8]{1,0:T(8,128)}, u32[]{:S(2)}) copy-start(f32[256,8]{1,0:T(8,128)} %constant.36.clone.r8_hbm) | copy-start | bytes 24580
  30.0 5.0 %collective-permute-start.3 = (bf16[128,256]{1,0:T(8,128)(2,1)S(1)}, bf16[128,256]{1,0:T(8,128)(2,1)S(1)}, u32[]{:S(2)}, u32[]{:S(2)}) collective-permute-start(bf16[128,256]{1,0:T(8,128)(2,1)S(1)} %stage1.1.near0), channel_id=1, source_target_pairs={{0,1},{1,2},{2,3},{3,0},{4,5},{5,6},{6,7},{7,4},{8,9},{9,10},{10,1... | collective-permute-start | bytes 196616 | tf_op jit(solution)/shard_map/ppermute | solution.py:580
  31.3 5.0 %collective-permute-start.4 = (bf16[128,256]{1,0:T(8,128)(2,1)S(1)}, bf16[128,256]{1,0:T(8,128)(2,1)S(1)}, u32[]{:S(2)}, u32[]{:S(2)}) collective-permute-start(bf16[128,256]{1,0:T(8,128)(2,1)S(1)} %stage1.1.near0), channel_id=1, source_target_pairs={{0,2},{1,3},{2,0},{3,1},{4,6},{5,7},{6,4},{7,5},{8,10},{9,11},{10,... | collective-permute-start | bytes 196616 | tf_op jit(solution)/shard_map/ppermute | solution.py:580
  33.9 3.4 %collective-permute-start.5 = (bf16[128,256]{1,0:T(8,128)(2,1)S(1)}, bf16[128,256]{1,0:T(8,128)(2,1)S(1)}, u32[]{:S(2)}, u32[]{:S(2)}) collective-permute-start(bf16[128,256]{1,0:T(8,128)(2,1)S(1)} %stage1.1.near0), channel_id=1, source_target_pairs={{0,3},{1,0},{2,1},{3,2},{4,7},{5,4},{6,5},{7,6},{8,11},{9,8},{10,9... | collective-permute-start | bytes 196616 | tf_op jit(solution)/shard_map/ppermute | solution.py:580
  38.1 6.8 %collective-permute-start.6 = (bf16[360,256]{1,0:T(8,128)(2,1)S(1)}, bf16[360,256]{1,0:T(8,128)(2,1)S(1)}, u32[]{:S(2)}, u32[]{:S(2)}) collective-permute-start(bf16[360,256]{1,0:T(8,128)(2,1)S(1)} %merge.1.far0), channel_id=1, source_target_pairs={{0,4},{1,5},{2,6},{3,7},{4,8},{5,9},{6,10},{7,11},{8,12},{9,13},{1... | collective-permute-start | bytes 552968 | tf_op jit(solution)/shard_map/ppermute | solution.py:580
  39.8 8.3 %collective-permute-start.7 = (bf16[360,256]{1,0:T(8,128)(2,1)S(1)}, bf16[360,256]{1,0:T(8,128)(2,1)S(1)}, u32[]{:S(2)}, u32[]{:S(2)}) collective-permute-start(bf16[360,256]{1,0:T(8,128)(2,1)S(1)} %merge.1.far0), channel_id=1, source_target_pairs={{0,8},{1,9},{2,10},{3,11},{4,12},{5,13},{6,14},{7,15},{8,0},{9,1},... | collective-permute-start | bytes 552968 | tf_op jit(solution)/shard_map/ppermute | solution.py:580
  43.1 5.0 %collective-permute-start.8 = (bf16[360,256]{1,0:T(8,128)(2,1)S(1)}, bf16[360,256]{1,0:T(8,128)(2,1)S(1)}, u32[]{:S(2)}, u32[]{:S(2)}) collective-permute-start(bf16[360,256]{1,0:T(8,128)(2,1)S(1)} %merge.1.far0), channel_id=1, source_target_pairs={{0,12},{1,13},{2,14},{3,15},{4,0},{5,1},{6,2},{7,3},{8,4},{9,5},{1... | collective-permute-start | bytes 552968 | tf_op jit(solution)/shard_map/ppermute | solution.py:580
  50.2 10.3 %collective-permute-start.10 = (f32[128,128]{1,0:T(8,128)S(1)}, f32[128,128]{1,0:T(8,128)S(1)}, u32[]{:S(2)}, u32[]{:S(2)}) collective-permute-start(f32[128,128]{1,0:T(8,128)S(1)} %get-tuple-element.27.own_ref), channel_id=1, source_target_pairs={{0,112},{16,0},{32,16},{48,32},{64,48},{80,64},{96,80},{112,96},{1... | collective-permute-start | bytes 196616 | tf_op jit(solution)/shard_map/ppermute | solution.py:585
  55.2 5.3 %collective-permute-start.9 = (f32[128,128]{1,0:T(8,128)S(1)}, f32[128,128]{1,0:T(8,128)S(1)}, u32[]{:S(2)}, u32[]{:S(2)}) collective-permute-start(f32[128,128]{1,0:T(8,128)S(1)} %get-tuple-element.27.own_ref), channel_id=1, source_target_pairs={{0,16},{16,32},{32,48},{48,64},{64,80},{80,96},{96,112},{112,0},{1... | collective-permute-start | bytes 196616 | tf_op jit(solution)/shard_map/ppermute | solution.py:585
  56.4 4.0 %collective-permute-start.11 = (f32[64,128]{1,0:T(8,128)S(1)}, f32[64,128]{1,0:T(8,128)S(1)}, u32[]{:S(2)}, u32[]{:S(2)}) collective-permute-start(f32[64,128]{1,0:T(8,128)S(1)} %get-tuple-element.28), channel_id=1, source_target_pairs={{0,32},{16,48},{32,64},{48,80},{64,96},{80,112},{96,0},{112,16},{1... | collective-permute-start | bytes 98312 | tf_op jit(solution)/shard_map/ppermute | solution.py:585
  57.3 3.2 %collective-permute-start.12 = (f32[64,128]{1,0:T(8,128)S(1)}, f32[64,128]{1,0:T(8,128)S(1)}, u32[]{:S(2)}, u32[]{:S(2)}) collective-permute-start(f32[64,128]{1,0:T(8,128)S(1)} %get-tuple-element.28), channel_id=1, source_target_pairs={{0,96},{16,112},{32,0},{48,16},{64,32},{80,48},{96,64},{112,80},{1... | collective-permute-start | bytes 98312 | tf_op jit(solution)/shard_map/ppermute | solution.py:585
  62.6 1.7 %collective-permute-start.13 = (f32[128,128]{1,0:T(8,128)S(1)}, f32[128,128]{1,0:T(8,128)S(1)}, u32[]{:S(2)}, u32[]{:S(2)}) collective-permute-start(f32[128,128]{1,0:T(8,128)S(1)} %solve_b.1.own_ref), channel_id=1, source_target_pairs={{0,16},{16,0},{32,48},{48,32},{64,80},{80,64},{96,112},{112,96},{1... | collective-permute-start | bytes 196616 | tf_op jit(solution)/shard_map/ppermute | solution.py:651
  64.9 7.3 %collective-permute-start.16 = (f32[128,128]{1,0:T(8,128)S(1)}, f32[128,128]{1,0:T(8,128)S(1)}, u32[]{:S(2)}, u32[]{:S(2)}) collective-permute-start(f32[128,128]{1,0:T(8,128)S(1)} %get-tuple-element.30), channel_id=1, source_target_pairs={{0,96},{16,112},{32,0},{48,16},{64,32},{80,48},{96,64},{112,80},{1... | collective-permute-start | bytes 196616 | tf_op jit(solution)/shard_map/ppermute | solution.py:585
  67.8 4.0 %collective-permute-start.14 = (f32[64,128]{1,0:T(8,128)S(1)}, f32[64,128]{1,0:T(8,128)S(1)}, u32[]{:S(2)}, u32[]{:S(2)}) collective-permute-start(f32[64,128]{1,0:T(8,128)S(1)} %get-tuple-element.29), channel_id=1, source_target_pairs={{0,32},{16,48},{32,64},{48,80},{64,96},{80,112},{96,0},{112,16},{1... | collective-permute-start | bytes 98312 | tf_op jit(solution)/shard_map/ppermute | solution.py:585
  67.8 4.3 %collective-permute-start.15 = (f32[64,128]{1,0:T(8,128)S(1)}, f32[64,128]{1,0:T(8,128)S(1)}, u32[]{:S(2)}, u32[]{:S(2)}) collective-permute-start(f32[64,128]{1,0:T(8,128)S(1)} %get-tuple-element.29), channel_id=1, source_target_pairs={{0,64},{16,80},{32,96},{48,112},{64,0},{80,16},{96,32},{112,48},{1... | collective-permute-start | bytes 98312 | tf_op jit(solution)/shard_map/ppermute | solution.py:585

commit v4 on v3

--- a/solution.py
+++ b/solution.py
@@ -591,12 +591,15 @@
 
 
 def call(kernel, name, args, outs, scratch, limit, hbm_out=False, hbm_in=()):
+    def body(*refs):
+        kernel((lax.axis_index("chain"), lax.axis_index("quad")), *refs)
+
     vm = pl.BlockSpec(memory_space=pltpu.VMEM)
-    specs = [pl.BlockSpec(memory_space=pltpu.SMEM) if a.dtype == jnp.int32 else vm for a in args]
+    specs = [vm] * len(args)
     for i in hbm_in:
         specs[i] = pl.BlockSpec(memory_space=pltpu.HBM)
     return pl.pallas_call(
-        kernel,
+        body,
         in_specs=specs,
         out_specs=[pl.BlockSpec(memory_space=pl.ANY) if hbm_out and i == 0 else vm for i in range(len(outs))],
         out_shape=outs,
@@ -608,7 +611,6 @@
 
 def local(sections, anchor):
     strip = sections[0]
-    pos = jnp.stack([lax.axis_index("chain"), lax.axis_index("quad")]).astype(jnp.int32)
     r8, blob, edge = host_tables()
     prior = ring(strip, "chain", 1)
     up = ring(strip[ROWS - 1 : ROWS], "quad", 1)
@@ -619,49 +621,49 @@
     h, p, xs, ys, before = call(
         stage0,
         "stage0",
-        (pos, strip, up, dn, blob, edge, anchor),
+        (strip, up, dn, blob, edge, anchor),
         [shape((96, 256), F32), shape((24, 128), F32), slope, slope, shape((ROWS, COLS), BF)],
         [pltpu.SemaphoreType.DMA] + [FIELD] * 7 + [pltpu.VMEM((96 * STEPS, 128), F32), pltpu.VMEM((24 * STEPS, 128), F32), pltpu.VMEM((8, COLS), F32), SMALL],
         24,
-        hbm_in=(6,),
+        hbm_in=(5,),
     )
     (packed,) = call(
         stage1,
         "stage1",
-        (pos, strip, xs, ys, blob, before, prior, h, p),
+        (strip, xs, ys, blob, before, prior, h, p),
         [shape((128, 256), BF)],
         [FIELD] * 4 + [pltpu.VMEM((16 * STEPS, 128), F32), SMALL],
         20,
     )
     packed, turned = lax.optimization_barrier((packed, turned))
     four = [packed] + [around_four(packed, 1, d) for d in (1, 2, 3)]
-    (near,) = call(merge, "merge", (pos, *four), [shape((360, 256), BF)], [pltpu.VMEM((4, 128, 256), BF)], 12)
+    (near,) = call(merge, "merge", tuple(four), [shape((360, 256), BF)], [pltpu.VMEM((4, 128, 256), BF)], 12)
     far = [near] + [around_four(near, 4, d) for d in (1, 2, 3)]
     operator = [shape((28, EXT, 128), F32)] * 2
     first, lead, a1, a2, kept = call(
         solve_a,
         "solve_a",
-        (pos, *far),
+        tuple(far),
         [shape((2 * GRID, 128), F32), shape((GRID, 128), F32), *operator, shape((3 * EXT + 8, 128), F32)],
         [pltpu.VMEM((4, 360, 256), BF)],
         12,
     )
     around = [ring(first, "chain", 1), ring(first, "chain", -1), ring(lead, "chain", 2), ring(lead, "chain", -2)]
-    (own,) = call(solve_b, "solve_b", (pos, a1, a2, kept, first, *around), [shape((2 * GRID, 128), F32)], [], 12)
+    (own,) = call(solve_b, "solve_b", (a1, a2, kept, first, *around), [shape((2 * GRID, 128), F32)], [], 12)
     other = lax.ppermute(own, "chain", [(i, i ^ 1) for i in range(8)])
-    both, more = call(pair_sum, "pair_sum", (pos, own, other), [shape((GRID, 128), F32), shape((2 * GRID, 128), F32)], [], 12)
+    both, more = call(pair_sum, "pair_sum", (own, other), [shape((GRID, 128), F32), shape((2 * GRID, 128), F32)], [], 12)
     earlier = [ring(both, "chain", 2), ring(both, "chain", 4), ring(more, "chain", -2)]
     registered, accumulated = call(
         finish,
         "finish",
-        (pos, strip, xs, ys, own, other, *earlier, jnp.asarray(r8), turned),
+        (strip, xs, ys, own, other, *earlier, jnp.asarray(r8), turned),
         [shape((ROWS, COLS), BF), shape((GRID, 128), F32)],
         [WIDE] * 2
         + [pltpu.VMEM((EXT, 128), F32), pltpu.VMEM((ROWS, 128), BF), pltpu.VMEM((ROWS, COLS), BF), pltpu.VMEM((ROWS, 8), F32)]
         + [pltpu.SemaphoreType.DMA((STEPS,)), pltpu.SemaphoreType.DMA],
         24,
         hbm_out=True,
-        hbm_in=(9,),
+        hbm_in=(8,),
     )
     return registered[None], accumulated[None]
 

time: 77.6 us -> 74.3 us (0.957)
  Pallas kernels: 22.4 us -> 18.5 us
    pallas_call x7, Pallas kernels: 22.4 us -> 18.5 us  [call(): pl.pallas_call(body, in_specs=specs, out_specs=[pl.BlockSpec(memory_space...]
where the time goes in v4:
time: 74.3 us; the launch traced here: 73.3 us
  starting transfers between devices  33.7 us (45%)
  Pallas kernels  18.5 us (25%)
  waiting for transfers between devices  13.5 us (18%)
  local copies, waits for them, and re-layouts  6.22 us (8%)
    ppermute x10, starting transfers between devices, ring(): return lax.ppermute(array, axis, [(i, (i + by) % n) for i in range(n)])  22.1 us
    pallas_call x7, Pallas kernels, call(): pl.pallas_call(body, in_specs=specs, out_specs=[pl.BlockSpec(memory_space...  18.5 us
    ppermute x6, starting transfers between devices, around_four(): return lax.ppermute(array, 'quad', [(q, to(q)) for q in range(16)])  10.7 us
    ppermute x6, waiting for transfers between devices, around_four(): return lax.ppermute(array, 'quad', [(q, to(q)) for q in range(16)])  6.61 us
    ppermute x10, waiting for transfers between devices, ring(): return lax.ppermute(array, axis, [(i, (i + by) % n) for i in range(n)])  5.97 us
    unnamed x12, local copies, waits for them, and re-layouts  5.32 us
  transfers between devices with their start and end apart: 17, of which 10 were waited for; matrix products, arithmetic and copies ran while one was open for 2% of the time, Pallas kernels for 12%

profile of v4, /device:TPU:1, one launch (start us, length us, event | category | flops | bytes accessed | tf_op | source)
XLA Modules:
  0.0 73.3 jit_solution(14437808559955867867)
XLA Ops:
  0.6 2.6 %collective-permute-start.2 = (bf16[256,4096]{1,0:T(8,128)(2,1)}, bf16[256,4096]{1,0:T(8,128)(2,1)S(1)}, u32[]{:S(2)}, u32[]{:S(2)}) collective-permute-start(bf16[256,4096]{1,0:T(8,128)(2,1)} %bitcast.7), channel_id=1, source_target_pairs={{0,16},{16,32},{32,48},{48,64},{64,80},{80,96},{96,112},{112,0},{1... | collective-permute-start | bytes 6291464 | tf_op jit(solution)/shard_map/ppermute | solution.py:585
  3.2 0.9 %slice_bitcast_fusion = (bf16[1,4096]{1,0:T(2,128)(2,1)S(1)}, bf16[1,4096]{1,0:T(2,128)(2,1)S(1)}) fusion(bf16[1,256,4096]{2,1,0:T(8,128)(2,1)} %param.5), kind=kLoop, calls=%fused_computation.12 | loop fusion | bytes 32768 | tf_op jit(solution)/shard_map/slice | solution.py:617
  4.1 1.4 %collective-permute-start = (bf16[1,4096]{1,0:T(2,128)(2,1)S(1)}, bf16[1,4096]{1,0:T(2,128)(2,1)S(1)}, u32[]{:S(2)}, u32[]{:S(2)}) collective-permute-start(bf16[1,4096]{1,0:T(2,128)(2,1)S(1)} %get-tuple-element.35), channel_id=1, source_target_pairs={{0,1},{1,2},{2,3},{3,4},{4,5},{5,6},{6,7},{7,8},{8,9},{9,10},{10,1... | collective-permute-start | bytes 24584 | tf_op jit(solution)/shard_map/ppermute | solution.py:585
  5.5 5.0 %collective-permute-start.1 = (bf16[1,4096]{1,0:T(2,128)(2,1)S(1)}, bf16[1,4096]{1,0:T(2,128)(2,1)S(1)}, u32[]{:S(2)}, u32[]{:S(2)}) collective-permute-start(bf16[1,4096]{1,0:T(2,128)(2,1)S(1)} %get-tuple-element.34), channel_id=1, source_target_pairs={{0,15},{1,0},{2,1},{3,2},{4,3},{5,4},{6,5},{7,6},{8,7},{9,8},{10,9... | collective-permute-start | bytes 24584 | tf_op jit(solution)/shard_map/ppermute | solution.py:585
  10.5 0.7 fusion.2.refs_9_
  11.2 0.3 collective-permute-done.refs_1_
  11.5 0.0 collective-permute-done.1.refs_2_
  11.5 0.0 copy-start
  11.5 1.6 %copy-done = bf16[1,256,4096]{2,1,0:T(8,128)(2,1)S(1)} copy-done((bf16[1,256,4096]{2,1,0:T(8,128)(2,1)S(1)}, bf16[1,256,4096]{2,1,0:T(8,128)(2,1)}, u32[]{:S(2)}) %copy-start) | copy-done | bytes 2097176
  13.1 0.0 copy-start.2
  13.1 1.4 %copy-done.2 = bf16[3200,256]{1,0:T(8,128)(2,1)S(1)} copy-done((bf16[3200,256]{1,0:T(8,128)(2,1)S(1)}, bf16[3200,256]{1,0:T(8,128)(2,1)}, u32[]{:S(2)}) %copy-start.2) | copy-done | bytes 1638424
  14.6 0.0 copy-start.3
  14.6 1.6 %copy-done.3 = bf16[256,4096]{1,0:T(8,128)(2,1)S(1)} copy-done((bf16[256,4096]{1,0:T(8,128)(2,1)S(1)}, bf16[256,4096]{1,0:T(8,128)(2,1)}, u32[]{:S(2)}) %copy-start.3) | copy-done | bytes 2097176
  16.2 0.0 copy-start.5
  16.2 0.7 copy-done.5
  16.9 0.0 copy-start.1
  16.9 8.5 %stage0.1 = (f32[96,256]{1,0:T(8,128)S(1)}, f32[24,128]{1,0:T(8,128)S(1)}, f32[256,4096]{1,0:T(8,128)S(1)}, f32[256,4096]{1,0:T(8,128)S(1)}, bf16[256,4096]{1,0:T(8,128)(2,1)S(1)}) custom-call(bf16[256,4096]{1,0:T(8,128)(2,1)S(1)} %bitcast.8, bf16[1,4096]{1,0:T(2,128)(2,1)S(1)} %collective-permute-done.refs_1_, ...), custom_call_target="tpu_custom_call" | custom-call | tf_op jit(solution)/shard_map/stage0/pallas_call | solution.py:601
  25.3 1.2 %collective-permute-done.2.refs_5_ = bf16[256,4096]{1,0:T(8,128)(2,1)S(1)} collective-permute-done((bf16[256,4096]{1,0:T(8,128)(2,1)}, bf16[256,4096]{1,0:T(8,128)(2,1)S(1)}, u32[]{:S(2)}, u32[]{:S(2)}) %collective-permute-start.2) | collective-permute-done | bytes 2097184 | tf_op jit(solution)/shard_map/ppermute | solution.py:585
  26.5 0.0 copy-done.1
  26.5 2.9 %stage1.1.refs_0_ = bf16[128,256]{1,0:T(8,128)(2,1)S(1)} custom-call(bf16[256,4096]{1,0:T(8,128)(2,1)S(1)} %bitcast.9, f32[256,4096]{1,0:T(8,128)S(1)} %get-tuple-element.18.refs_1_, f32[256,4096]{1,0:T(8,128)S(1)} %get-tuple-element.19.refs_2_, bf16[3200,256]{1,0:T(8,128)(2,1)S(1)} %copy-done.2, bf16[256,4096]{1,0:T(8,128)(2,1)S(1)} %get-tuple-element.20.refs_4_, ...), custom_call_target="tpu_custom_call" | custom-call | tf_op jit(solution)/shard_map/stage1/pallas_call | solution.py:601
  29.5 0.0 copy-start.4
  29.5 1.3 %collective-permute-start.3 = (bf16[128,256]{1,0:T(8,128)(2,1)S(1)}, bf16[128,256]{1,0:T(8,128)(2,1)S(1)}, u32[]{:S(2)}, u32[]{:S(2)}) collective-permute-start(bf16[128,256]{1,0:T(8,128)(2,1)S(1)} %stage1.1.refs_0_), channel_id=1, source_target_pairs={{0,1},{1,2},{2,3},{3,0},{4,5},{5,6},{6,7},{7,4},{8,9},{9,10},{10,1... | collective-permute-start | bytes 196616 | tf_op jit(solution)/shard_map/ppermute | solution.py:580
  30.8 2.6 %collective-permute-start.4 = (bf16[128,256]{1,0:T(8,128)(2,1)S(1)}, bf16[128,256]{1,0:T(8,128)(2,1)S(1)}, u32[]{:S(2)}, u32[]{:S(2)}) collective-permute-start(bf16[128,256]{1,0:T(8,128)(2,1)S(1)} %stage1.1.refs_0_), channel_id=1, source_target_pairs={{0,2},{1,3},{2,0},{3,1},{4,6},{5,7},{6,4},{7,5},{8,10},{9,11},{10,... | collective-permute-start | bytes 196616 | tf_op jit(solution)/shard_map/ppermute | solution.py:580
  33.4 1.1 %collective-permute-start.5 = (bf16[128,256]{1,0:T(8,128)(2,1)S(1)}, bf16[128,256]{1,0:T(8,128)(2,1)S(1)}, u32[]{:S(2)}, u32[]{:S(2)}) collective-permute-start(bf16[128,256]{1,0:T(8,128)(2,1)S(1)} %stage1.1.refs_0_), channel_id=1, source_target_pairs={{0,3},{1,0},{2,1},{3,2},{4,7},{5,4},{6,5},{7,6},{8,11},{9,8},{10,9... | collective-permute-start | bytes 196616 | tf_op jit(solution)/shard_map/ppermute | solution.py:580
  34.5 0.0 collective-permute-done.3.refs_1_
  34.5 1.3 %collective-permute-done.4.refs_2_ = bf16[128,256]{1,0:T(8,128)(2,1)S(1)} collective-permute-done((bf16[128,256]{1,0:T(8,128)(2,1)S(1)}, bf16[128,256]{1,0:T(8,128)(2,1)S(1)}, u32[]{:S(2)}, u32[]{:S(2)}) %collective-permute-start.4) | collective-permute-done | bytes 65568 | tf_op jit(solution)/shard_map/ppermute | solution.py:580
  35.7 1.1 %collective-permute-done.5.refs_3_ = bf16[128,256]{1,0:T(8,128)(2,1)S(1)} collective-permute-done((bf16[128,256]{1,0:T(8,128)(2,1)S(1)}, bf16[128,256]{1,0:T(8,128)(2,1)S(1)}, u32[]{:S(2)}, u32[]{:S(2)}) %collective-permute-start.5) | collective-permute-done | bytes 65568 | tf_op jit(solution)/shard_map/ppermute | solution.py:580
  36.8 0.2 merge.1.refs_0_
  37.0 1.7 %collective-permute-start.6 = (bf16[360,256]{1,0:T(8,128)(2,1)S(1)}, bf16[360,256]{1,0:T(8,128)(2,1)S(1)}, u32[]{:S(2)}, u32[]{:S(2)}) collective-permute-start(bf16[360,256]{1,0:T(8,128)(2,1)S(1)} %merge.1.refs_0_), channel_id=1, source_target_pairs={{0,4},{1,5},{2,6},{3,7},{4,8},{5,9},{6,10},{7,11},{8,12},{9,13},{1... | collective-permute-start | bytes 552968 | tf_op jit(solution)/shard_map/ppermute | solution.py:580
  38.7 3.3 %collective-permute-start.7 = (bf16[360,256]{1,0:T(8,128)(2,1)S(1)}, bf16[360,256]{1,0:T(8,128)(2,1)S(1)}, u32[]{:S(2)}, u32[]{:S(2)}) collective-permute-start(bf16[360,256]{1,0:T(8,128)(2,1)S(1)} %merge.1.refs_0_), channel_id=1, source_target_pairs={{0,8},{1,9},{2,10},{3,11},{4,12},{5,13},{6,14},{7,15},{8,0},{9,1},... | collective-permute-start | bytes 552968 | tf_op jit(solution)/shard_map/ppermute | solution.py:580
  42.0 0.7 collective-permute-start.8
  42.7 1.0 %collective-permute-done.6.refs_1_ = bf16[360,256]{1,0:T(8,128)(2,1)S(1)} collective-permute-done((bf16[360,256]{1,0:T(8,128)(2,1)S(1)}, bf16[360,256]{1,0:T(8,128)(2,1)S(1)}, u32[]{:S(2)}, u32[]{:S(2)}) %collective-permute-start.6) | collective-permute-done | bytes 184352 | tf_op jit(solution)/shard_map/ppermute | solution.py:580
  43.7 3.2 %collective-permute-done.7.refs_2_ = bf16[360,256]{1,0:T(8,128)(2,1)S(1)} collective-permute-done((bf16[360,256]{1,0:T(8,128)(2,1)S(1)}, bf16[360,256]{1,0:T(8,128)(2,1)S(1)}, u32[]{:S(2)}, u32[]{:S(2)}) %collective-permute-start.7) | collective-permute-done | bytes 184352 | tf_op jit(solution)/shard_map/ppermute | solution.py:580
  47.0 0.0 collective-permute-done.8.refs_3_
  47.0 1.5 %solve_a.1 = (f32[128,128]{1,0:T(8,128)S(1)}, f32[64,128]{1,0:T(8,128)S(1)}, f32[28,72,128]{2,1,0:T(8,128)S(1)}, f32[28,72,128]{2,1,0:T(8,128)S(1)}, f32[224,128]{1,0:T(8,128)S(1)}) custom-call(bf16[360,256]{1,0:T(8,128)(2,1)S(1)} %merge.1.refs_0_, bf16[360,256]{1,0:T(8,128)(2,1)S(1)} %collective-permute-done.6.refs_1_, ...), custom_call_target="tpu_custom_call" | custom-call | tf_op jit(solution)/shard_map/solve_a/pallas_call | solution.py:601
  48.5 5.0 %collective-permute-start.10 = (f32[128,128]{1,0:T(8,128)S(1)}, f32[128,128]{1,0:T(8,128)S(1)}, u32[]{:S(2)}, u32[]{:S(2)}) collective-permute-start(f32[128,128]{1,0:T(8,128)S(1)} %get-tuple-element.27.refs_3_), channel_id=1, source_target_pairs={{0,112},{16,0},{32,16},{48,32},{64,48},{80,64},{96,80},{112,96},{1... | collective-permute-start | bytes 196616 | tf_op jit(solution)/shard_map/ppermute | solution.py:585
  53.5 1.3 %collective-permute-start.9 = (f32[128,128]{1,0:T(8,128)S(1)}, f32[128,128]{1,0:T(8,128)S(1)}, u32[]{:S(2)}, u32[]{:S(2)}) collective-permute-start(f32[128,128]{1,0:T(8,128)S(1)} %get-tuple-element.27.refs_3_), channel_id=1, source_target_pairs={{0,16},{16,32},{32,48},{48,64},{64,80},{80,96},{96,112},{112,0},{1... | collective-permute-start | bytes 196616 | tf_op jit(solution)/shard_map/ppermute | solution.py:585
  54.8 0.9 %collective-permute-start.11 = (f32[64,128]{1,0:T(8,128)S(1)}, f32[64,128]{1,0:T(8,128)S(1)}, u32[]{:S(2)}, u32[]{:S(2)}) collective-permute-start(f32[64,128]{1,0:T(8,128)S(1)} %get-tuple-element.28), channel_id=1, source_target_pairs={{0,32},{16,48},{32,64},{48,80},{64,96},{80,112},{96,0},{112,16},{1... | collective-permute-start | bytes 98312 | tf_op jit(solution)/shard_map/ppermute | solution.py:585
  55.6 1.8 %collective-permute-start.12 = (f32[64,128]{1,0:T(8,128)S(1)}, f32[64,128]{1,0:T(8,128)S(1)}, u32[]{:S(2)}, u32[]{:S(2)}) collective-permute-start(f32[64,128]{1,0:T(8,128)S(1)} %get-tuple-element.28), channel_id=1, source_target_pairs={{0,96},{16,112},{32,0},{48,16},{64,32},{80,48},{96,64},{112,80},{1... | collective-permute-start | bytes 98312 | tf_op jit(solution)/shard_map/ppermute | solution.py:585
  57.4 1.4 %collective-permute-done.11.refs_6_ = f32[64,128]{1,0:T(8,128)S(1)} collective-permute-done((f32[64,128]{1,0:T(8,128)S(1)}, f32[64,128]{1,0:T(8,128)S(1)}, u32[]{:S(2)}, u32[]{:S(2)}) %collective-permute-start.11) | collective-permute-done | bytes 32800 | tf_op jit(solution)/shard_map/ppermute | solution.py:585
  58.8 0.0 collective-permute-done.12.refs_7_
  58.8 0.0 collective-permute-done.10.refs_5_
  58.8 0.0 collective-permute-done.9.refs_4_
  58.8 1.5 %solve_b.1.refs_0_.refs_3_ = f32[128,128]{1,0:T(8,128)S(1)} custom-call(f32[28,72,128]{2,1,0:T(8,128)S(1)} %get-tuple-element.24.refs_0_, f32[28,72,128]{2,1,0:T(8,128)S(1)} %get-tuple-element.25.refs_1_, f32[224,128]{1,0:T(8,128)S(1)} %get-tuple-element.26.refs_2_, f32[128,128]{1,0:T(8,128)S(1)} %get-tuple-element.27.refs_3_, ...), custom_call_target="tpu_custom_call" | custom-call | tf_op jit(solution)/shard_map/solve_b/pallas_call | solution.py:601
  60.3 0.8 %collective-permute-start.13 = (f32[128,128]{1,0:T(8,128)S(1)}, f32[128,128]{1,0:T(8,128)S(1)}, u32[]{:S(2)}, u32[]{:S(2)}) collective-permute-start(f32[128,128]{1,0:T(8,128)S(1)} %solve_b.1.refs_0_.refs_3_), channel_id=1, source_target_pairs={{0,16},{16,0},{32,48},{48,32},{64,80},{80,64},{96,112},{112,96},{1... | collective-permute-start | bytes 196616 | tf_op jit(solution)/shard_map/ppermute | solution.py:653
  61.1 0.9 %collective-permute-done.13.refs_1_.refs_4_ = f32[128,128]{1,0:T(8,128)S(1)} collective-permute-done((f32[128,128]{1,0:T(8,128)S(1)}, f32[128,128]{1,0:T(8,128)S(1)}, u32[]{:S(2)}, u32[]{:S(2)}) %collective-permute-start.13) | collective-permute-done | bytes 65568 | tf_op jit(solution)/shard_map/ppermute | solution.py:653
  62.1 2.9 %collective-permute-start.16 = (f32[128,128]{1,0:T(8,128)S(1)}, f32[128,128]{1,0:T(8,128)S(1)}, u32[]{:S(2)}, u32[]{:S(2)}) collective-permute-start(f32[128,128]{1,0:T(8,128)S(1)} %get-tuple-element.30), channel_id=1, source_target_pairs={{0,96},{16,112},{32,0},{48,16},{64,32},{80,48},{96,64},{112,80},{1... | collective-permute-start | bytes 196616 | tf_op jit(solution)/shard_map/ppermute | solution.py:585
  65.0 0.0 collective-permute-start.14
  65.0 1.3 %collective-permute-start.15 = (f32[64,128]{1,0:T(8,128)S(1)}, f32[64,128]{1,0:T(8,128)S(1)}, u32[]{:S(2)}, u32[]{:S(2)}) collective-permute-start(f32[64,128]{1,0:T(8,128)S(1)} %get-tuple-element.29), channel_id=1, source_target_pairs={{0,64},{16,80},{32,96},{48,112},{64,0},{80,16},{96,32},{112,48},{1... | collective-permute-start | bytes 98312 | tf_op jit(solution)/shard_map/ppermute | solution.py:585
  66.3 2.7 %collective-permute-done.14.refs_5_ = f32[64,128]{1,0:T(8,128)S(1)} collective-permute-done((f32[64,128]{1,0:T(8,128)S(1)}, f32[64,128]{1,0:T(8,128)S(1)}, u32[]{:S(2)}, u32[]{:S(2)}) %collective-permute-start.14) | collective-permute-done | bytes 32800 | tf_op jit(solution)/shard_map/ppermute | solution.py:585
  69.0 0.3 collective-permute-done.15.refs_6_
  69.3 0.0 collective-permute-done.16.refs_7_
  69.3 0.0 copy-done.4
  69.3 3.9 %finish.1 = (bf16[256,4096]{1,0:T(8,128)(2,1)}, f32[64,128]{1,0:T(8,128)}) custom-call(bf16[256,4096]{1,0:T(8,128)(2,1)S(1)} %bitcast.10, f32[256,4096]{1,0:T(8,128)S(1)} %get-tuple-element.18.refs_1_, f32[256,4096]{1,0:T(8,128)S(1)} %get-tuple-element.19.refs_2_, f32[128,128]{1,0:T(8,128)S(1)} %solve_b.1.refs_0_.refs_3_, ...), custom_call_target="tpu_custom_call" | custom-call | tf_op jit(solution)/shard_map/finish/pallas_call | solution.py:601
  (3 shorter events, 0.0 us)
Async XLA Ops:
  0.6 25.9 %collective-permute-start.2 = (bf16[256,4096]{1,0:T(8,128)(2,1)}, bf16[256,4096]{1,0:T(8,128)(2,1)S(1)}, u32[]{:S(2)}, u32[]{:S(2)}) collective-permute-start(bf16[256,4096]{1,0:T(8,128)(2,1)} %bitcast.7), channel_id=1, source_target_pairs={{0,16},{16,32},{32,48},{48,64},{64,80},{80,96},{96,112},{112,0},{1... | collective-permute-start | bytes 6291464 | tf_op jit(solution)/shard_map/ppermute | solution.py:585
  4.1 7.4 %collective-permute-start = (bf16[1,4096]{1,0:T(2,128)(2,1)S(1)}, bf16[1,4096]{1,0:T(2,128)(2,1)S(1)}, u32[]{:S(2)}, u32[]{:S(2)}) collective-permute-start(bf16[1,4096]{1,0:T(2,128)(2,1)S(1)} %get-tuple-element.35), channel_id=1, source_target_pairs={{0,1},{1,2},{2,3},{3,4},{4,5},{5,6},{6,7},{7,8},{8,9},{9,10},{10,1... | collective-permute-start | bytes 24584 | tf_op jit(solution)/shard_map/ppermute | solution.py:585
  5.5 6.0 %collective-permute-start.1 = (bf16[1,4096]{1,0:T(2,128)(2,1)S(1)}, bf16[1,4096]{1,0:T(2,128)(2,1)S(1)}, u32[]{:S(2)}, u32[]{:S(2)}) collective-permute-start(bf16[1,4096]{1,0:T(2,128)(2,1)S(1)} %get-tuple-element.34), channel_id=1, source_target_pairs={{0,15},{1,0},{2,1},{3,2},{4,3},{5,4},{6,5},{7,6},{8,7},{9,8},{10,9... | collective-permute-start | bytes 24584 | tf_op jit(solution)/shard_map/ppermute | solution.py:585
  11.5 1.6 %copy-start = (bf16[1,256,4096]{2,1,0:T(8,128)(2,1)S(1)}, bf16[1,256,4096]{2,1,0:T(8,128)(2,1)}, u32[]{:S(2)}) copy-start(bf16[1,256,4096]{2,1,0:T(8,128)(2,1)} %param.5) | copy-start | bytes 6291460
  13.1 1.4 %copy-start.2 = (bf16[3200,256]{1,0:T(8,128)(2,1)S(1)}, bf16[3200,256]{1,0:T(8,128)(2,1)}, u32[]{:S(2)}) copy-start(bf16[3200,256]{1,0:T(8,128)(2,1)} %constant.25.clone.refs_3_) | copy-start | bytes 4915204
  14.6 1.6 %copy-start.3 = (bf16[256,4096]{1,0:T(8,128)(2,1)S(1)}, bf16[256,4096]{1,0:T(8,128)(2,1)}, u32[]{:S(2)}) copy-start(bf16[256,4096]{1,0:T(8,128)(2,1)} %refs_5_.1) | copy-start | bytes 6291460
  16.2 0.7 copy-start.5
  16.9 9.7 %copy-start.1 = (bf16[1,256,4096]{2,1,0:T(8,128)(2,1)S(1)}, bf16[1,256,4096]{2,1,0:T(8,128)(2,1)}, u32[]{:S(2)}) copy-start(bf16[1,256,4096]{2,1,0:T(8,128)(2,1)} %param.5) | copy-start | bytes 6291460
  29.5 39.9 %copy-start.4 = (f32[256,8]{1,0:T(8,128)S(1)}, f32[256,8]{1,0:T(8,128)}, u32[]{:S(2)}) copy-start(f32[256,8]{1,0:T(8,128)} %constant.27.clone.refs_8_) | copy-start | bytes 24580
  29.5 5.0 %collective-permute-start.3 = (bf16[128,256]{1,0:T(8,128)(2,1)S(1)}, bf16[128,256]{1,0:T(8,128)(2,1)S(1)}, u32[]{:S(2)}, u32[]{:S(2)}) collective-permute-start(bf16[128,256]{1,0:T(8,128)(2,1)S(1)} %stage1.1.refs_0_), channel_id=1, source_target_pairs={{0,1},{1,2},{2,3},{3,0},{4,5},{5,6},{6,7},{7,4},{8,9},{9,10},{10,1... | collective-permute-start | bytes 196616 | tf_op jit(solution)/shard_map/ppermute | solution.py:580
  30.8 5.0 %collective-permute-start.4 = (bf16[128,256]{1,0:T(8,128)(2,1)S(1)}, bf16[128,256]{1,0:T(8,128)(2,1)S(1)}, u32[]{:S(2)}, u32[]{:S(2)}) collective-permute-start(bf16[128,256]{1,0:T(8,128)(2,1)S(1)} %stage1.1.refs_0_), channel_id=1, source_target_pairs={{0,2},{1,3},{2,0},{3,1},{4,6},{5,7},{6,4},{7,5},{8,10},{9,11},{10,... | collective-permute-start | bytes 196616 | tf_op jit(solution)/shard_map/ppermute | solution.py:580
  33.4 3.4 %collective-permute-start.5 = (bf16[128,256]{1,0:T(8,128)(2,1)S(1)}, bf16[128,256]{1,0:T(8,128)(2,1)S(1)}, u32[]{:S(2)}, u32[]{:S(2)}) collective-permute-start(bf16[128,256]{1,0:T(8,128)(2,1)S(1)} %stage1.1.refs_0_), channel_id=1, source_target_pairs={{0,3},{1,0},{2,1},{3,2},{4,7},{5,4},{6,5},{7,6},{8,11},{9,8},{10,9... | collective-permute-start | bytes 196616 | tf_op jit(solution)/shard_map/ppermute | solution.py:580
  37.0 6.8 %collective-permute-start.6 = (bf16[360,256]{1,0:T(8,128)(2,1)S(1)}, bf16[360,256]{1,0:T(8,128)(2,1)S(1)}, u32[]{:S(2)}, u32[]{:S(2)}) collective-permute-start(bf16[360,256]{1,0:T(8,128)(2,1)S(1)} %merge.1.refs_0_), channel_id=1, source_target_pairs={{0,4},{1,5},{2,6},{3,7},{4,8},{5,9},{6,10},{7,11},{8,12},{9,13},{1... | collective-permute-start | bytes 552968 | tf_op jit(solution)/shard_map/ppermute | solution.py:580
  38.7 8.3 %collective-permute-start.7 = (bf16[360,256]{1,0:T(8,128)(2,1)S(1)}, bf16[360,256]{1,0:T(8,128)(2,1)S(1)}, u32[]{:S(2)}, u32[]{:S(2)}) collective-permute-start(bf16[360,256]{1,0:T(8,128)(2,1)S(1)} %merge.1.refs_0_), channel_id=1, source_target_pairs={{0,8},{1,9},{2,10},{3,11},{4,12},{5,13},{6,14},{7,15},{8,0},{9,1},... | collective-permute-start | bytes 552968 | tf_op jit(solution)/shard_map/ppermute | solution.py:580
  42.0 5.0 %collective-permute-start.8 = (bf16[360,256]{1,0:T(8,128)(2,1)S(1)}, bf16[360,256]{1,0:T(8,128)(2,1)S(1)}, u32[]{:S(2)}, u32[]{:S(2)}) collective-permute-start(bf16[360,256]{1,0:T(8,128)(2,1)S(1)} %merge.1.refs_0_), channel_id=1, source_target_pairs={{0,12},{1,13},{2,14},{3,15},{4,0},{5,1},{6,2},{7,3},{8,4},{9,5},{1... | collective-permute-start | bytes 552968 | tf_op jit(solution)/shard_map/ppermute | solution.py:580
  48.5 10.3 %collective-permute-start.10 = (f32[128,128]{1,0:T(8,128)S(1)}, f32[128,128]{1,0:T(8,128)S(1)}, u32[]{:S(2)}, u32[]{:S(2)}) collective-permute-start(f32[128,128]{1,0:T(8,128)S(1)} %get-tuple-element.27.refs_3_), channel_id=1, source_target_pairs={{0,112},{16,0},{32,16},{48,32},{64,48},{80,64},{96,80},{112,96},{1... | collective-permute-start | bytes 196616 | tf_op jit(solution)/shard_map/ppermute | solution.py:585
  53.5 5.3 %collective-permute-start.9 = (f32[128,128]{1,0:T(8,128)S(1)}, f32[128,128]{1,0:T(8,128)S(1)}, u32[]{:S(2)}, u32[]{:S(2)}) collective-permute-start(f32[128,128]{1,0:T(8,128)S(1)} %get-tuple-element.27.refs_3_), channel_id=1, source_target_pairs={{0,16},{16,32},{32,48},{48,64},{64,80},{80,96},{96,112},{112,0},{1... | collective-permute-start | bytes 196616 | tf_op jit(solution)/shard_map/ppermute | solution.py:585
  54.8 4.0 %collective-permute-start.11 = (f32[64,128]{1,0:T(8,128)S(1)}, f32[64,128]{1,0:T(8,128)S(1)}, u32[]{:S(2)}, u32[]{:S(2)}) collective-permute-start(f32[64,128]{1,0:T(8,128)S(1)} %get-tuple-element.28), channel_id=1, source_target_pairs={{0,32},{16,48},{32,64},{48,80},{64,96},{80,112},{96,0},{112,16},{1... | collective-permute-start | bytes 98312 | tf_op jit(solution)/shard_map/ppermute | solution.py:585
  55.6 3.2 %collective-permute-start.12 = (f32[64,128]{1,0:T(8,128)S(1)}, f32[64,128]{1,0:T(8,128)S(1)}, u32[]{:S(2)}, u32[]{:S(2)}) collective-permute-start(f32[64,128]{1,0:T(8,128)S(1)} %get-tuple-element.28), channel_id=1, source_target_pairs={{0,96},{16,112},{32,0},{48,16},{64,32},{80,48},{96,64},{112,80},{1... | collective-permute-start | bytes 98312 | tf_op jit(solution)/shard_map/ppermute | solution.py:585
  60.3 1.7 %collective-permute-start.13 = (f32[128,128]{1,0:T(8,128)S(1)}, f32[128,128]{1,0:T(8,128)S(1)}, u32[]{:S(2)}, u32[]{:S(2)}) collective-permute-start(f32[128,128]{1,0:T(8,128)S(1)} %solve_b.1.refs_0_.refs_3_), channel_id=1, source_target_pairs={{0,16},{16,0},{32,48},{48,32},{64,80},{80,64},{96,112},{112,96},{1... | collective-permute-start | bytes 196616 | tf_op jit(solution)/shard_map/ppermute | solution.py:653
  62.1 7.3 %collective-permute-start.16 = (f32[128,128]{1,0:T(8,128)S(1)}, f32[128,128]{1,0:T(8,128)S(1)}, u32[]{:S(2)}, u32[]{:S(2)}) collective-permute-start(f32[128,128]{1,0:T(8,128)S(1)} %get-tuple-element.30), channel_id=1, source_target_pairs={{0,96},{16,112},{32,0},{48,16},{64,32},{80,48},{96,64},{112,80},{1... | collective-permute-start | bytes 196616 | tf_op jit(solution)/shard_map/ppermute | solution.py:585
  65.0 4.0 %collective-permute-start.14 = (f32[64,128]{1,0:T(8,128)S(1)}, f32[64,128]{1,0:T(8,128)S(1)}, u32[]{:S(2)}, u32[]{:S(2)}) collective-permute-start(f32[64,128]{1,0:T(8,128)S(1)} %get-tuple-element.29), channel_id=1, source_target_pairs={{0,32},{16,48},{32,64},{48,80},{64,96},{80,112},{96,0},{112,16},{1... | collective-permute-start | bytes 98312 | tf_op jit(solution)/shard_map/ppermute | solution.py:585
  65.0 4.3 %collective-permute-start.15 = (f32[64,128]{1,0:T(8,128)S(1)}, f32[64,128]{1,0:T(8,128)S(1)}, u32[]{:S(2)}, u32[]{:S(2)}) collective-permute-start(f32[64,128]{1,0:T(8,128)S(1)} %get-tuple-element.29), channel_id=1, source_target_pairs={{0,64},{16,80},{32,96},{48,112},{64,0},{80,16},{96,32},{112,48},{1... | collective-permute-start | bytes 98312 | tf_op jit(solution)/shard_map/ppermute | solution.py:585

commit v5 on v4

--- a/solution.py
+++ b/solution.py
@@ -101,7 +101,7 @@
     return r8, jnp.asarray(blob.astype(np.dtype(BF))), jnp.asarray(edge.astype(np.float32))
 
 
-DOWN, ACROSS, PAIRS, LIN, PLAIN, TABLE, PLACE, COLT, PUT, BLOB = 0, 256, 768, 832, 848, 896, 1920, 2432, 2944, 3200
+DOWN, ACROSS, PAIRS, LIN, PLAIN, TABLE, PLACE, COLT, PUT = 0, 256, 768, 832, 848, 896, 1920, 2432, 2944
 
 
 def col_part(blob_ref, lhs):
@@ -590,7 +590,7 @@
 SMALL = pltpu.VMEM((8, 128), F32)
 
 
-def call(kernel, name, args, outs, scratch, limit, hbm_out=False, hbm_in=()):
+def call(kernel, args, outs, scratch, limit, hbm_out=False, hbm_in=()):
     def body(*refs):
         kernel((lax.axis_index("chain"), lax.axis_index("quad")), *refs)
 
@@ -604,12 +604,11 @@
         out_specs=[pl.BlockSpec(memory_space=pl.ANY) if hbm_out and i == 0 else vm for i in range(len(outs))],
         out_shape=outs,
         scratch_shapes=scratch,
-        name=name,
         compiler_params=pltpu.CompilerParams(vmem_limit_bytes=limit << 20),
     )(*args)
 
 
-def local(sections, anchor):
+def registration(sections, anchor):
     strip = sections[0]
     r8, blob, edge = host_tables()
     prior = ring(strip, "chain", 1)
@@ -620,7 +619,6 @@
     slope = shape((ROWS, COLS), F32)
     h, p, xs, ys, before = call(
         stage0,
-        "stage0",
         (strip, up, dn, blob, edge, anchor),
         [shape((96, 256), F32), shape((24, 128), F32), slope, slope, shape((ROWS, COLS), BF)],
         [pltpu.SemaphoreType.DMA] + [FIELD] * 7 + [pltpu.VMEM((96 * STEPS, 128), F32), pltpu.VMEM((24 * STEPS, 128), F32), pltpu.VMEM((8, COLS), F32), SMALL],
@@ -629,7 +627,6 @@
     )
     (packed,) = call(
         stage1,
-        "stage1",
         (strip, xs, ys, blob, before, prior, h, p),
         [shape((128, 256), BF)],
         [FIELD] * 4 + [pltpu.VMEM((16 * STEPS, 128), F32), SMALL],
@@ -637,25 +634,24 @@
     )
     packed, turned = lax.optimization_barrier((packed, turned))
     four = [packed] + [around_four(packed, 1, d) for d in (1, 2, 3)]
-    (near,) = call(merge, "merge", tuple(four), [shape((360, 256), BF)], [pltpu.VMEM((4, 128, 256), BF)], 12)
+    (near,) = call(merge, tuple(four), [shape((360, 256), BF)], [pltpu.VMEM((4, 128, 256), BF)], 12)
     far = [near] + [around_four(near, 4, d) for d in (1, 2, 3)]
     operator = [shape((28, EXT, 128), F32)] * 2
     first, lead, a1, a2, kept = call(
         solve_a,
-        "solve_a",
         tuple(far),
         [shape((2 * GRID, 128), F32), shape((GRID, 128), F32), *operator, shape((3 * EXT + 8, 128), F32)],
         [pltpu.VMEM((4, 360, 256), BF)],
         12,
     )
     around = [ring(first, "chain", 1), ring(first, "chain", -1), ring(lead, "chain", 2), ring(lead, "chain", -2)]
-    (own,) = call(solve_b, "solve_b", (a1, a2, kept, first, *around), [shape((2 * GRID, 128), F32)], [], 12)
+    (own,) = call(solve_b, (a1, a2, kept, first, *around), [shape((2 * GRID, 128), F32)], [], 12)
     other = lax.ppermute(own, "chain", [(i, i ^ 1) for i in range(8)])
-    both, more = call(pair_sum, "pair_sum", (own, other), [shape((GRID, 128), F32), shape((2 * GRID, 128), F32)], [], 12)
-    earlier = [ring(both, "chain", 2), ring(both, "chain", 4), ring(more, "chain", -2)]
+    both, more = call(pair_sum, (own, other), [shape((GRID, 128), F32), shape((2 * GRID, 128), F32)], [], 12)
+    steps = ((both, 2), (both, 4), (more, -2))
+    earlier = [ring(a, "chain", by) for a, by in steps]
     registered, accumulated = call(
         finish,
-        "finish",
         (strip, xs, ys, own, other, *earlier, jnp.asarray(r8), turned),
         [shape((ROWS, COLS), BF), shape((GRID, 128), F32)],
         [WIDE] * 2
@@ -671,4 +667,4 @@
 def solution(mesh):
     in_specs = (P("chain", "quad", None), P("quad", None))
     out_specs = (P("chain", "quad", None), P("chain", None, None))
-    return jax.shard_map(local, mesh=mesh, in_specs=in_specs, out_specs=out_specs, check_vma=False)
+    return jax.shard_map(registration, mesh=mesh, in_specs=in_specs, out_specs=out_specs, check_vma=False)

time: 74.3 us -> 74.3 us (level)
  no operation moved by 1% of the time
where the time goes in v5:
time: 74.3 us; the launch traced here: 73.3 us
  starting transfers between devices  33.7 us (45%)
  Pallas kernels  18.5 us (25%)
  waiting for transfers between devices  13.5 us (18%)
  local copies, waits for them, and re-layouts  6.22 us (8%)
    ppermute x10, starting transfers between devices, ring(): return lax.ppermute(array, axis, [(i, (i + by) % n) for i in range(n)])  22.1 us
    pallas_call x7, Pallas kernels, call(): pl.pallas_call(body, in_specs=specs, out_specs=[pl.BlockSpec(memory_space...  18.5 us
    ppermute x6, starting transfers between devices, around_four(): return lax.ppermute(array, 'quad', [(q, to(q)) for q in range(16)])  10.7 us
    ppermute x6, waiting for transfers between devices, around_four(): return lax.ppermute(array, 'quad', [(q, to(q)) for q in range(16)])  6.61 us
    ppermute x10, waiting for transfers between devices, ring(): return lax.ppermute(array, axis, [(i, (i + by) % n) for i in range(n)])  5.97 us
    unnamed x12, local copies, waits for them, and re-layouts  5.32 us
  transfers between devices with their start and end apart: 17, of which 10 were waited for; matrix products, arithmetic and copies ran while one was open for 2% of the time, Pallas kernels for 12%

profile of v5, /device:TPU:1, one launch (start us, length us, event | category | flops | bytes accessed | tf_op | source)
XLA Modules:
  0.0 73.3 jit_solution(14437808559955867867)
XLA Ops:
  0.6 2.6 %collective-permute-start.2 = (bf16[256,4096]{1,0:T(8,128)(2,1)}, bf16[256,4096]{1,0:T(8,128)(2,1)S(1)}, u32[]{:S(2)}, u32[]{:S(2)}) collective-permute-start(bf16[256,4096]{1,0:T(8,128)(2,1)} %bitcast.7), channel_id=1, source_target_pairs={{0,16},{16,32},{32,48},{48,64},{64,80},{80,96},{96,112},{112,0},{1... | collective-permute-start | bytes 6291464 | tf_op jit(solution)/shard_map/ppermute | solution.py:585
  3.2 0.9 %slice_bitcast_fusion = (bf16[1,4096]{1,0:T(2,128)(2,1)S(1)}, bf16[1,4096]{1,0:T(2,128)(2,1)S(1)}) fusion(bf16[1,256,4096]{2,1,0:T(8,128)(2,1)} %param.5), kind=kLoop, calls=%fused_computation.12 | loop fusion | bytes 32768 | tf_op jit(solution)/shard_map/slice | solution.py:616
  4.1 1.4 %collective-permute-start = (bf16[1,4096]{1,0:T(2,128)(2,1)S(1)}, bf16[1,4096]{1,0:T(2,128)(2,1)S(1)}, u32[]{:S(2)}, u32[]{:S(2)}) collective-permute-start(bf16[1,4096]{1,0:T(2,128)(2,1)S(1)} %get-tuple-element.35), channel_id=1, source_target_pairs={{0,1},{1,2},{2,3},{3,4},{4,5},{5,6},{6,7},{7,8},{8,9},{9,10},{10,1... | collective-permute-start | bytes 24584 | tf_op jit(solution)/shard_map/ppermute | solution.py:585
  5.5 5.0 %collective-permute-start.1 = (bf16[1,4096]{1,0:T(2,128)(2,1)S(1)}, bf16[1,4096]{1,0:T(2,128)(2,1)S(1)}, u32[]{:S(2)}, u32[]{:S(2)}) collective-permute-start(bf16[1,4096]{1,0:T(2,128)(2,1)S(1)} %get-tuple-element.34), channel_id=1, source_target_pairs={{0,15},{1,0},{2,1},{3,2},{4,3},{5,4},{6,5},{7,6},{8,7},{9,8},{10,9... | collective-permute-start | bytes 24584 | tf_op jit(solution)/shard_map/ppermute | solution.py:585
  10.5 0.7 fusion.2.refs_9_
  11.2 0.3 collective-permute-done.refs_1_
  11.5 0.0 collective-permute-done.1.refs_2_
  11.5 0.0 copy-start
  11.5 1.6 %copy-done = bf16[1,256,4096]{2,1,0:T(8,128)(2,1)S(1)} copy-done((bf16[1,256,4096]{2,1,0:T(8,128)(2,1)S(1)}, bf16[1,256,4096]{2,1,0:T(8,128)(2,1)}, u32[]{:S(2)}) %copy-start) | copy-done | bytes 2097176
  13.1 0.0 copy-start.2
  13.1 1.4 %copy-done.2 = bf16[3200,256]{1,0:T(8,128)(2,1)S(1)} copy-done((bf16[3200,256]{1,0:T(8,128)(2,1)S(1)}, bf16[3200,256]{1,0:T(8,128)(2,1)}, u32[]{:S(2)}) %copy-start.2) | copy-done | bytes 1638424
  14.6 0.0 copy-start.3
  14.6 1.6 %copy-done.3 = bf16[256,4096]{1,0:T(8,128)(2,1)S(1)} copy-done((bf16[256,4096]{1,0:T(8,128)(2,1)S(1)}, bf16[256,4096]{1,0:T(8,128)(2,1)}, u32[]{:S(2)}) %copy-start.3) | copy-done | bytes 2097176
  16.2 0.0 copy-start.5
  16.2 0.7 copy-done.5
  16.9 0.0 copy-start.1
  16.9 8.5 %shard_map.68 = (f32[96,256]{1,0:T(8,128)S(1)}, f32[24,128]{1,0:T(8,128)S(1)}, f32[256,4096]{1,0:T(8,128)S(1)}, f32[256,4096]{1,0:T(8,128)S(1)}, bf16[256,4096]{1,0:T(8,128)(2,1)S(1)}) custom-call(bf16[256,4096]{1,0:T(8,128)(2,1)S(1)} %bitcast.8, bf16[1,4096]{1,0:T(2,128)(2,1)S(1)} %collective-permute-done.refs_1_, ...), custom_call_target="tpu_custom_call" | custom-call | tf_op jit(solution)/shard_map/pallas_call | solution.py:601
  25.3 1.2 %collective-permute-done.2.refs_5_ = bf16[256,4096]{1,0:T(8,128)(2,1)S(1)} collective-permute-done((bf16[256,4096]{1,0:T(8,128)(2,1)}, bf16[256,4096]{1,0:T(8,128)(2,1)S(1)}, u32[]{:S(2)}, u32[]{:S(2)}) %collective-permute-start.2) | collective-permute-done | bytes 2097184 | tf_op jit(solution)/shard_map/ppermute | solution.py:585
  26.5 0.0 copy-done.1
  26.5 2.9 %shard_map.69.refs_0_ = bf16[128,256]{1,0:T(8,128)(2,1)S(1)} custom-call(bf16[256,4096]{1,0:T(8,128)(2,1)S(1)} %bitcast.9, f32[256,4096]{1,0:T(8,128)S(1)} %get-tuple-element.18.refs_1_, f32[256,4096]{1,0:T(8,128)S(1)} %get-tuple-element.19.refs_2_, bf16[3200,256]{1,0:T(8,128)(2,1)S(1)} %copy-done.2, bf16[256,4096]{1,0:T(8,128)(2,1)S(1)} %get-tuple-element.20.refs_4_, ...), custom_call_target="tpu_custom_call" | custom-call | tf_op jit(solution)/shard_map/pallas_call | solution.py:601
  29.5 0.0 copy-start.4
  29.5 1.3 %collective-permute-start.3 = (bf16[128,256]{1,0:T(8,128)(2,1)S(1)}, bf16[128,256]{1,0:T(8,128)(2,1)S(1)}, u32[]{:S(2)}, u32[]{:S(2)}) collective-permute-start(bf16[128,256]{1,0:T(8,128)(2,1)S(1)} %shard_map.69.refs_0_), channel_id=1, source_target_pairs={{0,1},{1,2},{2,3},{3,0},{4,5},{5,6},{6,7},{7,4},{8,9},{9,10},{10,1... | collective-permute-start | bytes 196616 | tf_op jit(solution)/shard_map/ppermute | solution.py:580
  30.8 2.6 %collective-permute-start.4 = (bf16[128,256]{1,0:T(8,128)(2,1)S(1)}, bf16[128,256]{1,0:T(8,128)(2,1)S(1)}, u32[]{:S(2)}, u32[]{:S(2)}) collective-permute-start(bf16[128,256]{1,0:T(8,128)(2,1)S(1)} %shard_map.69.refs_0_), channel_id=1, source_target_pairs={{0,2},{1,3},{2,0},{3,1},{4,6},{5,7},{6,4},{7,5},{8,10},{9,11},{10,... | collective-permute-start | bytes 196616 | tf_op jit(solution)/shard_map/ppermute | solution.py:580
  33.4 1.1 %collective-permute-start.5 = (bf16[128,256]{1,0:T(8,128)(2,1)S(1)}, bf16[128,256]{1,0:T(8,128)(2,1)S(1)}, u32[]{:S(2)}, u32[]{:S(2)}) collective-permute-start(bf16[128,256]{1,0:T(8,128)(2,1)S(1)} %shard_map.69.refs_0_), channel_id=1, source_target_pairs={{0,3},{1,0},{2,1},{3,2},{4,7},{5,4},{6,5},{7,6},{8,11},{9,8},{10,9... | collective-permute-start | bytes 196616 | tf_op jit(solution)/shard_map/ppermute | solution.py:580
  34.5 0.0 collective-permute-done.3.refs_1_
  34.5 1.3 %collective-permute-done.4.refs_2_ = bf16[128,256]{1,0:T(8,128)(2,1)S(1)} collective-permute-done((bf16[128,256]{1,0:T(8,128)(2,1)S(1)}, bf16[128,256]{1,0:T(8,128)(2,1)S(1)}, u32[]{:S(2)}, u32[]{:S(2)}) %collective-permute-start.4) | collective-permute-done | bytes 65568 | tf_op jit(solution)/shard_map/ppermute | solution.py:580
  35.7 1.1 %collective-permute-done.5.refs_3_ = bf16[128,256]{1,0:T(8,128)(2,1)S(1)} collective-permute-done((bf16[128,256]{1,0:T(8,128)(2,1)S(1)}, bf16[128,256]{1,0:T(8,128)(2,1)S(1)}, u32[]{:S(2)}, u32[]{:S(2)}) %collective-permute-start.5) | collective-permute-done | bytes 65568 | tf_op jit(solution)/shard_map/ppermute | solution.py:580
  36.8 0.2 shard_map.70.refs_0_
  37.0 1.7 %collective-permute-start.6 = (bf16[360,256]{1,0:T(8,128)(2,1)S(1)}, bf16[360,256]{1,0:T(8,128)(2,1)S(1)}, u32[]{:S(2)}, u32[]{:S(2)}) collective-permute-start(bf16[360,256]{1,0:T(8,128)(2,1)S(1)} %shard_map.70.refs_0_), channel_id=1, source_target_pairs={{0,4},{1,5},{2,6},{3,7},{4,8},{5,9},{6,10},{7,11},{8,12},{9,13},{1... | collective-permute-start | bytes 552968 | tf_op jit(solution)/shard_map/ppermute | solution.py:580
  38.7 3.3 %collective-permute-start.7 = (bf16[360,256]{1,0:T(8,128)(2,1)S(1)}, bf16[360,256]{1,0:T(8,128)(2,1)S(1)}, u32[]{:S(2)}, u32[]{:S(2)}) collective-permute-start(bf16[360,256]{1,0:T(8,128)(2,1)S(1)} %shard_map.70.refs_0_), channel_id=1, source_target_pairs={{0,8},{1,9},{2,10},{3,11},{4,12},{5,13},{6,14},{7,15},{8,0},{9,1},... | collective-permute-start | bytes 552968 | tf_op jit(solution)/shard_map/ppermute | solution.py:580
  42.0 0.7 collective-permute-start.8
  42.7 1.0 %collective-permute-done.6.refs_1_ = bf16[360,256]{1,0:T(8,128)(2,1)S(1)} collective-permute-done((bf16[360,256]{1,0:T(8,128)(2,1)S(1)}, bf16[360,256]{1,0:T(8,128)(2,1)S(1)}, u32[]{:S(2)}, u32[]{:S(2)}) %collective-permute-start.6) | collective-permute-done | bytes 184352 | tf_op jit(solution)/shard_map/ppermute | solution.py:580
  43.7 3.2 %collective-permute-done.7.refs_2_ = bf16[360,256]{1,0:T(8,128)(2,1)S(1)} collective-permute-done((bf16[360,256]{1,0:T(8,128)(2,1)S(1)}, bf16[360,256]{1,0:T(8,128)(2,1)S(1)}, u32[]{:S(2)}, u32[]{:S(2)}) %collective-permute-start.7) | collective-permute-done | bytes 184352 | tf_op jit(solution)/shard_map/ppermute | solution.py:580
  47.0 0.0 collective-permute-done.8.refs_3_
  47.0 1.5 %shard_map.71 = (f32[128,128]{1,0:T(8,128)S(1)}, f32[64,128]{1,0:T(8,128)S(1)}, f32[28,72,128]{2,1,0:T(8,128)S(1)}, f32[28,72,128]{2,1,0:T(8,128)S(1)}, f32[224,128]{1,0:T(8,128)S(1)}) custom-call(bf16[360,256]{1,0:T(8,128)(2,1)S(1)} %shard_map.70.refs_0_, bf16[360,256]{1,0:T(8,128)(2,1)S(1)} %collective-permute-done.6.refs_1_, ...), custom_call_target="tpu_custom_call" | custom-call | tf_op jit(solution)/shard_map/pallas_call | solution.py:601
  48.5 5.0 %collective-permute-start.10 = (f32[128,128]{1,0:T(8,128)S(1)}, f32[128,128]{1,0:T(8,128)S(1)}, u32[]{:S(2)}, u32[]{:S(2)}) collective-permute-start(f32[128,128]{1,0:T(8,128)S(1)} %get-tuple-element.27.refs_3_), channel_id=1, source_target_pairs={{0,112},{16,0},{32,16},{48,32},{64,48},{80,64},{96,80},{112,96},{1... | collective-permute-start | bytes 196616 | tf_op jit(solution)/shard_map/ppermute | solution.py:585
  53.5 1.3 %collective-permute-start.9 = (f32[128,128]{1,0:T(8,128)S(1)}, f32[128,128]{1,0:T(8,128)S(1)}, u32[]{:S(2)}, u32[]{:S(2)}) collective-permute-start(f32[128,128]{1,0:T(8,128)S(1)} %get-tuple-element.27.refs_3_), channel_id=1, source_target_pairs={{0,16},{16,32},{32,48},{48,64},{64,80},{80,96},{96,112},{112,0},{1... | collective-permute-start | bytes 196616 | tf_op jit(solution)/shard_map/ppermute | solution.py:585
  54.8 0.9 %collective-permute-start.11 = (f32[64,128]{1,0:T(8,128)S(1)}, f32[64,128]{1,0:T(8,128)S(1)}, u32[]{:S(2)}, u32[]{:S(2)}) collective-permute-start(f32[64,128]{1,0:T(8,128)S(1)} %get-tuple-element.28), channel_id=1, source_target_pairs={{0,32},{16,48},{32,64},{48,80},{64,96},{80,112},{96,0},{112,16},{1... | collective-permute-start | bytes 98312 | tf_op jit(solution)/shard_map/ppermute | solution.py:585
  55.6 1.8 %collective-permute-start.12 = (f32[64,128]{1,0:T(8,128)S(1)}, f32[64,128]{1,0:T(8,128)S(1)}, u32[]{:S(2)}, u32[]{:S(2)}) collective-permute-start(f32[64,128]{1,0:T(8,128)S(1)} %get-tuple-element.28), channel_id=1, source_target_pairs={{0,96},{16,112},{32,0},{48,16},{64,32},{80,48},{96,64},{112,80},{1... | collective-permute-start | bytes 98312 | tf_op jit(solution)/shard_map/ppermute | solution.py:585
  57.4 1.4 %collective-permute-done.11.refs_6_ = f32[64,128]{1,0:T(8,128)S(1)} collective-permute-done((f32[64,128]{1,0:T(8,128)S(1)}, f32[64,128]{1,0:T(8,128)S(1)}, u32[]{:S(2)}, u32[]{:S(2)}) %collective-permute-start.11) | collective-permute-done | bytes 32800 | tf_op jit(solution)/shard_map/ppermute | solution.py:585
  58.8 0.0 collective-permute-done.12.refs_7_
  58.8 0.0 collective-permute-done.10.refs_5_
  58.8 0.0 collective-permute-done.9.refs_4_
  58.8 1.5 %shard_map.72.refs_0_.refs_3_ = f32[128,128]{1,0:T(8,128)S(1)} custom-call(f32[28,72,128]{2,1,0:T(8,128)S(1)} %get-tuple-element.24.refs_0_, f32[28,72,128]{2,1,0:T(8,128)S(1)} %get-tuple-element.25.refs_1_, f32[224,128]{1,0:T(8,128)S(1)} %get-tuple-element.26.refs_2_, f32[128,128]{1,0:T(8,128)S(1)} %get-tuple-element.27.refs_3_, ...), custom_call_target="tpu_custom_call" | custom-call | tf_op jit(solution)/shard_map/pallas_call | solution.py:601
  60.3 0.8 %collective-permute-start.13 = (f32[128,128]{1,0:T(8,128)S(1)}, f32[128,128]{1,0:T(8,128)S(1)}, u32[]{:S(2)}, u32[]{:S(2)}) collective-permute-start(f32[128,128]{1,0:T(8,128)S(1)} %shard_map.72.refs_0_.refs_3_), channel_id=1, source_target_pairs={{0,16},{16,0},{32,48},{48,32},{64,80},{80,64},{96,112},{112,96},{1... | collective-permute-start | bytes 196616 | tf_op jit(solution)/shard_map/ppermute | solution.py:649
  61.1 0.9 %collective-permute-done.13.refs_1_.refs_4_ = f32[128,128]{1,0:T(8,128)S(1)} collective-permute-done((f32[128,128]{1,0:T(8,128)S(1)}, f32[128,128]{1,0:T(8,128)S(1)}, u32[]{:S(2)}, u32[]{:S(2)}) %collective-permute-start.13) | collective-permute-done | bytes 65568 | tf_op jit(solution)/shard_map/ppermute | solution.py:649
  62.1 2.9 %collective-permute-start.16 = (f32[128,128]{1,0:T(8,128)S(1)}, f32[128,128]{1,0:T(8,128)S(1)}, u32[]{:S(2)}, u32[]{:S(2)}) collective-permute-start(f32[128,128]{1,0:T(8,128)S(1)} %get-tuple-element.30), channel_id=1, source_target_pairs={{0,96},{16,112},{32,0},{48,16},{64,32},{80,48},{96,64},{112,80},{1... | collective-permute-start | bytes 196616 | tf_op jit(solution)/shard_map/ppermute | solution.py:585
  65.0 0.0 collective-permute-start.14
  65.0 1.3 %collective-permute-start.15 = (f32[64,128]{1,0:T(8,128)S(1)}, f32[64,128]{1,0:T(8,128)S(1)}, u32[]{:S(2)}, u32[]{:S(2)}) collective-permute-start(f32[64,128]{1,0:T(8,128)S(1)} %get-tuple-element.29), channel_id=1, source_target_pairs={{0,64},{16,80},{32,96},{48,112},{64,0},{80,16},{96,32},{112,48},{1... | collective-permute-start | bytes 98312 | tf_op jit(solution)/shard_map/ppermute | solution.py:585
  66.3 2.7 %collective-permute-done.14.refs_5_ = f32[64,128]{1,0:T(8,128)S(1)} collective-permute-done((f32[64,128]{1,0:T(8,128)S(1)}, f32[64,128]{1,0:T(8,128)S(1)}, u32[]{:S(2)}, u32[]{:S(2)}) %collective-permute-start.14) | collective-permute-done | bytes 32800 | tf_op jit(solution)/shard_map/ppermute | solution.py:585
  69.0 0.3 collective-permute-done.15.refs_6_
  69.3 0.0 collective-permute-done.16.refs_7_
  69.3 0.0 copy-done.4
  69.3 3.9 %shard_map.74 = (bf16[256,4096]{1,0:T(8,128)(2,1)}, f32[64,128]{1,0:T(8,128)}) custom-call(bf16[256,4096]{1,0:T(8,128)(2,1)S(1)} %bitcast.10, f32[256,4096]{1,0:T(8,128)S(1)} %get-tuple-element.18.refs_1_, f32[256,4096]{1,0:T(8,128)S(1)} %get-tuple-element.19.refs_2_, f32[128,128]{1,0:T(8,128)S(1)} %shard_map.72.refs_0_.refs_3_, ...), custom_call_target="tpu_custom_call" | custom-call | tf_op jit(solution)/shard_map/pallas_call | solution.py:601
  (3 shorter events, 0.0 us)
Async XLA Ops:
  0.6 25.9 %collective-permute-start.2 = (bf16[256,4096]{1,0:T(8,128)(2,1)}, bf16[256,4096]{1,0:T(8,128)(2,1)S(1)}, u32[]{:S(2)}, u32[]{:S(2)}) collective-permute-start(bf16[256,4096]{1,0:T(8,128)(2,1)} %bitcast.7), channel_id=1, source_target_pairs={{0,16},{16,32},{32,48},{48,64},{64,80},{80,96},{96,112},{112,0},{1... | collective-permute-start | bytes 6291464 | tf_op jit(solution)/shard_map/ppermute | solution.py:585
  4.1 7.4 %collective-permute-start = (bf16[1,4096]{1,0:T(2,128)(2,1)S(1)}, bf16[1,4096]{1,0:T(2,128)(2,1)S(1)}, u32[]{:S(2)}, u32[]{:S(2)}) collective-permute-start(bf16[1,4096]{1,0:T(2,128)(2,1)S(1)} %get-tuple-element.35), channel_id=1, source_target_pairs={{0,1},{1,2},{2,3},{3,4},{4,5},{5,6},{6,7},{7,8},{8,9},{9,10},{10,1... | collective-permute-start | bytes 24584 | tf_op jit(solution)/shard_map/ppermute | solution.py:585
  5.5 6.0 %collective-permute-start.1 = (bf16[1,4096]{1,0:T(2,128)(2,1)S(1)}, bf16[1,4096]{1,0:T(2,128)(2,1)S(1)}, u32[]{:S(2)}, u32[]{:S(2)}) collective-permute-start(bf16[1,4096]{1,0:T(2,128)(2,1)S(1)} %get-tuple-element.34), channel_id=1, source_target_pairs={{0,15},{1,0},{2,1},{3,2},{4,3},{5,4},{6,5},{7,6},{8,7},{9,8},{10,9... | collective-permute-start | bytes 24584 | tf_op jit(solution)/shard_map/ppermute | solution.py:585
  11.5 1.6 %copy-start = (bf16[1,256,4096]{2,1,0:T(8,128)(2,1)S(1)}, bf16[1,256,4096]{2,1,0:T(8,128)(2,1)}, u32[]{:S(2)}) copy-start(bf16[1,256,4096]{2,1,0:T(8,128)(2,1)} %param.5) | copy-start | bytes 6291460
  13.1 1.4 %copy-start.2 = (bf16[3200,256]{1,0:T(8,128)(2,1)S(1)}, bf16[3200,256]{1,0:T(8,128)(2,1)}, u32[]{:S(2)}) copy-start(bf16[3200,256]{1,0:T(8,128)(2,1)} %constant.25.clone.refs_3_) | copy-start | bytes 4915204
  14.6 1.6 %copy-start.3 = (bf16[256,4096]{1,0:T(8,128)(2,1)S(1)}, bf16[256,4096]{1,0:T(8,128)(2,1)}, u32[]{:S(2)}) copy-start(bf16[256,4096]{1,0:T(8,128)(2,1)} %refs_5_.1) | copy-start | bytes 6291460
  16.2 0.7 copy-start.5
  16.9 9.7 %copy-start.1 = (bf16[1,256,4096]{2,1,0:T(8,128)(2,1)S(1)}, bf16[1,256,4096]{2,1,0:T(8,128)(2,1)}, u32[]{:S(2)}) copy-start(bf16[1,256,4096]{2,1,0:T(8,128)(2,1)} %param.5) | copy-start | bytes 6291460
  29.5 39.9 %copy-start.4 = (f32[256,8]{1,0:T(8,128)S(1)}, f32[256,8]{1,0:T(8,128)}, u32[]{:S(2)}) copy-start(f32[256,8]{1,0:T(8,128)} %constant.27.clone.refs_8_) | copy-start | bytes 24580
  29.5 5.0 %collective-permute-start.3 = (bf16[128,256]{1,0:T(8,128)(2,1)S(1)}, bf16[128,256]{1,0:T(8,128)(2,1)S(1)}, u32[]{:S(2)}, u32[]{:S(2)}) collective-permute-start(bf16[128,256]{1,0:T(8,128)(2,1)S(1)} %shard_map.69.refs_0_), channel_id=1, source_target_pairs={{0,1},{1,2},{2,3},{3,0},{4,5},{5,6},{6,7},{7,4},{8,9},{9,10},{10,1... | collective-permute-start | bytes 196616 | tf_op jit(solution)/shard_map/ppermute | solution.py:580
  30.8 5.0 %collective-permute-start.4 = (bf16[128,256]{1,0:T(8,128)(2,1)S(1)}, bf16[128,256]{1,0:T(8,128)(2,1)S(1)}, u32[]{:S(2)}, u32[]{:S(2)}) collective-permute-start(bf16[128,256]{1,0:T(8,128)(2,1)S(1)} %shard_map.69.refs_0_), channel_id=1, source_target_pairs={{0,2},{1,3},{2,0},{3,1},{4,6},{5,7},{6,4},{7,5},{8,10},{9,11},{10,... | collective-permute-start | bytes 196616 | tf_op jit(solution)/shard_map/ppermute | solution.py:580
  33.4 3.4 %collective-permute-start.5 = (bf16[128,256]{1,0:T(8,128)(2,1)S(1)}, bf16[128,256]{1,0:T(8,128)(2,1)S(1)}, u32[]{:S(2)}, u32[]{:S(2)}) collective-permute-start(bf16[128,256]{1,0:T(8,128)(2,1)S(1)} %shard_map.69.refs_0_), channel_id=1, source_target_pairs={{0,3},{1,0},{2,1},{3,2},{4,7},{5,4},{6,5},{7,6},{8,11},{9,8},{10,9... | collective-permute-start | bytes 196616 | tf_op jit(solution)/shard_map/ppermute | solution.py:580
  37.0 6.8 %collective-permute-start.6 = (bf16[360,256]{1,0:T(8,128)(2,1)S(1)}, bf16[360,256]{1,0:T(8,128)(2,1)S(1)}, u32[]{:S(2)}, u32[]{:S(2)}) collective-permute-start(bf16[360,256]{1,0:T(8,128)(2,1)S(1)} %shard_map.70.refs_0_), channel_id=1, source_target_pairs={{0,4},{1,5},{2,6},{3,7},{4,8},{5,9},{6,10},{7,11},{8,12},{9,13},{1... | collective-permute-start | bytes 552968 | tf_op jit(solution)/shard_map/ppermute | solution.py:580
  38.7 8.3 %collective-permute-start.7 = (bf16[360,256]{1,0:T(8,128)(2,1)S(1)}, bf16[360,256]{1,0:T(8,128)(2,1)S(1)}, u32[]{:S(2)}, u32[]{:S(2)}) collective-permute-start(bf16[360,256]{1,0:T(8,128)(2,1)S(1)} %shard_map.70.refs_0_), channel_id=1, source_target_pairs={{0,8},{1,9},{2,10},{3,11},{4,12},{5,13},{6,14},{7,15},{8,0},{9,1},... | collective-permute-start | bytes 552968 | tf_op jit(solution)/shard_map/ppermute | solution.py:580
  42.0 5.0 %collective-permute-start.8 = (bf16[360,256]{1,0:T(8,128)(2,1)S(1)}, bf16[360,256]{1,0:T(8,128)(2,1)S(1)}, u32[]{:S(2)}, u32[]{:S(2)}) collective-permute-start(bf16[360,256]{1,0:T(8,128)(2,1)S(1)} %shard_map.70.refs_0_), channel_id=1, source_target_pairs={{0,12},{1,13},{2,14},{3,15},{4,0},{5,1},{6,2},{7,3},{8,4},{9,5},{1... | collective-permute-start | bytes 552968 | tf_op jit(solution)/shard_map/ppermute | solution.py:580
  48.5 10.3 %collective-permute-start.10 = (f32[128,128]{1,0:T(8,128)S(1)}, f32[128,128]{1,0:T(8,128)S(1)}, u32[]{:S(2)}, u32[]{:S(2)}) collective-permute-start(f32[128,128]{1,0:T(8,128)S(1)} %get-tuple-element.27.refs_3_), channel_id=1, source_target_pairs={{0,112},{16,0},{32,16},{48,32},{64,48},{80,64},{96,80},{112,96},{1... | collective-permute-start | bytes 196616 | tf_op jit(solution)/shard_map/ppermute | solution.py:585
  53.5 5.3 %collective-permute-start.9 = (f32[128,128]{1,0:T(8,128)S(1)}, f32[128,128]{1,0:T(8,128)S(1)}, u32[]{:S(2)}, u32[]{:S(2)}) collective-permute-start(f32[128,128]{1,0:T(8,128)S(1)} %get-tuple-element.27.refs_3_), channel_id=1, source_target_pairs={{0,16},{16,32},{32,48},{48,64},{64,80},{80,96},{96,112},{112,0},{1... | collective-permute-start | bytes 196616 | tf_op jit(solution)/shard_map/ppermute | solution.py:585
  54.8 4.0 %collective-permute-start.11 = (f32[64,128]{1,0:T(8,128)S(1)}, f32[64,128]{1,0:T(8,128)S(1)}, u32[]{:S(2)}, u32[]{:S(2)}) collective-permute-start(f32[64,128]{1,0:T(8,128)S(1)} %get-tuple-element.28), channel_id=1, source_target_pairs={{0,32},{16,48},{32,64},{48,80},{64,96},{80,112},{96,0},{112,16},{1... | collective-permute-start | bytes 98312 | tf_op jit(solution)/shard_map/ppermute | solution.py:585
  55.6 3.2 %collective-permute-start.12 = (f32[64,128]{1,0:T(8,128)S(1)}, f32[64,128]{1,0:T(8,128)S(1)}, u32[]{:S(2)}, u32[]{:S(2)}) collective-permute-start(f32[64,128]{1,0:T(8,128)S(1)} %get-tuple-element.28), channel_id=1, source_target_pairs={{0,96},{16,112},{32,0},{48,16},{64,32},{80,48},{96,64},{112,80},{1... | collective-permute-start | bytes 98312 | tf_op jit(solution)/shard_map/ppermute | solution.py:585
  60.3 1.7 %collective-permute-start.13 = (f32[128,128]{1,0:T(8,128)S(1)}, f32[128,128]{1,0:T(8,128)S(1)}, u32[]{:S(2)}, u32[]{:S(2)}) collective-permute-start(f32[128,128]{1,0:T(8,128)S(1)} %shard_map.72.refs_0_.refs_3_), channel_id=1, source_target_pairs={{0,16},{16,0},{32,48},{48,32},{64,80},{80,64},{96,112},{112,96},{1... | collective-permute-start | bytes 196616 | tf_op jit(solution)/shard_map/ppermute | solution.py:649
  62.1 7.3 %collective-permute-start.16 = (f32[128,128]{1,0:T(8,128)S(1)}, f32[128,128]{1,0:T(8,128)S(1)}, u32[]{:S(2)}, u32[]{:S(2)}) collective-permute-start(f32[128,128]{1,0:T(8,128)S(1)} %get-tuple-element.30), channel_id=1, source_target_pairs={{0,96},{16,112},{32,0},{48,16},{64,32},{80,48},{96,64},{112,80},{1... | collective-permute-start | bytes 196616 | tf_op jit(solution)/shard_map/ppermute | solution.py:585
  65.0 4.0 %collective-permute-start.14 = (f32[64,128]{1,0:T(8,128)S(1)}, f32[64,128]{1,0:T(8,128)S(1)}, u32[]{:S(2)}, u32[]{:S(2)}) collective-permute-start(f32[64,128]{1,0:T(8,128)S(1)} %get-tuple-element.29), channel_id=1, source_target_pairs={{0,32},{16,48},{32,64},{48,80},{64,96},{80,112},{96,0},{112,16},{1... | collective-permute-start | bytes 98312 | tf_op jit(solution)/shard_map/ppermute | solution.py:585
  65.0 4.3 %collective-permute-start.15 = (f32[64,128]{1,0:T(8,128)S(1)}, f32[64,128]{1,0:T(8,128)S(1)}, u32[]{:S(2)}, u32[]{:S(2)}) collective-permute-start(f32[64,128]{1,0:T(8,128)S(1)} %get-tuple-element.29), channel_id=1, source_target_pairs={{0,64},{16,80},{32,96},{48,112},{64,0},{80,16},{96,32},{112,48},{1... | collective-permute-start | bytes 98312 | tf_op jit(solution)/shard_map/ppermute | solution.py:585
